TPU v7x, 256 devices: a whole 4x4x8 slice. The times are simulated.
256 devices in a mesh: rep: 1, r: 32 (over y, z), s: 8 (over x, core).
Axes of the slice: x: 4, y: 4, z: 8, core: 2. Of those that a mesh axis runs over, the one named last changes fastest.
Arguments:
- x: bfloat16 [256, 2048, 896], P(('rep', 'r', 's'))
- dy: bfloat16 [256, 2048, 896], P(('rep', 'r', 's'))
- w_gate: bfloat16 [2, 896, 2560], P(None, 's')
- w_up: bfloat16 [2, 896, 2560], P(None, 's')
- w_down: bfloat16 [2, 2560, 896], P(None, 's')
Outputs:
- output 1: bfloat16 [256, 2048, 896], P(('rep', 'r', 's'))
- output 2: bfloat16 [2, 896, 2560], P('rep', 's')
- output 3: bfloat16 [2, 896, 2560], P('rep', 's')
- output 4: bfloat16 [2, 2560, 896], P('rep', 's')
All inputs are finite; a program needn't handle non-finite values.
Results may differ from a plain program's by a relative error of at most 0.018.
Values are sent between devices in bfloat16 or wider.
A program may use at most 768 MiB of HBM per device.

v0:
```python
import jax
import jax.numpy as jnp
from jax import lax
from jax.sharding import PartitionSpec as P

NAMES = ("w_gate", "w_up", "w_down")


def matmul(a, w):
    return jnp.dot(a, w, preferred_element_type=jnp.float32).astype(jnp.bfloat16)


def normed(h):
    wide = h.astype(jnp.float32)
    scale = lax.rsqrt(jnp.mean(wide**2, -1, keepdims=True) + 1e-6)
    return (wide * scale).astype(jnp.bfloat16)


def layer(h, w):
    a = normed(h)
    gate = jnp.dot(a, w["w_gate"], preferred_element_type=jnp.float32)
    up = jnp.dot(a, w["w_up"], preferred_element_type=jnp.float32)
    return h + matmul((jax.nn.silu(gate) * up).astype(jnp.bfloat16), w["w_down"])


def solution(mesh):
    def fetched(weights, number):
        return {name: lax.all_gather(w[number], "s", axis=0, tiled=True) for name, w in zip(NAMES, weights, strict=True)}

    def summed(term):
        return lax.psum(lax.psum_scatter(term, "s", scatter_dimension=0, tiled=True), "r")

    def step(x, dy, *weights):
        layers = weights[0].shape[0]
        h, inputs = x[0], []
        for number in range(layers):
            inputs.append(h)
            h = layer(h, fetched(weights, number))
        by_h, mine = dy[0], [None] * layers
        for number in reversed(range(layers)):
            _, back = jax.vjp(lambda w, h: layer(h, w), fetched(weights, number), inputs[number])
            by_w, by_h = back(by_h)
            mine[number] = [summed(by_w[name]) for name in NAMES]
        return (by_h[None], *(jnp.stack([mine[number][i] for number in range(layers)]) for i in range(3)))

    states, cut = P(("rep", "r", "s"), None, None), P(None, "s", None)
    return jax.shard_map(
        step,
        mesh=mesh,
        in_specs=(states, states) + (cut,) * 3,
        out_specs=(states,) + (P("rep", "s", None),) * 3,
        check_vma=False,
    )
```

profile of v0, /device:TPU:1, one launch (start us, length us, event | category | flops | bytes accessed | tf_op | source)
XLA Modules:
  0.0 754.2 jit_solution(15902680157078591514)
XLA Ops:
  16.2 6.1 copy.10
  25.6 6.2 copy.9
  31.8 18.7 %all-gather.13.cloned.1.call-done = bf16[1,896,2560]{2,1,0:T(8,128)(2,1)} async-done(((bf16[1,112,2560]{2,1,0:T(8,128)(2,1)}), bf16[1,896,2560]{2,1,0:T(8,128)(2,1)}) %all-gather.13.cloned.1.call-update) | async-done | bytes 4587536 | tf_op jit(solution)/shard_map/all_gather | solution.py:28
  50.5 18.1 %fusion.40 = f32[2048,2560]{1,0:T(8,128)} fusion(bf16[1,896,2560]{2,1,0:T(8,128)(2,1)} %all-gather.13.cloned.1.call-done, bf16[1,2048,896]{1,2,0:T(8,128)(2,1)} %copy.10, f32[2048]{0:T(1024)S(1)} %fusion.61), kind=kOutput, calls=%fused_computation.65 | convolution fusion | flops 9400745984 | bytes 29237248 | tf_op jit(solution)/shard_map/dot_general | solution.py:21
  68.6 19.8 %all-gather.15.cloned.1.call-done = bf16[1,896,2560]{2,1,0:T(8,128)(2,1)} async-done(((bf16[1,112,2560]{2,1,0:T(8,128)(2,1)}), bf16[1,896,2560]{2,1,0:T(8,128)(2,1)}) %all-gather.15.cloned.1.call-update) | async-done | bytes 4587536 | tf_op jit(solution)/shard_map/all_gather | solution.py:28
  88.4 28.3 %multiply_convert_fusion.1 = (bf16[2048,2560]{1,0:T(8,128)(2,1)}, f32[2048,2560]{1,0:T(8,128)}) fusion(f32[2048,2560]{1,0:T(8,128)} %fusion.40, bf16[1,896,2560]{2,1,0:T(8,128)(2,1)} %all-gather.15.cloned.1.call-done, bf16[1,2048,896]{1,2,0:T(8,128)(2,1)} %copy.10, f32[2048]{0:T(1024)S(1)} %fusion.61), kind=kOutput, calls=%fused_computation.13 | convolution fusion | flops 9432203264 | bytes 60694528 | tf_op jit(solution)/shard_map/dot_general | solution.py:22
  116.6 9.6 %all-gather.17.cloned.1.call-done = bf16[1,2560,896]{2,1,0:T(8,128)(2,1)} async-done(((bf16[1,320,896]{2,1,0:T(8,128)(2,1)}), bf16[1,2560,896]{2,1,0:T(8,128)(2,1)}) %all-gather.17.cloned.1.call-update) | async-done | bytes 4587536 | tf_op jit(solution)/shard_map/all_gather | solution.py:28
  126.2 16.2 %fusion.18 = (f32[2048]{0:T(1024)S(1)}, bf16[2048,896]{0,1:T(8,128)(2,1)}) fusion(bf16[2048,2560]{1,0:T(8,128)(2,1)} %get-tuple-element.20, bf16[1,2560,896]{2,1,0:T(8,128)(2,1)} %all-gather.17.cloned.1.call-done, bf16[1,2048,896]{1,2,0:T(8,128)(2,1)} %copy.10), kind=kOutput, calls=%fused_computation.40 | convolution fusion | flops 9404413952 | bytes 22421504 | tf_op jit(solution)/shard_map/dot_general | solution.py:10
  142.5 22.1 %all-gather.23.cloned.1.call-done = bf16[1,896,2560]{2,1,0:T(8,128)(2,1)} async-done(((bf16[1,112,2560]{2,1,0:T(8,128)(2,1)}), bf16[1,896,2560]{2,1,0:T(8,128)(2,1)}) %all-gather.23.cloned.1.call-update) | async-done | bytes 4587536 | tf_op jit(solution)/shard_map/all_gather | solution.py:28
  164.5 18.2 %fusion.24 = f32[2048,2560]{1,0:T(8,128)} fusion(bf16[1,896,2560]{2,1,0:T(8,128)(2,1)} %all-gather.23.cloned.1.call-done, bf16[2048,896]{0,1:T(8,128)(2,1)} %get-tuple-element.23, f32[2048]{0:T(1024)S(1)} %fusion.62), kind=kOutput, calls=%fused_computation.49 | convolution fusion | flops 9400745984 | bytes 29237248 | tf_op jit(solution)/shard_map/jvp()/dot_general | solution.py:22
  182.7 19.5 %all-gather.21.cloned.1.call-done = bf16[1,2560,896]{2,1,0:T(8,128)(2,1)} async-done(((bf16[1,320,896]{2,1,0:T(8,128)(2,1)}), bf16[1,2560,896]{2,1,0:T(8,128)(2,1)}) %all-gather.21.cloned.1.call-update) | async-done | bytes 4587536 | tf_op jit(solution)/shard_map/all_gather | solution.py:28
  202.3 16.4 %convolution_convert_fusion.1 = bf16[2048,2560]{1,0:T(8,128)(2,1)} fusion(bf16[1,2560,896]{2,1,0:T(8,128)(2,1)} %all-gather.21.cloned.1.call-done, bf16[1,2048,896]{2,1,0:T(8,128)(2,1)} %param.6), kind=kOutput, calls=%fused_computation.29 | convolution fusion | flops 9400483840 | bytes 18743296 | tf_op jit(solution)/shard_map/transpose(jvp())/dot_general | solution.py:10
  218.7 21.9 %all-gather.19.cloned.1.call-done = bf16[1,896,2560]{2,1,0:T(8,128)(2,1)} async-done(((bf16[1,112,2560]{2,1,0:T(8,128)(2,1)}), bf16[1,896,2560]{2,1,0:T(8,128)(2,1)}) %all-gather.19.cloned.1.call-update) | async-done | bytes 4587536 | tf_op jit(solution)/shard_map/all_gather | solution.py:28
  240.6 31.9 %fusion.1 = (bf16[2048,2560]{1,0:T(8,128)(2,1)}, f32[2048,2560]{1,0:T(8,128)}) fusion(f32[2048,2560]{1,0:T(8,128)} %fusion.24, bf16[2048,2560]{1,0:T(8,128)(2,1)} %convolution_convert_fusion.1, bf16[1,896,2560]{2,1,0:T(8,128)(2,1)} %all-gather.19.cloned.1.call-done, bf16[2048,896]{0,1:T(8,128)(2,1)} %get-tuple-element.23, f32[2048]{0:T(1024)S(1)} %fusion.62), kind=kOutput, calls=%fused_computation.7 | convolution fusion | flops 9463660544 | bytes 71180288 | tf_op jit(solution)/shard_map/jvp()/dot_general | solution.py:21
  272.5 18.4 %fusion.7 = bf16[2048,896]{0,1:T(8,128)(2,1)} fusion(bf16[2048,2560]{1,0:T(8,128)(2,1)} %convolution_convert_fusion.1, bf16[1,896,2560]{2,1,0:T(8,128)(2,1)} %all-gather.23.cloned.1.call-done, f32[2048,2560]{1,0:T(8,128)} %get-tuple-element.25), kind=kOutput, calls=%fused_computation.17 | convolution fusion | flops 9426698240 | bytes 39714816 | tf_op jit(solution)/shard_map/transpose(jvp())/dot_general | solution.py:22
  290.9 15.4 %fusion.20 = (f32[2048]{0:T(1024)S(1)}, bf16[2048,896]{0,1:T(8,128)(2,1)S(1)}) fusion(bf16[2048,896]{0,1:T(8,128)(2,1)S(1)} %copy-done.4, bf16[2048,896]{0,1:T(8,128)(2,1)} %fusion.7, bf16[2048,2560]{1,0:T(8,128)(2,1)} %get-tuple-element.24, bf16[1,896,2560]{2,1,0:T(8,128)(2,1)} %all-gather.19.cloned.1.call-done), kind=kOutput, calls=%fused_computation.42 | convolution fusion | flops 9404413952 | bytes 26091520 | tf_op jit(solution)/shard_map/transpose(jvp())/dot_general | solution.py:21
  310.8 15.3 %convolution_convert_fusion.2 = bf16[2560,896]{1,0:T(8,128)(2,1)} fusion(bf16[2048,2560]{1,0:T(8,128)(2,1)} %get-tuple-element.20, bf16[2048,896]{0,1:T(8,128)(2,1)S(1)} %fusion.44), kind=kOutput, calls=%fused_computation.46 | convolution fusion | flops 9397534720 | bytes 18743296 | tf_op jit(solution)/shard_map/transpose(jvp())/dot_general | solution.py:10
  326.1 21.6 %fusion.23 = bf16[2560,896]{1,0:T(8,128)(2,1)} fusion(f32[2048,2560]{1,0:T(8,128)} %fusion.24, bf16[1,2048,896]{2,1,0:T(8,128)(2,1)} %param.6, f32[2048,2560]{1,0:T(8,128)} %get-tuple-element.25), kind=kOutput, calls=%fused_computation.45 | convolution fusion | flops 9428992000 | bytes 50200576 | tf_op jit(solution)/shard_map/transpose(jvp())/dot_general | solution.py:10
  347.8 30.7 %fusion.3 = (bf16[2048,2560]{1,0:T(8,128)(2,1)}, bf16[2048,2560]{1,0:T(8,128)(2,1)}) fusion(f32[2048,2560]{1,0:T(8,128)} %fusion.40, f32[2048,2560]{1,0:T(8,128)} %get-tuple-element.21, bf16[2048,896]{0,1:T(8,128)(2,1)} %copy-done.2, bf16[1,2560,896]{2,1,0:T(8,128)(2,1)} %all-gather.17.cloned.1.call-done), kind=kOutput, calls=%fused_computation.9 | convolution fusion | flops 9463398400 | bytes 71172096 | tf_op jit(solution)/shard_map/transpose(jvp())/dot_general | solution.py:10
  378.5 18.6 %fusion.21 = bf16[896,2560]{1,0:T(8,128)(2,1)} fusion(bf16[2048,2560]{1,0:T(8,128)(2,1)} %get-tuple-element.29, bf16[1,2048,896]{1,2,0:T(8,128)(2,1)} %copy.10, f32[2048]{0:T(1024)S(1)} %copy-done.8, f32[2048,2560]{1,0:T(8,128)} %fusion.40), kind=kOutput, calls=%fused_computation.43 | convolution fusion | flops 9434497024 | bytes 39723008 | tf_op jit(solution)/shard_map/transpose(jvp())/dot_general | solution.py:22
  397.2 18.9 %fusion.22 = bf16[896,2560]{1,0:T(8,128)(2,1)} fusion(bf16[2048,2560]{1,0:T(8,128)(2,1)} %convolution_convert_fusion.1, bf16[2048,896]{0,1:T(8,128)(2,1)} %get-tuple-element.23, f32[2048]{0:T(1024)S(1)} %copy-done.10, f32[2048,2560]{1,0:T(8,128)} %get-tuple-element.25), kind=kOutput, calls=%fused_computation.44 | convolution fusion | flops 9434497024 | bytes 39723008 | tf_op jit(solution)/shard_map/transpose(jvp())/dot_general | solution.py:22
  416.2 14.9 %convolution_convert_fusion.3 = bf16[896,2560]{1,0:T(8,128)(2,1)} fusion(bf16[2048,2560]{1,0:T(8,128)(2,1)} %get-tuple-element.24, bf16[2048,896]{0,1:T(8,128)(2,1)} %get-tuple-element.23, f32[2048]{0:T(1024)S(1)} %copy-done.10), kind=kOutput, calls=%fused_computation.47 | convolution fusion | flops 9400745984 | bytes 18751488 | tf_op jit(solution)/shard_map/transpose(jvp())/dot_general | solution.py:21
  431.2 14.9 %convolution_convert_fusion.4 = bf16[896,2560]{1,0:T(8,128)(2,1)} fusion(bf16[2048,2560]{1,0:T(8,128)(2,1)} %get-tuple-element.28, bf16[1,2048,896]{1,2,0:T(8,128)(2,1)} %copy.10, f32[2048]{0:T(1024)S(1)} %copy-done.8), kind=kOutput, calls=%fused_computation.48 | convolution fusion | flops 9400745984 | bytes 18751488 | tf_op jit(solution)/shard_map/transpose(jvp())/dot_general | solution.py:21
  446.2 4.3 reduce-scatter.11.cloned.1.call-done
  450.5 42.9 %reduce-scatter.13.cloned.1.call-done = bf16[112,2560]{1,0:T(8,128)(2,1)} async-done(((bf16[896,2560]{1,0:T(8,128)(2,1)}), bf16[112,2560]{1,0:T(8,128)(2,1)}) %reduce-scatter.13.cloned.1.call-update) | async-done | bytes 573456 | tf_op jit(solution)/shard_map/reduce_scatter | solution.py:31
  493.4 43.0 %reduce-scatter.9.cloned.1.call-done = bf16[112,2560]{1,0:T(8,128)(2,1)} async-done(((bf16[896,2560]{1,0:T(8,128)(2,1)}), bf16[112,2560]{1,0:T(8,128)(2,1)}) %reduce-scatter.9.cloned.1.call-update) | async-done | bytes 573456 | tf_op jit(solution)/shard_map/reduce_scatter | solution.py:31
  536.4 42.9 %reduce-scatter.7.cloned.1.call-done = bf16[112,2560]{1,0:T(8,128)(2,1)} async-done(((bf16[896,2560]{1,0:T(8,128)(2,1)}), bf16[112,2560]{1,0:T(8,128)(2,1)}) %reduce-scatter.7.cloned.1.call-update) | async-done | bytes 573456 | tf_op jit(solution)/shard_map/reduce_scatter | solution.py:31
  579.3 18.5 %fusion.9 = bf16[2048,896]{0,1:T(8,128)(2,1)} fusion(bf16[2048,2560]{1,0:T(8,128)(2,1)} %get-tuple-element.29, bf16[1,896,2560]{2,1,0:T(8,128)(2,1)} %all-gather.15.cloned.1.call-done, f32[2048,2560]{1,0:T(8,128)} %fusion.40), kind=kOutput, calls=%fused_computation.19 | convolution fusion | flops 9426698240 | bytes 39714816 | tf_op jit(solution)/shard_map/transpose(jvp())/dot_general | solution.py:22
  597.8 14.9 %fusion.17 = (f32[2048]{0:T(1024)S(1)}, bf16[2048,896]{0,1:T(8,128)(2,1)S(1)}) fusion(bf16[1,2048,896]{1,2,0:T(8,128)(2,1)S(1)} %copy-done, bf16[2048,896]{0,1:T(8,128)(2,1)} %fusion.9, bf16[2048,2560]{1,0:T(8,128)(2,1)} %get-tuple-element.28, bf16[1,896,2560]{2,1,0:T(8,128)(2,1)} %all-gather.13.cloned.1.call-done), kind=kOutput, calls=%fused_computation.39 | convolution fusion | flops 9404413952 | bytes 26091520 | tf_op jit(solution)/shard_map/transpose(jvp())/dot_general | solution.py:21
  612.7 4.5 fusion.43
  617.1 6.0 copy.11
  623.2 118.8 %all-reduce.3.cloned.1.call-done = (bf16[1,112,2560]{2,1,0:T(8,128)(2,1)}, bf16[1,112,2560]{2,1,0:T(8,128)(2,1)}, bf16[1,112,2560]{2,1,0:T(8,128)(2,1)}, bf16[1,...) async-done(((bf16[1,112,2560]{2,1,0:T(8,128)(2,1)}, bf16[1,112,2560]{2,1,0:T(8,128)(2,1)}, bf16[1,112,2560]{2,1,0:T(8,128)(2,1)}, ...) | async-done | bytes 3440656 | tf_op jit(solution)/shard_map/psum | solution.py:31
  (61 shorter events, 22.7 us)
Async XLA Ops:
  7.2 43.3 %all-gather.13.cloned.1.call-start = ((), (), s32[]{:S(2)}) async-start(), calls=%async_computation.12 | async-start | bytes 5160960 | tf_op jit(solution)/shard_map/all_gather | solution.py:28
  9.5 78.8 %all-gather.15.cloned.1.call-start = ((), (), s32[]{:S(2)}) async-start(), calls=%async_computation.13 | async-start | bytes 5160960 | tf_op jit(solution)/shard_map/all_gather | solution.py:28
  11.9 114.3 %all-gather.17.cloned.1.call-start = ((), (), s32[]{:S(2)}) async-start(), calls=%async_computation.14 | async-start | bytes 5160960 | tf_op jit(solution)/shard_map/all_gather | solution.py:28
  14.4 150.2 %all-gather.23.cloned.1.call-start = ((), (), s32[]{:S(2)}) async-start(), calls=%async_computation.17 | async-start | bytes 5160960 | tf_op jit(solution)/shard_map/all_gather | solution.py:28
  14.9 187.3 %all-gather.21.cloned.1.call-start = ((), (), s32[]{:S(2)}) async-start(), calls=%async_computation.16 | async-start | bytes 5160960 | tf_op jit(solution)/shard_map/all_gather | solution.py:28
  15.5 225.1 %all-gather.19.cloned.1.call-start = ((), (), s32[]{:S(2)}) async-start(), calls=%async_computation.15 | async-start | bytes 5160960 | tf_op jit(solution)/shard_map/all_gather | solution.py:28
  16.1 430.1 %reduce-scatter.15.cloned.1.call-start = ((), (), s32[]{:S(2)}) async-start(), calls=%async_computation.10 | async-start | bytes 5160960 | tf_op jit(solution)/shard_map/reduce_scatter | solution.py:31
  25.0 0.6 copy-start.5
  25.6 62.7 %copy-start.7 = (f32[2048]{0:T(1024)}, f32[2048]{0:T(1024)S(1)}, u32[]{:S(2)}) copy-start(f32[2048]{0:T(1024)S(1)} %fusion.61) | copy-start | bytes 24580
  142.5 163.9 %copy-start.9 = (f32[2048]{0:T(1024)}, f32[2048]{0:T(1024)S(1)}, u32[]{:S(2)}) copy-start(f32[2048]{0:T(1024)S(1)} %fusion.62) | copy-start | bytes 24580
  272.5 18.4 %copy-start.4 = (bf16[2048,896]{0,1:T(8,128)(2,1)S(1)}, bf16[2048,896]{0,1:T(8,128)(2,1)}, u32[]{:S(2)}) copy-start(bf16[2048,896]{0,1:T(8,128)(2,1)} %get-tuple-element.23) | copy-start | bytes 11010052
  290.9 15.4 %copy-start.1 = (bf16[1,2048,896]{1,2,0:T(8,128)(2,1)S(1)}, bf16[1,2048,896]{1,2,0:T(8,128)(2,1)}, u32[]{:S(2)}) copy-start(bf16[1,2048,896]{1,2,0:T(8,128)(2,1)} %copy.9) | copy-start | bytes 11010052
  309.0 1.8 copy-start.2
  326.1 120.1 %reduce-scatter.17.cloned.1.call-start = ((), (), s32[]{:S(2)}) async-start(), calls=%async_computation.11 | async-start | bytes 5160960 | tf_op jit(solution)/shard_map/reduce_scatter | solution.py:31
  347.8 102.7 %reduce-scatter.11.cloned.1.call-start = ((), (), s32[]{:S(2)}) async-start(), calls=%async_computation.8 | async-start | bytes 5160960 | tf_op jit(solution)/shard_map/reduce_scatter | solution.py:31
  347.8 30.7 %copy-start.8 = (f32[2048]{0:T(1024)S(1)}, f32[2048]{0:T(1024)}, u32[]{:S(2)}) copy-start(f32[2048]{0:T(1024)} %copy-done.7) | copy-start | bytes 24580
  378.5 18.7 %copy-start.10 = (f32[2048]{0:T(1024)S(1)}, f32[2048]{0:T(1024)}, u32[]{:S(2)}) copy-start(f32[2048]{0:T(1024)} %copy-done.9) | copy-start | bytes 24580
  397.2 96.2 %reduce-scatter.13.cloned.1.call-start = ((), (), s32[]{:S(2)}) async-start(), calls=%async_computation.9 | async-start | bytes 5160960 | tf_op jit(solution)/shard_map/reduce_scatter | solution.py:31
  416.2 120.2 %reduce-scatter.9.cloned.1.call-start = ((), (), s32[]{:S(2)}) async-start(), calls=%async_computation.7 | async-start | bytes 5160960 | tf_op jit(solution)/shard_map/reduce_scatter | solution.py:31
  431.1 148.1 %reduce-scatter.7.cloned.1.call-start = ((), (), s32[]{:S(2)}) async-start(), calls=%async_computation.6 | async-start | bytes 5160960 | tf_op jit(solution)/shard_map/reduce_scatter | solution.py:31
  446.1 295.9 %all-reduce.3.cloned.1.call-start = ((), (), s32[]{:S(2)}) async-start(), calls=%async_computation.18 | async-start | bytes 6881280 | tf_op jit(solution)/shard_map/psum | solution.py:31
  579.2 18.5 %copy-start = (bf16[1,2048,896]{1,2,0:T(8,128)(2,1)S(1)}, bf16[1,2048,896]{1,2,0:T(8,128)(2,1)}, u32[]{:S(2)}) copy-start(bf16[1,2048,896]{1,2,0:T(8,128)(2,1)} %copy.10) | copy-start | bytes 11010052
  597.7 14.9 %copy-start.6 = (f32[2048]{0:T(1024)S(1)}, f32[2048]{0:T(1024)}, u32[]{:S(2)}) copy-start(f32[2048]{0:T(1024)} %copy-done.5) | copy-start | bytes 24580
  597.7 14.9 %copy-start.3 = (bf16[2048,896]{0,1:T(8,128)(2,1)S(1)}, bf16[2048,896]{0,1:T(8,128)(2,1)}, u32[]{:S(2)}) copy-start(bf16[2048,896]{0,1:T(8,128)(2,1)} %copy-done.2) | copy-start | bytes 11010052
Sparse Core Ops, SparseCore 0:
  10.4 40.0 all-gather.12
  52.3 36.0 all-gather.14
  90.2 36.0 all-gather.16
  128.5 36.0 all-gather.22
  166.2 36.0 all-gather.20
  204.5 36.0 all-gather.18
  326.2 38.2 reduce-scatter.14
  367.1 40.3 reduce-scatter.16
  410.1 40.3 reduce-scatter.10
  452.9 40.3 reduce-scatter.12
  495.9 40.3 reduce-scatter.8
  538.8 40.3 reduce-scatter.6
  583.4 158.4 all-reduce.2
where the time goes:
time: 764 us; the launch traced here: 754 us
  waiting for transfers between devices  365 us (48%)
  matrix products  331 us (43%)
  local copies, waits for them, and re-layouts  27.7 us (4%)
  other arithmetic  15.5 us (2%)
  between operations  14.2 us (2%)
    reduce_scatter x6, waiting for transfers between devices, summed(): lax.psum_scatter(term, 's', scatter_dimension=0, tiled=True)  133 us
    dot_general x6, matrix products, layer(): up = jnp.dot(a, w['w_up'], preferred_element_type=jnp.float32)  121 us
    psum x1, waiting for transfers between devices, summed(): lax.psum(lax.psum_scatter(term, 's', scatter_dimension=0, tiled=True), 'r')  119 us
    all_gather x6, waiting for transfers between devices, fetched(): lax.all_gather(w[number], 's', axis=0, tiled=True)  112 us
    dot_general x6, matrix products, layer(): gate = jnp.dot(a, w['w_gate'], preferred_element_type=jnp.float32)  110 us
    dot_general x5, matrix products, matmul(): jnp.dot(a, w, preferred_element_type=jnp.float32).astype(jnp.bfloat16)  100 us
    unnamed x25, local copies, waits for them, and re-layouts  20.7 us
  transfers between devices with their start and end apart: 13, of which 11 were waited for; matrix products, arithmetic and copies ran while one was open for 37% of the time, Pallas kernels for 0%

commit v1 on v0

v1 whole, which is shorter than its diff:
```python
import functools

import jax
import jax.numpy as jnp
from jax import lax
from jax.experimental import pallas as pl
from jax.experimental.pallas import tpu as pltpu
from jax.sharding import PartitionSpec as P

f32, bf16 = jnp.float32, jnp.bfloat16
MESH = pl.DeviceIdType.MESH
LANES = 128
X, CORES, Y = 4, 2, 4
HBM, VMEM, DMA = pl.ANY, pltpu.VMEM, pltpu.SemaphoreType.DMA


def dot(a, b, dims=((1,), (0,))):
    return lax.dot_general(a, b, (dims, ((), ())), preferred_element_type=f32)


def at(start, size, multiple=16):
    return pl.ds(pl.multiple_of(start, multiple) if not isinstance(start, int) else start, size)


class Sizes:
    chunk, rows = 512, 256

    def __init__(self, mesh, tokens, d, ff):
        self.R = mesh.shape["r"]
        self.Z = self.R // Y
        self.T, self.D, self.F = tokens, d, ff
        self.NB = ff // (X * LANES)
        self.FB = X * LANES
        self.h = d // (X * CORES)
        self.TC = min(self.chunk, tokens)
        self.T3 = min(self.rows, tokens)
        self.half = X * self.h
        self.U = 3 * self.half
        per = -(-self.U // self.R)
        self.PR = -(-per // 16) * 16
        self.active = self.U // self.PR
        assert self.active * self.PR == self.U and mesh.shape["s"] == X * CORES


class Here:
    def __init__(self, z):
        s, self.r = lax.axis_index("s"), lax.axis_index("r")
        self.x, self.c = lax.div(s, CORES), lax.rem(s, CORES)
        self.y, self.z, self.Z = lax.div(self.r, z.Z), lax.rem(self.r, z.Z), z.Z
        self.R = z.R

    def partner(self):
        return {"s": self.x * CORES + 1 - self.c}

    def along_x(self, k):
        return {"s": lax.rem(self.x + k, X) * CORES + self.c}

    def along_y(self, k):
        return {"r": lax.rem(self.y + k, Y) * self.Z + self.z}

    def along_r(self, k):
        return {"r": lax.rem(self.r + k, self.R)}


def remote(src, dst, sent, got, where):
    return pltpu.make_async_remote_copy(src_ref=src, dst_ref=dst, send_sem=sent, recv_sem=got, device_id=where, device_id_type=MESH)


def start(copies):
    for copy in copies:
        copy.start()


def wait(ref, sem):
    pltpu.make_async_copy(ref, ref, sem).wait()


def meet(peers):
    barrier = pltpu.get_barrier_semaphore()
    for peer in peers:
        pl.semaphore_signal(barrier, inc=1, device_id=peer, device_id_type=MESH)
    return lambda: pl.semaphore_wait(barrier, len(peers))


class Fetch:
    def __init__(self, z, here, shards, w, sems):
        self.z, self.here, self.shards, self.w = z, here, shards, w
        (
            self.local, self.local_d, self.pair, self.pair_sent, self.a_got, self.a_sent, self.b_got, self.b_sent, self.c_got, self.c_sent,
            self.d_got, self.d_sent, self.e_got, self.e_sent,
        ) = sems

    @staticmethod
    def scratch(z):
        return [DMA((z.NB,)), DMA, DMA, DMA] + [DMA((z.NB,)) for _ in range(10)]

    def rows(self, x):
        return at(x * (CORES * self.z.h) + self.here.c * self.z.h, self.z.h)

    def own(self, j):
        z, here = self.z, self.here
        return [
            pltpu.make_async_copy(shard.at[:, pl.ds((l * z.NB + j) * LANES, LANES)], w.at[j, self.rows(here.x), pl.ds(l * LANES, LANES)], self.local.at[j])
            for shard, w in zip(self.shards[:2], self.w[:2], strict=True)
            for l in range(X)
        ]

    def own_down(self):
        z, here = self.z, self.here
        local, away = [], []
        for k in range(z.NB):
            place = here.c * z.NB + k
            slot = self.w[2].at[lax.div(place, 2), at(here.x * LANES + lax.rem(place, 2) * 64, 64), :]
            src = self.shards[2].at[pl.ds(64 * k, 64), :]
            local.append(pltpu.make_async_copy(src, slot, self.local_d))
            away.append(remote(src, slot, self.pair_sent, self.pair, here.partner()))
        return local, away

    def a(self, j):
        here = self.here
        out = []
        for k in range(1, X):
            for w in self.w[:2]:
                slot = w.at[j, self.rows(here.x), at(here.y * LANES, LANES, LANES)]
                out.append(remote(slot, slot, self.a_sent.at[j], self.a_got.at[j], here.along_x(k)))
        return out

    def d(self, j):
        here = self.here
        slot = self.w[2].at[j, at(here.x * LANES + here.c * 64, 64), :]
        return [remote(slot, slot, self.d_sent.at[j], self.d_got.at[j], here.along_x(k)) for k in range(1, X)]

    def b(self, j):
        here = self.here
        out = []
        for m in range(1, X):
            for k in range(1, Y):
                for w in self.w[:2]:
                    slot = w.at[j, self.rows(lax.rem(here.x + m, X)), at(here.y * LANES, LANES, LANES)]
                    out.append(remote(slot, slot, self.b_sent.at[j], self.b_got.at[j], here.along_y(k)))
        return out

    def c(self, j):
        here = self.here
        return [
            remote(w.at[j, self.rows(x), :], w.at[j, self.rows(x), :], self.c_sent.at[j], self.c_got.at[j], here.partner())
            for w in self.w[:2]
            for x in range(X)
        ]

    def e(self, j):
        here = self.here
        out = []
        for m in range(1, X):
            slot = self.w[2].at[j, at(lax.rem(here.x + m, X) * LANES + here.c * 64, 64), :]
            out.append(remote(slot, slot, self.e_sent.at[j], self.e_got.at[j], here.partner()))
        return out

    def bytes_own(self, j):
        return self.w[0].at[j, pl.ds(0, 2 * self.z.h), :]

    def bytes_down(self):
        return self.w[2].at[0, pl.ds(0, 64 * self.z.NB), :]

    def bytes_a(self, j):
        return self.w[0].at[j, pl.ds(0, 6 * self.z.h), pl.ds(0, LANES)]

    def bytes_b(self, j):
        return self.w[0].at[j, pl.ds(0, 6 * self.z.h), pl.ds(0, 3 * LANES)]

    def bytes_d(self, j):
        return self.w[2].at[j, pl.ds(0, 192), :]

    def begin_local(self):
        for j in range(self.z.NB):
            start(self.own(j))
        start(self.own_down()[0])

    def start_a(self, j):
        wait(self.bytes_own(j), self.local.at[j])
        start(self.a(j))

    def begin(self):
        nb = self.z.NB
        start(self.own_down()[1])
        for j in range(min(2, nb)):
            self.start_a(j)
        wait(self.bytes_down(), self.local_d)
        wait(self.bytes_down(), self.pair)
        for j in range(nb):
            if j >= 2:
                self.start_a(j)
            start(self.d(j))

    def pass_b(self, j):
        wait(self.bytes_a(j), self.a_got.at[j])
        start(self.b(j))

    def pass_c(self, j):
        wait(self.bytes_b(j), self.b_got.at[j])
        start(self.c(j))
        wait(self.bytes_d(j), self.d_got.at[j])
        start(self.e(j))

    def ready(self, j):
        wait(self.w[0].at[j], self.c_got.at[j])
        wait(self.bytes_d(j), self.e_got.at[j])

    def head(self):
        self.pass_b(0)
        if self.z.NB > 1:
            self.pass_b(1)
        self.pass_c(0)

    def serve(self, j):
        pl.when(j + 2 < self.z.NB)(lambda: self.pass_b(j + 2))
        pl.when(j + 1 < self.z.NB)(lambda: self.pass_c(j + 1))
        self.ready(j)

    def end(self):
        wait(self.bytes_down(), self.pair_sent)

        def one(j, _):
            wait(self.bytes_a(j), self.a_sent.at[j])
            wait(self.bytes_b(j), self.b_sent.at[j])
            wait(self.w[0].at[j], self.c_sent.at[j])
            wait(self.bytes_d(j), self.d_sent.at[j])
            wait(self.bytes_d(j), self.e_sent.at[j])
            return 0

        lax.fori_loop(0, self.z.NB, one, 0)


def normed(wide):
    scale = lax.rsqrt(jnp.mean(wide * wide, -1, keepdims=True) + 1e-6)
    return (wide * scale).astype(bf16), scale


def forward_kernel(z, x_in, sg, su, sd, h_out, wg_out, wu_out, wd_out, a, acc, xs, wg, wu, wd, x_sem, out_sem, h_sem, *sems):
    here = Here(z)
    fetch = Fetch(z, here, (sg, su, sd), (wg, wu, wd), sems)
    met = meet([here.partner()] + [here.along_x(k) for k in range(1, X)] + [here.along_y(k) for k in range(1, Y)])
    fetch.begin_local()
    load = pltpu.make_async_copy(x_in, xs, x_sem)
    load.start()
    met()
    fetch.begin()
    load.wait()

    def prepare(i, _):
        rows = at(i * z.T3, z.T3)
        a[rows, :] = normed(xs[rows, :].astype(f32))[0]
        acc[rows, :] = jnp.zeros((z.T3, z.D), f32)
        return 0

    lax.fori_loop(0, z.T // z.T3, prepare, 0)
    fetch.head()

    held = ((wg, wg_out), (wu, wu_out), (wd, wd_out))

    def block(j, _):
        fetch.serve(j)
        start([pltpu.make_async_copy(v.at[j], o.at[j], out_sem.at[k]) for k, (v, o) in enumerate(held)])

        def chunk(i, _):
            rows = at(i * z.TC, z.TC)
            gate, up = dot(a[rows, :], wg[j]), dot(a[rows, :], wu[j])
            act = (gate * (1.0 / (1.0 + jnp.exp(-gate))) * up).astype(bf16)
            acc[rows, :] += dot(act, wd[j])
            return 0

        lax.fori_loop(0, z.T // z.TC, chunk, 0)
        return 0

    lax.fori_loop(0, z.NB, block, 0)

    def finish(i, _):
        rows = at(i * z.T3, z.T3)
        xs[rows, :] = xs[rows, :] + acc[rows, :].astype(bf16)
        return 0

    lax.fori_loop(0, z.T // z.T3, finish, 0)
    store = pltpu.make_async_copy(xs, h_out, h_sem)
    store.start()

    for k, (v, _) in enumerate(held):
        wait(v, out_sem.at[k])
    fetch.end()
    store.wait()


class Reduce:
    def __init__(self, z, here, units, stage, got_p, got_x1, got_x2, got_r, send_x1, send_x2, kept, send_r, send_a, fin, fin_pair, sems):
        self.z, self.here, self.units = z, here, units
        self.stage, self.got_p, self.got_x1, self.got_x2, self.got_r = stage, got_p, got_x1, got_x2, got_r
        self.send_x1, self.send_x2, self.kept, self.send_r, self.send_a = send_x1, send_x2, kept, send_r, send_a
        self.fin, self.fin_pair = fin, fin_pair
        self.p_sent, self.p_got, self.x1_sent, self.x1_got, self.x2_sent, self.x2_got, self.r_sent, self.r_got, self.a_sent, self.a_got, self.f_sent, self.f_got, self.own_done = sems

    @staticmethod
    def scratch(z, units):
        u = z.U
        return [
            VMEM((2, X, CORES, u, LANES), bf16),
            VMEM((units, X, u, LANES), bf16),
            VMEM((units, 2, u // 2, LANES), bf16),
            VMEM((units, 2, u, LANES), bf16),
            VMEM((units, z.R, z.PR, LANES), bf16),
            VMEM((u, LANES), bf16),
            VMEM((2, u, LANES), bf16),
            VMEM((u, LANES), f32),
            VMEM((u, LANES), bf16),
            VMEM((z.PR, LANES), bf16),
        ]

    @staticmethod
    def sems(units):
        return [DMA((units,)) for _ in range(10)] + [DMA, DMA, DMA]

    def peers(self):
        here = self.here
        return [here.partner(), here.along_x(1), here.along_x(X - 1)] + [here.along_r(k) for k in range(1, here.R)]

    def p(self, u):
        here = self.here
        return [remote(self.stage.at[lax.rem(u, 2), x, 1 - here.c], self.got_p.at[u, x], self.p_sent.at[u], self.p_got.at[u], here.partner()) for x in range(X)]

    def start_p(self, u):
        start(self.p(u))

    def both(self, u, x, rows):
        return self.stage[lax.rem(u, 2), x, self.here.c, rows, :].astype(f32) + self.got_p[u, x, rows, :].astype(f32)

    def over(self, work, begin=0, end=None):
        size = self.z.h
        end = self.z.U if end is None else end

        def one(i, _):
            work(at(begin + i * size, size))
            return 0

        lax.fori_loop(0, (end - begin) // size, one, 0)

    def x1(self, u):
        here, half = self.here, self.z.U // 2
        return [
            remote(self.send_x1.at[pl.ds(0, half), :], self.got_x1.at[u, 0], self.x1_sent.at[u], self.x1_got.at[u], here.along_x(1)),
            remote(self.send_x1.at[pl.ds(half, half), :], self.got_x1.at[u, 1], self.x1_sent.at[u], self.x1_got.at[u], here.along_x(X - 1)),
        ]

    def start_x1(self, u):
        wait(self.got_p.at[u], self.p_got.at[u])
        far = lax.rem(self.here.x + 2, X)

        def work(rows):
            self.send_x1[rows, :] = self.both(u, far, rows).astype(bf16)

        self.over(work)
        start(self.x1(u))

    def x2(self, u):
        here = self.here
        return [
            remote(self.send_x2.at[side], self.got_x2.at[u, side], self.x2_sent.at[u], self.x2_got.at[u], here.along_x((1, X - 1)[side]))
            for side in range(2)
        ]

    def start_x2(self, u):
        wait(self.got_x1.at[u], self.x1_got.at[u])
        wait(self.got_x1.at[u], self.x1_sent.at[u])
        half = self.z.U // 2
        right, left = lax.rem(self.here.x + 1, X), lax.rem(self.here.x + X - 1, X)

        def first(rows):
            self.send_x2[0, rows, :] = (self.both(u, right, rows) + self.got_x1[u, 0, rows, :].astype(f32)).astype(bf16)
            self.send_x2[1, rows, :] = self.both(u, left, rows).astype(bf16)

        def second(rows):
            there = at(rows.start - half, rows.size)
            self.send_x2[0, rows, :] = self.both(u, right, rows).astype(bf16)
            self.send_x2[1, rows, :] = (self.both(u, left, rows) + self.got_x1[u, 1, there, :].astype(f32)).astype(bf16)

        self.over(first, 0, half)
        self.over(second, half)
        start(self.x2(u))

    def share(self, p):
        return at(p * self.z.PR, self.z.PR)

    def is_active(self):
        return self.here.r < self.z.active

    def start_r(self, u):
        wait(self.got_x2.at[u], self.x2_got.at[u])
        wait(self.got_x2.at[u], self.x2_sent.at[u])
        wait(self.got_p.at[u], self.p_sent.at[u])

        def work(rows):
            total = self.both(u, self.here.x, rows) + self.got_x2[u, 0, rows, :].astype(f32) + self.got_x2[u, 1, rows, :].astype(f32)
            self.kept[rows, :] = total
            self.send_r[rows, :] = total.astype(bf16)

        self.over(work)

        def send(k, _):
            here, p = self.here, lax.rem(self.here.r + k, self.here.R)

            @pl.when(p < self.z.active)
            def _():
                remote(self.send_r.at[self.share(p), :], self.got_r.at[u, here.r], self.r_sent.at[u], self.r_got.at[u], here.along_r(k)).start()

            return 0

        lax.fori_loop(1, self.z.R, send, 0)

    def start_a(self, u):
        z, here = self.z, self.here

        @pl.when(jnp.logical_not(self.is_active()))
        def _():
            wait(self.got_r.at[u, pl.ds(0, z.active)], self.r_sent.at[u])

        @pl.when(self.is_active())
        def _():
            wait(self.got_r.at[u, pl.ds(0, z.active - 1)], self.r_sent.at[u])
            wait(self.got_r.at[u, pl.ds(0, z.R - 1)], self.r_got.at[u])
            total = self.kept[self.share(here.r), :]
            total = lax.fori_loop(1, z.R, lambda k, t: t + self.got_r[u, lax.rem(here.r + k, z.R)].astype(f32), total)
            pl.when(u > 0)(lambda: self.wait_a_sent(u - 1))
            self.send_a[...] = total.astype(bf16)
            pltpu.make_async_copy(self.send_a, self.fin.at[u, self.share(here.r), :], self.own_done).start()

            def send(k, _):
                remote(self.send_a, self.fin.at[u, self.share(here.r), :], self.a_sent.at[u], self.a_got.at[u], here.along_r(k)).start()
                return 0

            lax.fori_loop(1, z.R, send, 0)

    def wait_a_sent(self, u):
        wait(self.send_a, self.own_done)
        wait(self.got_r.at[u, pl.ds(0, self.z.R - 1)], self.a_sent.at[u])

    def end(self):
        z = self.z
        pl.when(self.is_active())(lambda: self.wait_a_sent(self.units - 1))

        def arrive(u, _):
            @pl.when(jnp.logical_not(self.is_active()))
            def _():
                wait(self.got_r.at[u, pl.ds(0, z.active)], self.a_got.at[u])

            @pl.when(self.is_active())
            def _():
                wait(self.got_r.at[u, pl.ds(0, z.active - 1)], self.a_got.at[u])

            self.f(u).start()
            return 0

        lax.fori_loop(0, self.units, arrive, 0)
        wait(self.fin_pair, self.f_sent)
        wait(self.fin_pair, self.f_got)

    def f(self, u):
        z = self.z
        return remote(self.fin.at[u, pl.ds(2 * z.half, z.half), :], self.fin_pair.at[u], self.f_sent, self.f_got, self.here.partner())


def backward_kernel(z, fetching, h_in, dh_in, w0, w1, w2, dx_out, fin, fin_pair, spill, dx_buf, h_buf, a, at_, dh, dht, wg, wu, wd, work, ld_sem, dh_sem, w_sem, sp_sem, s3_sem, o_sem, *rest):
    T, TC, T3, NB, FB, D = z.T, z.TC, z.T3, z.NB, z.FB, z.D
    here = Here(z)
    n_fetch = len(Fetch.scratch(z)) if fetching else 0
    fetch_sems, rest = rest[:n_fetch], rest[n_fetch:]
    reduce = Reduce(z, here, NB, *rest[:10], fin, fin_pair, rest[10:])
    peers = reduce.peers() + ([here.along_x(2)] if fetching else [])
    met = meet(peers)
    whole = pltpu.make_async_copy(dh_in, dh, dh_sem)
    whole.start()

    def load_h(i):
        return pltpu.make_async_copy(h_in.at[at(i * T3, T3), :], h_buf.at[lax.rem(i, 2)], ld_sem.at[lax.rem(i, 2)])

    load_h(0).start()
    if fetching:
        fetch = Fetch(z, here, (w0, w1, w2), (wg, wu, wd), fetch_sems)
        fetch.begin_local()
        met()
        fetch.begin()
    else:

        def loads(j):
            return [pltpu.make_async_copy(src.at[j], dst.at[j], w_sem.at[k, j]) for k, (src, dst) in enumerate(((w0, wg), (w1, wu), (w2, wd)))]

        for j in range(NB):
            start(loads(j))
    whole.wait()
    n3 = T // T3

    def prepare(i, _):
        rows = at(i * T3, T3, 128)
        pl.when(i + 1 < n3)(lambda: load_h(i + 1).start())
        load_h(i).wait()
        value = normed(h_buf[lax.rem(i, 2)].astype(f32))[0]
        a[rows, :] = value
        at_[:, rows] = value.T
        dht[:, rows] = dh[rows, :].T
        return 0

    lax.fori_loop(0, n3, prepare, 0)
    if fetching:
        fetch.head()
    else:
        met()

    def product(k, rows):
        return work.at[at(k * T + rows.start, rows.size), :]

    def spills(j):
        return [pltpu.make_async_copy(work.at[pl.ds((1 + k) * T, T), :], spill.at[k, j], sp_sem.at[k]) for k in range(2)]

    def spilled(j):
        for copy in spills(j):
            copy.wait()

    def block(j, _):
        if fetching:
            fetch.serve(j)
        else:
            for copy in loads(j):
                copy.wait()
        pl.when(j > 0)(lambda: spilled(j - 1))

        def chunk(i, _):
            rows = at(i * TC, TC)
            gate, up = dot(a[rows, :], wg[j]), dot(a[rows, :], wu[j])
            by_act = dot(dh[rows, :], wd[j], ((1,), (1,))).astype(bf16).astype(f32)
            sig = 1.0 / (1.0 + jnp.exp(-gate))
            silu = gate * sig
            product(0, rows)[...] = (silu * up).astype(bf16)
            product(1, rows)[...] = (by_act * up * (sig + silu * (1.0 - sig))).astype(bf16)
            product(2, rows)[...] = (by_act * silu).astype(bf16)
            return 0

        lax.fori_loop(0, T // TC, chunk, 0)
        start(spills(j))
        pl.when(j > 0)(lambda: reduce.start_x1(j - 1))
        pl.when(j > 1)(lambda: reduce.start_r(j - 2))

        stage, slot = reduce.stage, lax.rem(j, 2)
        m = CORES * z.h

        def rows_of(i, _):
            rows = at(i * m, m)
            gates = dot(at_[rows, :], work[pl.ds(T, T), :]).astype(bf16)
            ups = dot(at_[rows, :], work[pl.ds(2 * T, T), :]).astype(bf16)
            downs = dot(dht[rows, :], work[pl.ds(0, T), :]).astype(bf16)
            for l in range(X):
                lanes = slice(l * LANES, (l + 1) * LANES)
                for c in range(CORES):
                    part = slice(c * z.h, (c + 1) * z.h)
                    stage[slot, i, c, pl.ds(l * z.h, z.h), :] = gates[part, lanes]
                    stage[slot, i, c, pl.ds(z.half + l * z.h, z.h), :] = ups[part, lanes]
                stage[slot, l, lax.div(i, 2), at(2 * z.half + lax.rem(i, 2) * m, m), :] = downs[:, lanes]
            return 0

        lax.fori_loop(0, X, rows_of, 0)
        reduce.start_p(j)
        pl.when(j > 0)(lambda: reduce.start_x2(j - 1))
        pl.when(j > 1)(lambda: reduce.start_a(j - 2))
        return 0

    lax.fori_loop(0, NB, block, 0)
    spilled(NB - 1)

    def load_3(i):
        slot, rows = lax.rem(i, 2), at(i * T3, T3)
        out = [load_h(i)]
        for k in range(2):
            for j in range(NB):
                out.append(pltpu.make_async_copy(spill.at[k, j, rows, :], work.at[at(((slot * 2 + k) * NB + j) * T3, T3), :], s3_sem.at[slot]))
        return out

    def store_3(i):
        return pltpu.make_async_copy(dx_buf.at[lax.rem(i, 2)], dx_out.at[at(i * T3, T3), :], o_sem.at[lax.rem(i, 2)])

    start(load_3(0))
    steps = {1: [lambda: reduce.start_x1(NB - 1)], 3: [lambda: reduce.start_x2(NB - 1)], 6: [lambda: reduce.start_r(NB - 1)]}
    if NB > 1:
        steps.setdefault(0, []).append(lambda: reduce.start_r(NB - 2))
        steps.setdefault(2, []).append(lambda: reduce.start_a(NB - 2))
    last = []
    for i in sorted(steps):
        if i >= n3:
            last += steps.pop(i)

    def rows_back(i, _):
        slot, rows = lax.rem(i, 2), at(i * T3, T3)
        pl.when(i + 1 < n3)(lambda: start(load_3(i + 1)))
        load_h(i).wait()
        wait(work.at[at(slot * 2 * NB * T3, 2 * NB * T3), :], s3_sem.at[slot])
        pl.when(i > 1)(lambda: store_3(i - 2).wait())
        back = []
        for k, w in ((0, wg), (1, wu)):
            total = None
            for j in range(NB):
                part = dot(work[at(((slot * 2 + k) * NB + j) * T3, T3), :], w[j], ((1,), (1,)))
                total = part if total is None else total + part
            back.append(total.astype(bf16))
        by_a = (back[0] + back[1]).astype(f32)
        wide = h_buf[slot].astype(f32)
        square = jnp.mean(wide * wide, -1, keepdims=True) + 1e-6
        scale = lax.rsqrt(square)
        by_scale = jnp.sum(by_a * wide, -1, keepdims=True)
        by_square = by_scale * (-0.5 * scale / square) * (2.0 / D)
        dx_buf[slot] = dh[rows, :] + (by_a * scale + by_square * wide).astype(bf16)
        store_3(i).start()
        for when, todo in steps.items():

            def now(todo=todo):
                for do in todo:
                    do()

            pl.when(i == when)(now)
        return 0

    lax.fori_loop(0, n3, rows_back, 0)
    for do in last:
        do()
    reduce.start_a(NB - 1)
    reduce.end()
    if fetching:
        fetch.end()
    for i in range(max(0, n3 - 2), n3):
        store_3(i).wait()


def call(body, z, out, n_in, scratch, number):
    return pl.pallas_call(
        functools.partial(body, z),
        out_shape=out,
        in_specs=[pl.BlockSpec(memory_space=HBM)] * n_in,
        out_specs=[pl.BlockSpec(memory_space=HBM)] * len(out),
        scratch_shapes=scratch,
        compiler_params=pltpu.CompilerParams(collective_id=number, has_side_effects=True, vmem_limit_bytes=66_900_000),
    )


def forward(z, x, shards):
    S = jax.ShapeDtypeStruct
    wide, tall = (z.NB, z.D, z.FB), (z.NB, z.FB, z.D)
    scratch = [VMEM((z.T, z.D), bf16), VMEM((z.T, z.D), f32), VMEM((z.T, z.D), bf16), VMEM(wide, bf16), VMEM(wide, bf16), VMEM(tall, bf16)]
    out = [S((z.T, z.D), bf16), S(wide, bf16), S(wide, bf16), S(tall, bf16)]
    h, *w = call(forward_kernel, z, out, 4, scratch + [DMA, DMA((3,)), DMA] + Fetch.scratch(z), 0)(x, *shards)
    return h, w


def backward(z, h, dh, w, fetching, number):
    S = jax.ShapeDtypeStruct
    wide, tall = (z.NB, z.D, z.FB), (z.NB, z.FB, z.D)
    tokens = (z.T, z.D)
    scratch = [VMEM((2, z.T3, z.D), bf16), VMEM((2, z.T3, z.D), bf16)]
    scratch += [VMEM(tokens, bf16), VMEM(tokens[::-1], bf16), VMEM(tokens, bf16), VMEM(tokens[::-1], bf16)]
    scratch += [VMEM(wide, bf16), VMEM(wide, bf16), VMEM(tall, bf16), VMEM((max(3 * z.T, 4 * z.NB * z.T3), z.FB), bf16)]
    scratch += [DMA((2,)), DMA, DMA((3, z.NB)), DMA((2,)), DMA((2,)), DMA((2,))]
    if fetching:
        scratch += Fetch.scratch(z)
    scratch += Reduce.scratch(z, z.NB) + Reduce.sems(z.NB)
    out = [S(tokens, bf16), S((z.NB, z.U, LANES), bf16), S((z.NB, z.half, LANES), bf16), S((2, z.NB, z.T, z.FB), bf16)]

    def body(z, *refs):
        backward_kernel(z, fetching, *refs)

    dx, fin, fin_pair, _ = call(body, z, out, 5, scratch, number)(h, dh, *w)
    return dx, fin, fin_pair


def blocks_of(z, fin, fin_pair):
    c = lax.rem(lax.axis_index("s"), CORES)

    def wide(part):
        return part.reshape(z.NB, X, z.h, LANES).transpose(2, 1, 0, 3).reshape(z.h, z.F)

    mine, other = fin[:, 2 * z.half :], fin_pair
    low, high = jnp.where(c == 0, mine, other), jnp.where(c == 0, other, mine)
    down = jnp.concatenate([low, high], 1).transpose(0, 2, 1).reshape(z.NB * LANES, z.D)
    down = lax.dynamic_slice(down, (c * (z.NB * 64), 0), (z.NB * 64, z.D))
    return wide(fin[:, : z.half]), wide(fin[:, z.half : 2 * z.half]), down


def solution(mesh):
    def step(x, dy, *weights):
        z = Sizes(mesh, x.shape[1], x.shape[2], weights[0].shape[2])
        h, w = forward(z, x[0], [v[0] for v in weights])
        dh, *one = backward(z, h, dy[0], [v[1] for v in weights], True, 1)
        dx, *zero = backward(z, x[0], dh, w, False, 2)
        grads = zip(blocks_of(z, *zero), blocks_of(z, *one), strict=True)
        return (dx[None], *(jnp.stack(pair) for pair in grads))

    states, cut = P(("rep", "r", "s"), None, None), P(None, "s", None)
    return jax.shard_map(
        step,
        mesh=mesh,
        in_specs=(states, states) + (cut,) * 3,
        out_specs=(states,) + (P("rep", "s", None),) * 3,
        check_vma=False,
    )
```

time: 764 us -> 438 us (0.57); the launches traced: 754 us -> 437 us
  Pallas kernels: 0 us -> 412 us
  waiting for transfers between devices: 365 us -> 0 us
  matrix products: 331 us -> 0 us
  between operations: 14.2 us -> 0.78 us
  local copies, waits for them, and re-layouts: 27.7 us -> 17.9 us
  other arithmetic: 15.5 us -> 6.14 us
    pallas_call x0 -> x3, Pallas kernels: none -> 412 us  [the longest x2 346 us: backward(): dx, fin, fin_pair, _ = call(body, z, out, 5, scratch, number)(h, dh, *w)]
    dot_general x17 -> x0, matrix products: 331 us -> none  [the longest x6 121 us: layer(): up = jnp.dot(a, w['w_up'], preferred_element_type=jnp.float32)]
    reduce_scatter x6 -> x0, waiting for transfers between devices: 133 us -> none  [summed(): lax.psum_scatter(term, 's', scatter_dimension=0, tiled=True)]
    psum x1 -> x0, waiting for transfers between devices: 119 us -> none  [summed(): lax.psum(lax.psum_scatter(term, 's', scatter_dimension=0, tiled=True), 'r')]
    all_gather x6 -> x0, waiting for transfers between devices: 112 us -> none  [fetched(): lax.all_gather(w[number], 's', axis=0, tiled=True)]
    unnamed x25 -> x15, local copies, waits for them, and re-layouts: 20.7 us -> 8.2 us
  transfers between devices with their start and end apart: 13 -> 0, of which waited for: 11 -> 0; matrix products, arithmetic and copies ran while one was open for 37% -> 0% of each run, Pallas kernels for 0% -> 0%
where the time goes in v1:
time: 438 us; the launch traced here: 437 us
  Pallas kernels  412 us (94%)
  local copies, waits for them, and re-layouts  17.9 us (4%)
  other arithmetic  6.14 us (1%)
    pallas_call x2, Pallas kernels, backward(): dx, fin, fin_pair, _ = call(body, z, out, 5, scratch, number)(h, dh, *w)  346 us
    pallas_call x1, Pallas kernels, forward(): call(forward_kernel, z, out, 4, scratch + [DMA, DMA((3,)), DMA] + Fetch.s...  66.2 us

profile of v1, /device:TPU:1, one launch (start us, length us, event | category | flops | bytes accessed | tf_op | source)
XLA Modules:
  0.0 437.0 jit_solution(9944435947350279852)
XLA Ops:
  0.6 0.0 copy-start.4
  0.6 0.0 copy-start.5
  0.7 2.5 slice_bitcast_fusion
  3.1 0.0 copy-done.4
  3.2 1.4 slice_bitcast_fusion.1
  4.6 66.2 %shard_map.84 = (bf16[2048,896]{1,0:T(8,128)(2,1)}, bf16[5,896,512]{2,1,0:T(8,128)(2,1)}, bf16[5,896,512]{2,1,0:T(8,128)(2,1)}, bf16[5,512,896]{2,1,0:T(8,128)(2,1)}) custom-call(bf16[2048,896]{1,0:T(8,128)(2,1)} %bitcast.41, bf16[112,2560]{1,0:T(8,128)(2,1)} %get-tuple-element.42.sg, bf16[112,2560]{1,0:T(8,128)(2,1)} %get-tuple-element.39.su, ...), custom_call_target="tpu_custom_call" | custom-call | tf_op jit(solution)/shard_map/pallas_call | solution.py:652
  70.8 185.1 %shard_map.85 = (bf16[2048,896]{1,0:T(8,128)(2,1)}, bf16[5,1344,128]{2,1,0:T(8,128)(2,1)}, bf16[5,448,128]{2,1,0:T(8,128)(2,1)}, bf16[2,5,2048,512]{3,2,1,0:T(8,128)(2,1)}) custom-call(bf16[2048,896]{1,0:T(8,128)(2,1)} %get-tuple-element.14.refs_0_, bf16[2048,896]{1,0:T(8,128)(2,1)} %bitcast.43, bf16[112,2560]{1,0:T(8,128)(2,1)} %get-tuple-element.43.refs_2_, ...), custom_call_target="tpu_custom_call" | custom-call | tf_op jit(solution)/shard_map/pallas_call | solution.py:672
  255.9 1.7 broadcast_select_fusion.1
  257.6 0.1 maximum_bitcast_fusion.1
  257.7 1.0 copy.18
  258.7 0.9 dynamic-slice_bitcast_fusion
  259.6 1.1 copy.16
  260.7 1.1 copy.14
  261.8 161.0 %shard_map.86 = (bf16[2048,896]{1,0:T(8,128)(2,1)}, bf16[5,1344,128]{2,1,0:T(8,128)(2,1)}, bf16[5,448,128]{2,1,0:T(8,128)(2,1)}, bf16[2,5,2048,512]{3,2,1,0:T(8,128)(2,1)}) custom-call(bf16[2048,896]{1,0:T(8,128)(2,1)} %bitcast.42, bf16[2048,896]{1,0:T(8,128)(2,1)} %get-tuple-element.15.refs_1_, bf16[5,896,512]{2,1,0:T(8,128)(2,1)} %get-tuple-element.16.refs_2_, ...), custom_call_target="tpu_custom_call" | custom-call | tf_op jit(solution)/shard_map/pallas_call | solution.py:672
  422.7 2.5 broadcast_select_fusion.3
  425.3 0.1 maximum_bitcast_fusion
  425.4 1.0 copy.17
  426.4 0.0 copy-start.3
  426.4 0.1 dynamic-slice_bitcast_fusion.1
  426.4 1.0 copy-done.3
  427.4 1.1 pad_maximum_fusion.2
  428.6 0.0 copy-done.2
  428.6 0.3 copy.15
  428.9 0.2 copy-done.1
  429.1 0.3 pad_maximum_fusion.1
  429.4 0.0 copy-start
  429.4 1.4 copy.20
  430.8 0.3 copy.13
  431.2 0.0 copy-done
  431.2 0.3 pad_maximum_fusion
  431.5 1.4 copy.19
  432.9 4.2 copy.22
  (3 shorter events, 0.0 us)
Async XLA Ops:
  0.6 2.5 copy-start.4
  0.6 2.5 copy-start.5
  426.4 1.1 copy-start.3
  427.4 1.2 copy-start.2
  427.4 1.7 copy-start.1
  429.4 1.8 copy-start

commit v2 on v0

v2 whole, which is shorter than its diff:
```python
import functools

import jax
import jax.numpy as jnp
from jax import lax
from jax.experimental import pallas as pl
from jax.experimental.pallas import tpu as pltpu
from jax.sharding import PartitionSpec as P

f32, bf16 = jnp.float32, jnp.bfloat16
MESH = pl.DeviceIdType.MESH
LANES = 128
X, CORES, Y = 4, 2, 4
HBM, VMEM, DMA = pl.ANY, pltpu.VMEM, pltpu.SemaphoreType.DMA


def dot(a, b, dims=((1,), (0,))):
    return lax.dot_general(a, b, (dims, ((), ())), preferred_element_type=f32)


def at(start, size, multiple=16):
    return pl.ds(pl.multiple_of(start, multiple) if not isinstance(start, int) else start, size)


class Sizes:
    chunk, rows = 1024, 256

    def __init__(self, mesh, tokens, d, ff):
        self.R = mesh.shape["r"]
        self.Z = self.R // Y
        self.T, self.D, self.F = tokens, d, ff
        self.NB = ff // (X * LANES)
        self.FB = X * LANES
        self.h = d // (X * CORES)
        self.TC = min(self.chunk, tokens)
        self.T3 = min(self.rows, tokens)
        self.U = 3 * X * self.h
        self.S = self.U // Y
        self.active = self.h // 16
        assert self.h % 16 == 0 and self.active <= self.Z and mesh.shape["s"] == X * CORES

    def piece(self, y, z, matrix):
        return pl.ds(y * self.S + z * 48 + matrix * 16, 16)


class Here:
    def __init__(self, z):
        s, self.r = lax.axis_index("s"), lax.axis_index("r")
        self.x, self.c = lax.div(s, CORES), lax.rem(s, CORES)
        self.y, self.z, self.Z = lax.div(self.r, z.Z), lax.rem(self.r, z.Z), z.Z
        self.R = z.R

    def partner(self):
        return {"s": self.x * CORES + 1 - self.c}

    def along_x(self, k):
        return {"s": lax.rem(self.x + k, X) * CORES + self.c}

    def along_y(self, k):
        return {"r": lax.rem(self.y + k, Y) * self.Z + self.z}

    def along_z(self, k):
        return {"r": self.y * self.Z + lax.rem(self.z + k, self.Z)}


def remote(src, dst, sent, got, where):
    return pltpu.make_async_remote_copy(src_ref=src, dst_ref=dst, send_sem=sent, recv_sem=got, device_id=where, device_id_type=MESH)


def start(copies):
    for copy in copies:
        copy.start()


def wait(ref, sem):
    pltpu.make_async_copy(ref, ref, sem).wait()


def meet(peers):
    barrier = pltpu.get_barrier_semaphore()
    for peer in peers:
        pl.semaphore_signal(barrier, inc=1, device_id=peer, device_id_type=MESH)
    return lambda: pl.semaphore_wait(barrier, len(peers))


class Fetch:
    PHASES = ("a1", "a2", "b1", "b2", "c", "d1", "d2", "e")

    def __init__(self, z, here, shards, w, sems):
        self.z, self.here, self.shards, self.w = z, here, shards, w
        self.local, self.local_d, self.pair, self.pair_sent = sems[:4]
        self.got = dict(zip(self.PHASES, sems[4::2], strict=True))
        self.sent = dict(zip(self.PHASES, sems[5::2], strict=True))

    @classmethod
    def scratch(cls, z):
        return [DMA((z.NB,)), DMA, DMA, DMA] + [DMA((z.NB,)) for _ in range(2 * len(cls.PHASES))]

    def peers(self):
        here = self.here
        return [here.partner()] + [here.along_x(k) for k in range(1, X)] + [here.along_y(k) for k in range(1, Y)]

    def own(self, j):
        z, here = self.z, self.here
        for shard, w in zip(self.shards[:2], self.w[:2], strict=True):
            for l in range(X):
                slot = w.at[j, self.rows(here.x), pl.ds(l * LANES, LANES)]
                pltpu.make_async_copy(shard.at[:, at((l * z.NB + j) * LANES, LANES, LANES)], slot, self.local.at[j]).start()

    def own_down(self, k):
        z, here = self.z, self.here
        place = here.c * z.NB + k
        return self.shards[2].at[pl.ds(64 * k, 64), :], self.w[2].at[lax.div(place, 2), at(here.x * LANES + lax.rem(place, 2) * 64, 64), :]

    def rows(self, x):
        return at(x * (CORES * self.z.h) + self.here.c * self.z.h, self.z.h)

    def lanes(self, y):
        return at(y * LANES, LANES, LANES)

    def down(self, x, begin=0, size=64):
        return at(x * LANES + self.here.c * 64 + begin, size)

    def send(self, phase, j, w, rows, lanes, where):
        slot = self.w[w].at[j, rows, lanes]
        remote(slot, slot, self.sent[phase].at[j], self.got[phase].at[j], where).start()

    def begin_local(self):
        for j in range(self.z.NB):
            self.own(j)
        for k in range(self.z.NB):
            pltpu.make_async_copy(*self.own_down(k), self.local_d).start()

    def start_a1(self, j, first=False):
        here = self.here
        wait(self.w[0].at[j, pl.ds(0, 2 * self.z.h), :], self.local.at[j])
        for k in (1, 3, 2) if first else (1, 3):
            for w in range(2):
                self.send("a1", j, w, self.rows(here.x), self.lanes(here.y), here.along_x(k))

    def start_d1(self, j, first=False):
        here = self.here
        for k in (1, 3, 2) if first else (1, 3):
            self.send("d1", j, 2, self.down(here.x), slice(None), here.along_x(k))

    def start_2(self, j):
        here = self.here
        left, right = lax.rem(here.x + 3, X), lax.rem(here.x + 1, X)
        wait(self.pieces(j, 4), self.got["a1"].at[j])
        self.send("a2", j, 0, self.rows(left), self.lanes(here.y), here.along_x(1))
        self.send("a2", j, 1, self.rows(right), self.lanes(here.y), here.along_x(3))
        wait(self.halves(j, 2), self.got["d1"].at[j])
        self.send("d2", j, 2, self.down(left, 0, 32), slice(None), here.along_x(1))
        self.send("d2", j, 2, self.down(right, 32, 32), slice(None), here.along_x(3))

    def start_b1(self, j, first=False):
        here = self.here
        if first:
            wait(self.pieces(j, 6), self.got["a1"].at[j])
        else:
            wait(self.pieces(j, 2), self.got["a2"].at[j])
        for k in (1, 3, 2) if first else (1, 3):
            for m in range(1, X):
                for w in range(2):
                    self.send("b1", j, w, self.rows(lax.rem(here.x + m, X)), self.lanes(here.y), here.along_y(k))

    def start_b2(self, j):
        here = self.here
        wait(self.pieces(j, 12), self.got["b1"].at[j])
        for m in range(1, X):
            rows = self.rows(lax.rem(here.x + m, X))
            self.send("b2", j, 0, rows, self.lanes(lax.rem(here.y + 3, Y)), here.along_y(1))
            self.send("b2", j, 1, rows, self.lanes(lax.rem(here.y + 1, Y)), here.along_y(3))

    def start_c(self, j, first=False):
        here = self.here
        if first:
            wait(self.pieces(j, 18), self.got["b1"].at[j])
        else:
            wait(self.pieces(j, 6), self.got["b2"].at[j])
        for w in range(2):
            for x in range(X):
                self.send("c", j, w, self.rows(x), slice(None), here.partner())
        if first:
            wait(self.halves(j, 3), self.got["d1"].at[j])
        else:
            wait(self.halves(j, 1), self.got["d2"].at[j])
        for m in range(1, X):
            self.send("e", j, 2, self.down(lax.rem(here.x + m, X)), slice(None), here.partner())

    def pieces(self, j, n):
        return self.w[0].at[j, pl.ds(0, min(n, 6) * self.z.h), pl.ds(0, max(n // 6, 1) * LANES)]

    def halves(self, j, n):
        return self.w[2].at[j, pl.ds(0, 64 * n), :]

    def begin(self):
        nb = self.z.NB
        for k in range(nb):
            src, slot = self.own_down(k)
            remote(src, slot, self.pair_sent, self.pair, self.here.partner()).start()
        self.start_a1(0, True)
        if nb > 1:
            self.start_a1(1)
        wait(self.halves(0, nb), self.local_d)
        wait(self.halves(0, nb), self.pair)
        self.start_d1(0, True)
        if nb > 1:
            self.start_d1(1)

    def head(self):
        nb = self.z.NB
        self.start_b1(0, True)
        if nb > 1:
            self.start_2(1)
        if nb > 2:
            self.start_a1(2)
            self.start_d1(2)
        self.start_c(0, True)
        if nb > 1:
            self.start_b1(1)

    def serve_a(self, j):
        nb = self.z.NB
        pl.when(j + 1 < nb)(lambda: self.start_b2(j + 1))
        pl.when(j + 2 < nb)(lambda: self.start_2(j + 2))
        wait(self.w[0].at[j], self.got["c"].at[j])
        wait(self.halves(j, 3), self.got["e"].at[j])

    def serve_b(self, j):
        nb = self.z.NB
        pl.when(j + 1 < nb)(lambda: self.start_c(j + 1))
        pl.when(j + 2 < nb)(lambda: self.start_b1(j + 2))

        @pl.when(j + 3 < nb)
        def _():
            self.start_a1(j + 3)
            self.start_d1(j + 3)

    def end(self):
        wait(self.halves(0, self.z.NB), self.pair_sent)

        def drain(j, first):
            wait(self.pieces(j, 6 if first else 4), self.sent["a1"].at[j])
            wait(self.pieces(j, 18 if first else 12), self.sent["b1"].at[j])
            wait(self.halves(j, 3 if first else 2), self.sent["d1"].at[j])
            if not first:
                wait(self.pieces(j, 2), self.sent["a2"].at[j])
                wait(self.pieces(j, 6), self.sent["b2"].at[j])
                wait(self.halves(j, 1), self.sent["d2"].at[j])
            wait(self.w[0].at[j], self.sent["c"].at[j])
            wait(self.halves(j, 3), self.sent["e"].at[j])
            return 0

        drain(0, True)
        lax.fori_loop(1, self.z.NB, lambda j, _: drain(j, False), 0)


def normed(wide):
    scale = lax.rsqrt(jnp.mean(wide * wide, -1, keepdims=True) + 1e-6)
    return (wide * scale).astype(bf16), scale


def forward_kernel(z, x_in, sg, su, sd, h_out, wg_out, wu_out, wd_out, a, acc, xs, act, wg, wu, wd, x_sem, out_sem, h_sem, *sems):
    here = Here(z)
    fetch = Fetch(z, here, (sg.at[0], su.at[0], sd.at[0]), (wg, wu, wd), sems)
    met = meet(fetch.peers())
    fetch.begin_local()
    load = pltpu.make_async_copy(x_in, xs, x_sem)
    load.start()
    met()
    fetch.begin()
    load.wait()

    def prepare(i, _):
        rows = at(i * z.T3, z.T3)
        a[rows, :] = normed(xs[rows, :].astype(f32))[0]
        acc[rows, :] = jnp.zeros((z.T3, z.D), f32)
        return 0

    lax.fori_loop(0, z.T // z.T3, prepare, 0)
    fetch.head()
    held = ((wg, wg_out), (wu, wu_out), (wd, wd_out))
    n = z.T // z.TC

    def block(j, _):
        fetch.serve_a(j)
        start([pltpu.make_async_copy(v.at[j], o.at[j], out_sem.at[k]) for k, (v, o) in enumerate(held)])

        def chunk(i, _):
            pl.when(i == n // 2)(lambda: fetch.serve_b(j))
            rows = at(i * z.TC, z.TC)
            for half in range(2):
                cols = slice(half * z.FB // 2, (half + 1) * z.FB // 2)
                gate, up = dot(a[rows, :], wg[j, :, cols]), dot(a[rows, :], wu[j, :, cols])
                act[:, cols] = (gate * (1.0 / (1.0 + jnp.exp(-gate))) * up).astype(bf16)
            acc[rows, :] += dot(act[...], wd[j])
            return 0

        lax.fori_loop(0, n, chunk, 0)
        return 0

    lax.fori_loop(0, z.NB, block, 0)

    def finish(i, _):
        rows = at(i * z.T3, z.T3)
        xs[rows, :] = xs[rows, :] + acc[rows, :].astype(bf16)
        return 0

    lax.fori_loop(0, z.T // z.T3, finish, 0)
    store = pltpu.make_async_copy(xs, h_out, h_sem)
    store.start()
    for k, (v, _) in enumerate(held):
        wait(v, out_sem.at[k])
    fetch.end()
    store.wait()


class Reduce:
    PHASES = ("p", "x1", "x2", "y", "z", "az", "ay", "f")

    def __init__(self, z, here, units, fin_out, pair_out, refs):
        self.z, self.here, self.units, self.fin_out, self.pair_out = z, here, units, fin_out, pair_out
        (self.stage, self.got_p, self.got_x1, self.got_x2, self.got_y, self.got_z) = refs[:6]
        (self.send_x1, self.send_x2, self.send_y, self.send_z, self.kept_y, self.kept_z, self.fin) = refs[6:13]
        self.got = dict(zip(self.PHASES, refs[13:29:2], strict=True))
        self.sent = dict(zip(self.PHASES, refs[14:29:2], strict=True))
        self.out_sem = refs[29]

    @classmethod
    def scratch(cls, z, units):
        u, s = z.U, z.S
        data = [(2, X, CORES, u), (3, X, u), (2, 2, u // 2), (2, 2, u), (2, Y, s), (units, z.Z, 48), (u,), (2, u), (u,), (s,)]
        return (
            [VMEM((*shape, LANES), bf16) for shape in data]
            + [VMEM((s, LANES), f32), VMEM((s, LANES), f32), VMEM((units, u, LANES), bf16)]
            + [DMA((units,)) for _ in range(2 * len(cls.PHASES))]
            + [DMA((units,))]
        )

    def peers(self):
        here = self.here
        return (
            [here.partner(), here.along_x(1), here.along_x(3)] + [here.along_y(k) for k in range(1, Y)] + [here.along_z(k) for k in range(1, here.Z)]
        )

    def send(self, phase, u, src, dst, where):
        remote(src, dst, self.sent[phase].at[u], self.got[phase].at[u], where).start()

    def over(self, work, begin, end):
        size = self.z.h

        def one(i, _):
            work(at(begin + i * size, size))
            return 0

        lax.fori_loop(0, (end - begin) // size, one, 0)

    def start_p(self, u):
        here = self.here
        for x in range(X):
            self.send("p", u, self.stage.at[lax.rem(u, 2), x, 1 - here.c], self.got_p.at[lax.rem(u, 3), x], here.partner())

    def both(self, u, x, rows):
        return self.stage[lax.rem(u, 2), x, self.here.c, rows, :].astype(f32) + self.got_p[lax.rem(u, 3), x, rows, :].astype(f32)

    def start_x1(self, u):
        here, half, slot = self.here, self.z.U // 2, lax.rem(u, 2)
        wait(self.got_p.at[lax.rem(u, 3)], self.got["p"].at[u])
        far = lax.rem(here.x + 2, X)

        def work(rows):
            self.send_x1[rows, :] = self.both(u, far, rows).astype(bf16)

        self.over(work, 0, self.z.U)
        for side in range(2):
            self.send("x1", u, self.send_x1.at[pl.ds(side * half, half), :], self.got_x1.at[slot, side], here.along_x((1, 3)[side]))

    def start_x2(self, u):
        here, half, slot = self.here, self.z.U // 2, lax.rem(u, 2)
        wait(self.got_x1.at[slot], self.got["x1"].at[u])
        wait(self.got_x1.at[slot], self.sent["x1"].at[u])
        right, left = lax.rem(here.x + 1, X), lax.rem(here.x + 3, X)

        def first(rows):
            self.send_x2[0, rows, :] = (self.both(u, right, rows) + self.got_x1[slot, 0, rows, :].astype(f32)).astype(bf16)
            self.send_x2[1, rows, :] = self.both(u, left, rows).astype(bf16)

        def second(rows):
            there = at(rows.start - half, rows.size)
            self.send_x2[0, rows, :] = self.both(u, right, rows).astype(bf16)
            self.send_x2[1, rows, :] = (self.both(u, left, rows) + self.got_x1[slot, 1, there, :].astype(f32)).astype(bf16)

        self.over(first, 0, half)
        self.over(second, half, self.z.U)
        for side in range(2):
            self.send("x2", u, self.send_x2.at[side], self.got_x2.at[slot, side], here.along_x((1, 3)[side]))

    def start_y(self, u):
        z, here, slot = self.z, self.here, lax.rem(u, 2)
        wait(self.got_x2.at[slot], self.got["x2"].at[u])
        wait(self.got_x2.at[slot], self.sent["x2"].at[u])
        wait(self.got_p.at[lax.rem(u, 3)], self.sent["p"].at[u])

        def total(rows):
            return self.both(u, here.x, rows) + self.got_x2[slot, 0, rows, :].astype(f32) + self.got_x2[slot, 1, rows, :].astype(f32)

        def work(rows):
            self.send_y[rows, :] = total(rows).astype(bf16)

        def own(rows):
            self.kept_y[rows, :] = total(at(here.y * z.S + rows.start, rows.size))

        self.over(work, 0, z.U)
        self.over(own, 0, z.S)
        for k in (1, 3, 2):
            self.send("y", u, self.send_y.at[at(lax.rem(here.y + k, Y) * z.S, z.S), :], self.got_y.at[slot, here.y], here.along_y(k))

    def start_z(self, u):
        z, here, slot = self.z, self.here, lax.rem(u, 2)
        wait(self.got_y.at[slot, pl.ds(0, Y - 1)], self.got["y"].at[u])
        wait(self.got_y.at[slot, pl.ds(0, Y - 1)], self.sent["y"].at[u])

        def work(rows):
            total = self.kept_y[rows, :]
            for k in range(1, Y):
                total += self.got_y[slot, lax.rem(here.y + k, Y), rows, :].astype(f32)
            self.kept_z[rows, :] = total
            self.send_z[rows, :] = total.astype(bf16)

        self.over(work, 0, z.S)
        for k in range(1, z.Z):
            to = lax.rem(here.z + k, z.Z)
            pl.when(to < z.active)(lambda k=k, to=to: self.send("z", u, self.send_z.at[at(to * 48, 48), :], self.got_z.at[u, here.z], here.along_z(k)))

    def if_active(self, yes, no):
        pl.when(self.here.z < self.z.active)(yes)
        pl.when(self.here.z >= self.z.active)(no)

    def pieces(self, u, n):
        return self.fin.at[u, pl.ds(0, 48 * n), :]

    def wait_pieces(self, u, n, sem):
        if n:
            wait(self.pieces(u, n), sem.at[u])

    def start_az(self, u):
        z, here = self.z, self.here

        def yes():
            self.wait_pieces(u, z.active - 1, self.sent["z"])
            self.wait_pieces(u, z.Z - 1, self.got["z"])
            total = self.kept_z[at(here.z * 48, 48), :]
            for k in range(1, z.Z):
                total += self.got_z[u, lax.rem(here.z + k, z.Z)].astype(f32)
            mine = at(here.y * z.S + here.z * 48, 48)
            self.fin[u, mine, :] = total.astype(bf16)
            for k in range(1, z.Z):
                self.send("az", u, self.fin.at[u, mine, :], self.fin.at[u, mine, :], here.along_z(k))

        self.if_active(yes, lambda: self.wait_pieces(u, z.active, self.sent["z"]))

    def start_ay(self, u):
        z, here = self.z, self.here
        self.if_active(lambda: self.wait_pieces(u, z.active - 1, self.got["az"]), lambda: self.wait_pieces(u, z.active, self.got["az"]))
        share = self.fin.at[u, at(here.y * z.S, z.S), :]
        for k in (1, 3, 2):
            self.send("ay", u, share, share, here.along_y(k))

    def start_f(self, u):
        wait(self.fin.at[u, pl.ds(0, (Y - 1) * self.z.S), :], self.got["ay"].at[u])
        self.send("f", u, self.fin.at[u], self.pair_out.at[u], self.here.partner())
        pltpu.make_async_copy(self.fin.at[u], self.fin_out.at[u], self.out_sem.at[u]).start()

    def end(self):
        z = self.z

        def one(u, _):
            self.if_active(lambda: self.wait_pieces(u, z.Z - 1, self.sent["az"]), lambda: None)
            wait(self.fin.at[u, pl.ds(0, (Y - 1) * z.S), :], self.sent["ay"].at[u])
            wait(self.fin.at[u], self.sent["f"].at[u])
            wait(self.fin.at[u], self.got["f"].at[u])
            wait(self.fin.at[u], self.out_sem.at[u])
            return 0

        lax.fori_loop(0, self.units, one, 0)


def backward_kernel(z, first, *refs):
    T, TC, T3, NB, FB, D = z.T, z.TC, z.T3, z.NB, z.FB, z.D
    here = Here(z)
    refs = list(refs)

    def take(n):
        out, refs[:] = refs[:n], refs[n:]
        return out

    h_in, dh_in, w0, w1, w2 = take(5)
    left_in = None if first else take(1)[0]
    dx_out, fin_out, pair_out, spill = take(4)
    left_out = take(1)[0] if first else None
    dx_buf, h_buf, a, a_t, dh, dh_t, wg, wu, wd, work = take(10)
    ld_sem, dh_sem, w_sem, sp_sem, s3_sem, o_sem, left_sem = take(7)
    fetch = Fetch(z, here, (w0.at[1], w1.at[1], w2.at[1]), (wg, wu, wd), take(len(Fetch.scratch(z)))) if first else None
    base = 0 if first else 1
    units = NB - 1 if first else NB + 1
    reduce = Reduce(z, here, units, fin_out, pair_out, refs)
    met = meet(reduce.peers() + ([here.along_x(2)] if first else []))
    whole = pltpu.make_async_copy(dh_in, dh, dh_sem)
    whole.start()

    def load_h(i):
        return pltpu.make_async_copy(h_in.at[at(i * T3, T3), :], h_buf.at[lax.rem(i, 2)], ld_sem.at[lax.rem(i, 2)])

    load_h(0).start()

    def loads(j):
        return [pltpu.make_async_copy(src.at[j], dst.at[j], w_sem.at[k, j]) for k, (src, dst) in enumerate(((w0, wg), (w1, wu), (w2, wd)))]

    if first:
        fetch.begin_local()
        met()
        fetch.begin()
    else:
        left = pltpu.make_async_copy(left_in, reduce.stage.at[0], left_sem)
        left.start()
        for j in range(NB):
            start(loads(j))
    whole.wait()
    n3 = T // T3

    def prepare(i, _):
        rows = at(i * T3, T3, 128)
        pl.when(i + 1 < n3)(lambda: load_h(i + 1).start())
        load_h(i).wait()
        value = normed(h_buf[lax.rem(i, 2)].astype(f32))[0]
        a[rows, :] = value
        a_t[:, rows] = value.T
        dh_t[:, rows] = dh[rows, :].T
        return 0

    if not first:
        met()
        left.wait()
        reduce.start_p(0)
    lax.fori_loop(0, n3, prepare, 0)
    if first:
        fetch.head()

    def product(k, rows, cols):
        return work.at[at(k * T + rows.start, rows.size), cols]

    def spills(j):
        return [pltpu.make_async_copy(work.at[pl.ds((1 + k) * T, T), :], spill.at[k, j], sp_sem.at[k]) for k in range(2)]

    def spilled(j):
        for copy in spills(j):
            copy.wait()

    def step(name, u):
        do = getattr(reduce, "start_" + name)
        if isinstance(u, int):
            if 0 <= u < units:
                do(u)
        else:
            pl.when(jnp.logical_and(u >= 0, u < units))(lambda: do(u))

    def halfway(i, n, before, after):
        if n == 1:
            before()
            after()
        else:
            pl.when(i == 0)(before)
            pl.when(i == n // 2)(after)

    def block(j, _):
        u = j + base - 1
        if first:
            fetch.serve_a(j)
        else:
            for copy in loads(j):
                copy.wait()
        pl.when(j > 0)(lambda: spilled(j - 1))

        def chunk(i, _):
            def before():
                step("ay", u - 3)
                step("z", u - 2)

            halfway(i, T // TC, before, lambda: step("x1", u))
            rows = at(i * TC, TC)
            for half in range(2):
                cols = slice(half * FB // 2, (half + 1) * FB // 2)
                gate, up = dot(a[rows, :], wg[j, :, cols]), dot(a[rows, :], wu[j, :, cols])
                by_act = dot(dh[rows, :], wd[j, cols, :], ((1,), (1,))).astype(bf16).astype(f32)
                sig = 1.0 / (1.0 + jnp.exp(-gate))
                silu = gate * sig
                product(0, rows, cols)[...] = (silu * up).astype(bf16)
                product(1, rows, cols)[...] = (by_act * up * (sig + silu * (1.0 - sig))).astype(bf16)
                product(2, rows, cols)[...] = (by_act * silu).astype(bf16)
            return 0

        lax.fori_loop(0, T // TC, chunk, 0)
        start(spills(j))
        stage, slot, m = reduce.stage, lax.rem(j + base, 2), D // 2

        def rows_of(i, _):
            def before():
                if first:
                    fetch.serve_b(j)
                step("y", u - 1)
                step("az", u - 2)

            halfway(i, 2, before, lambda: step("x2", u))
            rows = at(i * m, m)
            gates = dot(a_t[rows, :], work[pl.ds(T, T), :]).astype(bf16)
            ups = dot(a_t[rows, :], work[pl.ds(2 * T, T), :]).astype(bf16)
            downs = dot(dh_t[rows, :], work[pl.ds(0, T), :]).astype(bf16)
            for y in range(Y):
                lanes = slice(y * LANES, (y + 1) * LANES)
                for p in range(z.active):
                    for x in range(X // 2):
                        for c in range(CORES):
                            part = slice((x * CORES + c) * z.h + p * 16, (x * CORES + c) * z.h + (p + 1) * 16)
                            stage[slot, i * (X // 2) + x, c, z.piece(y, p, 0), :] = gates[part, lanes]
                            stage[slot, i * (X // 2) + x, c, z.piece(y, p, 1), :] = ups[part, lanes]
                    for x in range(X):
                        stage[slot, x, i, z.piece(y, p, 2), :] = downs[y * z.h + p * 16 : y * z.h + (p + 1) * 16, x * LANES : (x + 1) * LANES]
            return 0

        lax.fori_loop(0, 2, rows_of, 0)
        step("p", j + base)
        return 0

    lax.fori_loop(0, NB, block, 0)
    if first:
        left = pltpu.make_async_copy(reduce.stage.at[(NB - 1) % 2], left_out, left_sem)
        left.start()
    spilled(NB - 1)

    def load_3(i):
        slot, rows = lax.rem(i, 2), at(i * T3, T3)
        out = [load_h(i)]
        for k in range(2):
            for j in range(NB):
                out.append(pltpu.make_async_copy(spill.at[k, j, rows, :], work.at[at(((slot * 2 + k) * NB + j) * T3, T3), :], s3_sem.at[slot]))
        return out

    def store_3(i):
        return pltpu.make_async_copy(dx_buf.at[lax.rem(i, 2)], dx_out.at[at(i * T3, T3), :], o_sem.at[lax.rem(i, 2)])

    start(load_3(0))
    u = NB + base - 1
    todo = {
        0: [("ay", u - 3), ("z", u - 2)],
        1: [("x1", u), ("az", u - 2)],
        2: [("y", u - 1)],
        3: [("x2", u), ("ay", u - 2)],
        4: [("z", u - 1)],
        5: [("az", u - 1), ("f", 0)],
        6: [("y", u), ("ay", u - 1)],
        7: [("f", v) for v in range(1, u - 1)],
    }

    def rows_back(i, _):
        slot, rows = lax.rem(i, 2), at(i * T3, T3)
        pl.when(i + 1 < n3)(lambda: start(load_3(i + 1)))
        for when, steps in todo.items():

            def now(steps=steps):
                for each in steps:
                    step(*each)

            pl.when(i == when)(now)
        load_h(i).wait()
        wait(work.at[at(slot * 2 * NB * T3, 2 * NB * T3), :], s3_sem.at[slot])
        pl.when(i > 1)(lambda: store_3(i - 2).wait())
        back = []
        for k, w in ((0, wg), (1, wu)):
            total = None
            for j in range(NB):
                part = dot(work[at(((slot * 2 + k) * NB + j) * T3, T3), :], w[j], ((1,), (1,)))
                total = part if total is None else total + part
            back.append(total.astype(bf16))
        by_a = (back[0] + back[1]).astype(f32)
        wide = h_buf[slot].astype(f32)
        square = jnp.mean(wide * wide, -1, keepdims=True) + 1e-6
        scale = lax.rsqrt(square)
        by_scale = jnp.sum(by_a * wide, -1, keepdims=True)
        by_square = by_scale * (-0.5 * scale / square) * (2.0 / D)
        dx_buf[slot] = dh[rows, :] + (by_a * scale + by_square * wide).astype(bf16)
        store_3(i).start()
        return 0

    lax.fori_loop(0, n3, rows_back, 0)
    assert n3 > max(todo)
    step("f", u - 1)
    for name in ("z", "az", "ay", "f"):
        step(name, u)
    reduce.end()
    if first:
        fetch.end()
        left.wait()
    for i in range(max(0, n3 - 2), n3):
        store_3(i).wait()


def call(body, out, n_in, scratch, number):
    return pl.pallas_call(
        body,
        out_shape=out,
        in_specs=[pl.BlockSpec(memory_space=HBM)] * n_in,
        out_specs=[pl.BlockSpec(memory_space=HBM)] * len(out),
        scratch_shapes=scratch,
        compiler_params=pltpu.CompilerParams(collective_id=number, has_side_effects=True, vmem_limit_bytes=66_900_000),
    )


def forward(z, x, shards):
    S = jax.ShapeDtypeStruct
    wide, tall, tokens = (z.NB, z.D, z.FB), (z.NB, z.FB, z.D), (z.T, z.D)
    scratch = [VMEM(tokens, bf16), VMEM(tokens, f32), VMEM(tokens, bf16), VMEM((z.TC, z.FB), bf16), VMEM(wide, bf16), VMEM(wide, bf16), VMEM(tall, bf16)]
    scratch += [DMA, DMA((3,)), DMA] + Fetch.scratch(z)
    out = [S(tokens, bf16), S(wide, bf16), S(wide, bf16), S(tall, bf16)]
    h, *w = call(functools.partial(forward_kernel, z), out, 4, scratch, 0)(x, *shards)
    return h, w


def backward(z, h, dh, w, left):
    S = jax.ShapeDtypeStruct
    first = left is None
    wide, tall, tokens = (z.NB, z.D, z.FB), (z.NB, z.FB, z.D), (z.T, z.D)
    units = z.NB - 1 if first else z.NB + 1
    scratch = [VMEM((2, z.T3, z.D), bf16), VMEM((2, z.T3, z.D), bf16)]
    scratch += [VMEM(tokens, bf16), VMEM(tokens[::-1], bf16), VMEM(tokens, bf16), VMEM(tokens[::-1], bf16)]
    scratch += [VMEM(wide, bf16), VMEM(wide, bf16), VMEM(tall, bf16), VMEM((max(3 * z.T, 4 * z.NB * z.T3), z.FB), bf16)]
    scratch += [DMA((2,)), DMA, DMA((3, z.NB)), DMA((2,)), DMA((2,)), DMA((2,)), DMA]
    if first:
        scratch += Fetch.scratch(z)
    scratch += Reduce.scratch(z, units)
    out = [S(tokens, bf16), S((units, z.U, LANES), bf16), S((units, z.U, LANES), bf16), S((2, z.NB, z.T, z.FB), bf16)]
    if first:
        out.append(S((X, CORES, z.U, LANES), bf16))
    args = (h, dh, *w) if first else (h, dh, *w, left)
    dx, fin, pair, _, *left = call(functools.partial(backward_kernel, z, first), out, len(args), scratch, 1 if first else 2)(*args)
    return dx, fin, pair, left


def gradients(z, fin, pair):
    c = lax.rem(lax.axis_index("s"), CORES)
    fin, pair = (v.reshape(2, z.NB, Y, z.active, 3, 16, LANES)[::-1] for v in (fin, pair))

    def wide(matrix):
        return fin[:, :, :, :, matrix].transpose(0, 3, 4, 2, 1, 5).reshape(2, z.h, z.F)

    mine, other = fin[:, :, :, :, 2], pair[:, :, :, :, 2]
    low, high = jnp.where(c == 0, mine, other), jnp.where(c == 0, other, mine)
    down = jnp.stack([low, high], 1)
    down = down.transpose(0, 2, 6, 1, 3, 4, 5).reshape(2, z.NB * LANES, z.D)
    return wide(0), wide(1), lax.dynamic_slice(down, (0, c * (z.NB * 64), 0), (2, z.NB * 64, z.D))


def solution(mesh):
    def step(x, dy, *weights):
        z = Sizes(mesh, x.shape[1], x.shape[2], weights[0].shape[2])
        h, w = forward(z, x[0], weights)
        dh, fin_1, pair_1, left = backward(z, h, dy[0], weights, None)
        dx, fin_0, pair_0, _ = backward(z, x[0], dh, w, left[0])
        return (dx[None], *gradients(z, jnp.concatenate([fin_1, fin_0]), jnp.concatenate([pair_1, pair_0])))

    states, cut = P(("rep", "r", "s"), None, None), P(None, "s", None)
    return jax.shard_map(
        step,
        mesh=mesh,
        in_specs=(states, states) + (cut,) * 3,
        out_specs=(states,) + (P("rep", "s", None),) * 3,
        check_vma=False,
    )
```

time: 764 us -> 387 us (0.51); the launches traced: 754 us -> 387 us
  waiting for transfers between devices: 365 us -> 0 us
  Pallas kernels: 0 us -> 351 us
  matrix products: 331 us -> 0 us
  between operations: 14.2 us -> 0.72 us
    pallas_call x0 -> x3, Pallas kernels: none -> 351 us  [the longest x2 279 us: backward(): call(functools.partial(backward_kernel, z, first), out, len(args), scratc...]
    dot_general x17 -> x0, matrix products: 331 us -> none  [the longest x6 121 us: layer(): up = jnp.dot(a, w['w_up'], preferred_element_type=jnp.float32)]
    reduce_scatter x6 -> x0, waiting for transfers between devices: 133 us -> none  [summed(): lax.psum_scatter(term, 's', scatter_dimension=0, tiled=True)]
    psum x1 -> x0, waiting for transfers between devices: 119 us -> none  [summed(): lax.psum(lax.psum_scatter(term, 's', scatter_dimension=0, tiled=True), 'r')]
    all_gather x6 -> x0, waiting for transfers between devices: 112 us -> none  [fetched(): lax.all_gather(w[number], 's', axis=0, tiled=True)]
    reshape x0 -> x3, local copies, waits for them, and re-layouts: none -> 9.3 us  [the longest x1 5.11 us: gradients(): down = down.transpose(0, 2, 6, 1, 3, 4, 5).reshape(2, z.NB * LANES, z.D)]
    unnamed x25 -> x8, local copies, waits for them, and re-layouts: 20.7 us -> 12.4 us
  transfers between devices with their start and end apart: 13 -> 0, of which waited for: 11 -> 0; matrix products, arithmetic and copies ran while one was open for 37% -> 0% of each run, Pallas kernels for 0% -> 0%
where the time goes in v2:
time: 387 us
  Pallas kernels  351 us (91%)
  local copies, waits for them, and re-layouts  26.2 us (7%)
  other arithmetic  8.36 us (2%)
    pallas_call x2, Pallas kernels, backward(): call(functools.partial(backward_kernel, z, first), out, len(args), scratc...  279 us
    pallas_call x1, Pallas kernels, forward(): call(functools.partial(forward_kernel, z), out, 4, scratch, 0)(x, *shards)  71.9 us
    unnamed x8, local copies, waits for them, and re-layouts  12.4 us

profile of v2, /device:TPU:1, one launch (start us, length us, event | category | flops | bytes accessed | tf_op | source)
XLA Modules:
  0.0 386.5 jit_solution(6174301917558137258)
XLA Ops:
  0.6 71.9 %shard_map.84 = (bf16[2048,896]{1,0:T(8,128)(2,1)}, bf16[5,896,512]{2,1,0:T(8,128)(2,1)}, bf16[5,896,512]{2,1,0:T(8,128)(2,1)}, bf16[5,512,896]{2,1,0:T(8,128)(2,1)}) custom-call(bf16[2048,896]{1,0:T(8,128)(2,1)} %bitcast.23, bf16[2,112,2560]{2,1,0:T(8,128)(2,1)} %refs_2_.1, bf16[2,112,2560]{2,1,0:T(8,128)(2,1)} %refs_3_.1, bf16[2,320,896]{2,1,0:T(8,128)(2,1)} %refs_4_.1), custom_call_target="tpu_custom_call" | custom-call | tf_op jit(solution)/shard_map/pallas_call | solution.py:725
  72.6 142.4 %shard_map.85 = (bf16[2048,896]{1,0:T(8,128)(2,1)}, bf16[4,1344,128]{2,1,0:T(8,128)(2,1)}, bf16[4,1344,128]{2,1,0:T(8,128)(2,1)}, bf16[2,5,2048,512]{3,2,1,0:T(8,128)(2,1)}, bf16[4,2,1344,128]{3,2,1,0:T(8,128)(2,1)}) custom-call(bf16[2048,896]{1,0:T(8,128)(2,1)} %get-tuple-element.15.refs_0_, bf16[2048,896]{1,0:T(8,128)(2,1)} %bitcast.28, ...), custom_call_target="tpu_custom_call" | custom-call | tf_op jit(solution)/shard_map/pallas_call | solution.py:745
  214.9 136.9 %shard_map.86 = (bf16[2048,896]{1,0:T(8,128)(2,1)}, bf16[6,1344,128]{2,1,0:T(8,128)(2,1)}, bf16[6,1344,128]{2,1,0:T(8,128)(2,1)}, bf16[2,5,2048,512]{3,2,1,0:T(8,128)(2,1)}) custom-call(bf16[2048,896]{1,0:T(8,128)(2,1)} %bitcast.24, bf16[2048,896]{1,0:T(8,128)(2,1)} %get-tuple-element.16.refs_1_, bf16[5,896,512]{2,1,0:T(8,128)(2,1)} %get-tuple-element.17.refs_2_, ...), custom_call_target="tpu_custom_call" | custom-call | tf_op jit(solution)/shard_map/pallas_call | solution.py:745
  351.8 3.3 pad_maximum_fusion
  355.1 2.0 fusion
  357.1 1.4 copy.24
  358.5 0.2 slice.35
  358.7 2.6 copy.25
  361.4 2.4 select_bitcast_fusion.1
  363.8 2.7 maximum_bitcast_fusion
  366.5 5.1 %reshape.65 = bf16[2,640,896]{1,2,0:T(8,128)(2,1)S(1)} reshape(bf16[2,5,128,2,4,7,16]{2,1,6,5,4,3,0:T(8,128)(2,1)} %maximum_bitcast_fusion) | data formatting | bytes 4587520 | tf_op jit(solution)/shard_map/reshape | solution.py:759
  371.6 1.7 constant_dynamic-slice_fusion
  373.3 0.0 copy-start
  373.3 2.5 copy.21
  375.8 0.0 copy-done
  375.8 0.8 copy.22
  376.7 0.3 reverse_bitcast_fusion.1
  377.0 2.1 reshape.62
  379.1 0.8 copy.23
  379.9 0.3 reverse_bitcast_fusion
  380.2 2.1 reshape.63
  382.3 4.2 %copy.27 = bf16[1,2048,896]{2,1,0:T(8,128)(2,1)} copy(bf16[1,2048,896]{2,1,0:T(8,128)(2,1)} %bitcast.27) | data formatting | bytes 7340032
Async XLA Ops:
  373.3 2.5 copy-start

commit v3 on v2

v3 whole, which is shorter than its diff:
```python
import functools

import jax
import jax.numpy as jnp
from jax import lax
from jax.experimental import pallas as pl
from jax.experimental.pallas import tpu as pltpu
from jax.sharding import PartitionSpec as P

f32, bf16 = jnp.float32, jnp.bfloat16
MESH = pl.DeviceIdType.MESH
LANES = 128
X, CORES, Y = 4, 2, 4
HBM, VMEM, DMA = pl.ANY, pltpu.VMEM, pltpu.SemaphoreType.DMA


def dot(a, b, dims=((1,), (0,))):
    return lax.dot_general(a, b, (dims, ((), ())), preferred_element_type=f32)


def at(start, size, multiple=16):
    return pl.ds(pl.multiple_of(start, multiple) if not isinstance(start, int) else start, size)


class Sizes:
    chunk, piece, rows = 1024, 512, 256

    def __init__(self, mesh, tokens, d, ff):
        self.R = mesh.shape["r"]
        self.Z = self.R // Y
        self.T, self.D, self.F = tokens, d, ff
        self.NB = ff // (X * LANES)
        self.FB = X * LANES
        self.h = d // (X * CORES)
        self.TC = min(self.chunk, tokens)
        self.T3 = min(self.rows, tokens)
        self.TS = min(self.piece, tokens)
        self.unit = (Y, 3, self.h, LANES)
        self.active = self.h // 16
        assert self.h % 16 == 0 and self.active <= self.Z and mesh.shape["s"] == X * CORES


class Here:
    def __init__(self, z):
        s, self.r = lax.axis_index("s"), lax.axis_index("r")
        self.x, self.c = lax.div(s, CORES), lax.rem(s, CORES)
        self.y, self.z, self.Z = lax.div(self.r, z.Z), lax.rem(self.r, z.Z), z.Z
        self.R = z.R

    def partner(self):
        return {"s": self.x * CORES + 1 - self.c}

    def along_x(self, k):
        return {"s": lax.rem(self.x + k, X) * CORES + self.c}

    def along_y(self, k):
        return {"r": lax.rem(self.y + k, Y) * self.Z + self.z}

    def along_z(self, k):
        return {"r": self.y * self.Z + lax.rem(self.z + k, self.Z)}


def remote(src, dst, sent, got, where):
    return pltpu.make_async_remote_copy(src_ref=src, dst_ref=dst, send_sem=sent, recv_sem=got, device_id=where, device_id_type=MESH)


def start(copies):
    for copy in copies:
        copy.start()


def wait(ref, sem):
    pltpu.make_async_copy(ref, ref, sem).wait()


def meet(peers):
    barrier = pltpu.get_barrier_semaphore()
    for peer in peers:
        pl.semaphore_signal(barrier, inc=1, device_id=peer, device_id_type=MESH)
    return lambda: pl.semaphore_wait(barrier, len(peers))


class Fetch:
    PHASES = ("a1", "a2", "b1", "b2", "c", "d1", "d2", "e")

    def __init__(self, z, here, shards, w, sems):
        self.z, self.here, self.shards, self.w = z, here, shards, w
        self.local, self.local_d, self.pair, self.pair_sent = sems[:4]
        self.got = dict(zip(self.PHASES, sems[4::2], strict=True))
        self.sent = dict(zip(self.PHASES, sems[5::2], strict=True))

    @classmethod
    def scratch(cls, z):
        return [DMA((z.NB,)), DMA, DMA, DMA] + [DMA((z.NB,)) for _ in range(2 * len(cls.PHASES))]

    def peers(self):
        here = self.here
        return [here.partner()] + [here.along_x(k) for k in (1, 3)] + [here.along_y(k) for k in (1, 3)]

    def own(self, j):
        z, here = self.z, self.here
        for shard, w in zip(self.shards[:2], self.w[:2], strict=True):
            for l in range(X):
                slot = w.at[j, self.rows(here.x), pl.ds(l * LANES, LANES)]
                pltpu.make_async_copy(shard.at[:, at((l * z.NB + j) * LANES, LANES, LANES)], slot, self.local.at[j]).start()

    def own_down(self, k):
        z, here = self.z, self.here
        place = here.c * z.NB + k
        return self.shards[2].at[pl.ds(64 * k, 64), :], self.w[2].at[lax.div(place, 2), at(here.x * LANES + lax.rem(place, 2) * 64, 64), :]

    def rows(self, x):
        return at(x * (CORES * self.z.h) + self.here.c * self.z.h, self.z.h)

    def lanes(self, y):
        return at(y * LANES, LANES, LANES)

    def down(self, x, begin=0, size=64):
        return at(x * LANES + self.here.c * 64 + begin, size)

    def send(self, phase, j, w, rows, lanes, where):
        slot = self.w[w].at[j, rows, lanes]
        remote(slot, slot, self.sent[phase].at[j], self.got[phase].at[j], where).start()

    def begin_local(self):
        for j in range(self.z.NB):
            self.own(j)
        for k in range(self.z.NB):
            pltpu.make_async_copy(*self.own_down(k), self.local_d).start()

    def start_a1(self, j, first=False):
        here = self.here
        wait(self.w[0].at[j, pl.ds(0, 2 * self.z.h), :], self.local.at[j])
        for k in (1, 3):
            for w in range(2):
                self.send("a1", j, w, self.rows(here.x), slice(None) if first else self.lanes(here.y), here.along_x(k))

    def start_d1(self, j):
        for k in (1, 3):
            self.send("d1", j, 2, self.down(self.here.x), slice(None), self.here.along_x(k))

    def start_a2(self, j, first=False):
        here = self.here
        wait(self.pieces(j, 16 if first else 4), self.got["a1"].at[j])
        lanes = slice(None) if first else self.lanes(here.y)
        self.send("a2", j, 0, self.rows(lax.rem(here.x + 3, X)), lanes, here.along_x(1))
        self.send("a2", j, 1, self.rows(lax.rem(here.x + 1, X)), lanes, here.along_x(3))

    def start_d2(self, j):
        here = self.here
        wait(self.halves(j, 2), self.got["d1"].at[j])
        self.send("d2", j, 2, self.down(lax.rem(here.x + 3, X), 0, 32), slice(None), here.along_x(1))
        self.send("d2", j, 2, self.down(lax.rem(here.x + 1, X), 32, 32), slice(None), here.along_x(3))

    def start_b1(self, j):
        here = self.here
        wait(self.pieces(j, 2), self.got["a2"].at[j])
        for k in (1, 3):
            for m in range(1, X):
                for w in range(2):
                    self.send("b1", j, w, self.rows(lax.rem(here.x + m, X)), self.lanes(here.y), here.along_y(k))

    def start_b2(self, j):
        here = self.here
        wait(self.pieces(j, 12), self.got["b1"].at[j])
        for m in range(1, X):
            rows = self.rows(lax.rem(here.x + m, X))
            self.send("b2", j, 0, rows, self.lanes(lax.rem(here.y + 3, Y)), here.along_y(1))
            self.send("b2", j, 1, rows, self.lanes(lax.rem(here.y + 1, Y)), here.along_y(3))

    def start_c(self, j, first=False):
        if first:
            wait(self.pieces(j, 8), self.got["a2"].at[j])
        else:
            wait(self.pieces(j, 6), self.got["b2"].at[j])
        for w in range(2):
            for x in range(X):
                self.send("c", j, w, self.rows(x), slice(None), self.here.partner())

    def start_e(self, j):
        wait(self.halves(j, 1), self.got["d2"].at[j])
        for m in range(1, X):
            self.send("e", j, 2, self.down(lax.rem(self.here.x + m, X)), slice(None), self.here.partner())

    def pieces(self, j, n):
        rows, lanes = {2: (2, 1), 4: (4, 1), 6: (6, 1), 8: (8, 1), 12: (6, 2), 16: (8, 2)}[n]
        return self.w[0].at[j, pl.ds(0, rows * self.z.h), pl.ds(0, lanes * LANES)]

    def halves(self, j, n):
        return self.w[2].at[j, pl.ds(0, 64 * n), :]

    def begin(self):
        nb = self.z.NB
        for k in range(nb):
            src, slot = self.own_down(k)
            remote(src, slot, self.pair_sent, self.pair, self.here.partner()).start()
        if nb > 1:
            self.start_a1(1)
        self.start_a1(0, True)
        wait(self.halves(0, nb), self.local_d)
        wait(self.halves(0, nb), self.pair)
        self.start_d1(0)

    def head(self):
        nb = self.z.NB
        if nb > 1:
            self.start_a2(1)
        self.start_a2(0, True)
        if nb > 1:
            self.start_b1(1)
        self.start_d2(0)
        if nb > 1:
            self.start_d1(1)
        if nb > 2:
            self.start_a1(2)
        self.start_c(0, True)
        self.start_e(0)

    def serve_a(self, j):
        nb = self.z.NB

        @pl.when(j + 1 < nb)
        def _():
            self.start_b2(j + 1)
            self.start_d2(j + 1)

        pl.when(j + 2 < nb)(lambda: self.start_a2(j + 2))
        wait(self.w[0].at[j], self.got["c"].at[j])
        wait(self.halves(j, 3), self.got["e"].at[j])

    def serve_b(self, j):
        nb = self.z.NB

        @pl.when(j + 1 < nb)
        def _():
            self.start_c(j + 1)
            self.start_e(j + 1)

        @pl.when(j + 2 < nb)
        def _():
            self.start_b1(j + 2)
            self.start_d1(j + 2)

        pl.when(j + 3 < nb)(lambda: self.start_a1(j + 3))

    def end(self):
        wait(self.halves(0, self.z.NB), self.pair_sent)

        def drain(j, first):
            wait(self.pieces(j, 16 if first else 4), self.sent["a1"].at[j])
            wait(self.pieces(j, 8 if first else 2), self.sent["a2"].at[j])
            if not first:
                wait(self.pieces(j, 12), self.sent["b1"].at[j])
                wait(self.pieces(j, 6), self.sent["b2"].at[j])
            wait(self.halves(j, 2), self.sent["d1"].at[j])
            wait(self.halves(j, 1), self.sent["d2"].at[j])
            wait(self.w[0].at[j], self.sent["c"].at[j])
            wait(self.halves(j, 3), self.sent["e"].at[j])
            return 0

        drain(0, True)
        lax.fori_loop(1, self.z.NB, lambda j, _: drain(j, False), 0)


def normed(wide):
    scale = lax.rsqrt(jnp.mean(wide * wide, -1, keepdims=True) + 1e-6)
    return (wide * scale).astype(bf16), scale


def forward_kernel(z, x_in, sg, su, sd, h_out, wg_out, wu_out, wd_out, by_up_out, by_gate_out, act_out, a, acc, xs, act, by_up, by_gate, wg, wu, wd, x_sem, out_sem, h_sem, keep_sem, *sems):
    here = Here(z)
    fetch = Fetch(z, here, (sg.at[0], su.at[0], sd.at[0]), (wg, wu, wd), sems)
    met = meet(fetch.peers())
    fetch.begin_local()
    load = pltpu.make_async_copy(x_in, xs, x_sem)
    load.start()
    met()
    fetch.begin()
    load.wait()

    def prepare(i, _):
        rows = at(i * z.T3, z.T3)
        a[rows, :] = normed(xs[rows, :].astype(f32))[0]
        acc[rows, :] = jnp.zeros((z.T3, z.D), f32)
        return 0

    lax.fori_loop(0, z.T // z.T3, prepare, 0)
    fetch.head()
    held = ((wg, wg_out), (wu, wu_out), (wd, wd_out))
    n = z.T // z.TC

    def keep(j, i):
        slot = lax.rem(i, 2)
        return [
            pltpu.make_async_copy(v.at[slot], o.at[j, at(i * z.TC, z.TC), :], keep_sem.at[k, slot])
            for k, (v, o) in enumerate(((act, act_out), (by_up, by_up_out), (by_gate, by_gate_out)))
        ]

    def kept(j, i):
        for copy in keep(j, i):
            copy.wait()

    def block(j, _):
        fetch.serve_a(j)
        start([pltpu.make_async_copy(v.at[j], o.at[j], out_sem.at[k]) for k, (v, o) in enumerate(held)])

        def chunk(i, _):
            pl.when(i == n // 2)(lambda: fetch.serve_b(j))
            pl.when(j * n + i > 1)(lambda: kept(j, i))
            rows, slot = at(i * z.TC, z.TC), lax.rem(i, 2)
            for half in range(2):
                cols = slice(half * z.FB // 2, (half + 1) * z.FB // 2)
                gate, up = dot(a[rows, :], wg[j, :, cols]), dot(a[rows, :], wu[j, :, cols])
                sig = 1.0 / (1.0 + jnp.exp(-gate))
                silu = gate * sig
                act[slot, :, cols] = (silu * up).astype(bf16)
                by_up[slot, :, cols] = silu
                by_gate[slot, :, cols] = up * (sig + silu * (1.0 - sig))
            acc[rows, :] += dot(act[slot], wd[j])
            start(keep(j, i))
            return 0

        lax.fori_loop(0, n, chunk, 0)
        return 0

    lax.fori_loop(0, z.NB, block, 0)

    def finish(i, _):
        rows = at(i * z.T3, z.T3)
        xs[rows, :] = xs[rows, :] + acc[rows, :].astype(bf16)
        return 0

    lax.fori_loop(0, z.T // z.T3, finish, 0)
    store = pltpu.make_async_copy(xs, h_out, h_sem)
    store.start()
    for i in range(2):
        kept(z.NB - 1, n - 2 + i)
    for k, (v, _) in enumerate(held):
        wait(v, out_sem.at[k])
    fetch.end()
    store.wait()


class Reduce:
    PHASES = ("p", "x1", "x2", "y", "z", "az", "ay", "f")

    def __init__(self, z, here, units, layer_first, outs, refs):
        self.z, self.here, self.units, self.layer_first, self.outs = z, here, units, layer_first, outs
        (self.stage, self.got_p, self.got_x1, self.got_x2, self.got_y, self.got_z) = refs[:6]
        (self.send_x1, self.send_x2, self.send_y, self.send_z, self.kept_y, self.kept_z, self.fin, self.down, self.turned) = refs[6:15]
        self.got = dict(zip(self.PHASES, refs[15:31:2], strict=True))
        self.sent = dict(zip(self.PHASES, refs[16:31:2], strict=True))
        self.out_sem, self.turned_sem = refs[31:33]

    @classmethod
    def scratch(cls, z, units):
        unit, share = z.unit, z.unit[1:]
        data = [(2, X, CORES, *unit), (3, X, *unit), (2, 2, Y // 2, *share), (2, 2, *unit), (2, *unit), (units, z.Z, 3, 16, LANES)]
        data += [unit, (2, *unit), unit, share]
        return (
            [VMEM(shape, bf16) for shape in data]
            + [VMEM(share, f32), VMEM(share, f32), VMEM((units, *unit), bf16), VMEM((units, CORES, Y, z.h, LANES), bf16), VMEM((2, LANES, z.D), bf16)]
            + [DMA((units,)) for _ in range(2 * len(cls.PHASES))]
            + [DMA((2, units)), DMA((2, 2))]
        )

    def peers(self):
        here = self.here
        return (
            [here.partner(), here.along_x(1), here.along_x(3)] + [here.along_y(k) for k in range(1, Y)] + [here.along_z(k) for k in range(1, here.Z)]
        )

    def send(self, phase, u, src, dst, where):
        remote(src, dst, self.sent[phase].at[u], self.got[phase].at[u], where).start()

    def over(self, work, begin=0, end=Y):
        def one(i, _):
            work(lax.div(i, 3), lax.rem(i, 3))
            return 0

        lax.fori_loop(begin * 3, end * 3, one, 0)

    def start_p(self, u):
        here = self.here
        for x in range(X):
            self.send("p", u, self.stage.at[lax.rem(u, 2), x, 1 - here.c], self.got_p.at[lax.rem(u, 3), x], here.partner())

    def both(self, u, x, y, m):
        return self.stage[lax.rem(u, 2), x, self.here.c, y, m].astype(f32) + self.got_p[lax.rem(u, 3), x, y, m].astype(f32)

    def start_x1(self, u):
        here, half, slot = self.here, Y // 2, lax.rem(u, 2)
        wait(self.got_p.at[lax.rem(u, 3)], self.got["p"].at[u])
        far = lax.rem(here.x + 2, X)

        def work(y, m):
            self.send_x1[y, m] = self.both(u, far, y, m).astype(bf16)

        self.over(work)
        for side in range(2):
            self.send("x1", u, self.send_x1.at[pl.ds(side * half, half)], self.got_x1.at[slot, side], here.along_x((1, 3)[side]))

    def start_x2(self, u):
        here, half, slot = self.here, Y // 2, lax.rem(u, 2)
        wait(self.got_x1.at[slot], self.got["x1"].at[u])
        wait(self.got_x1.at[slot], self.sent["x1"].at[u])
        right, left = lax.rem(here.x + 1, X), lax.rem(here.x + 3, X)

        def first(y, m):
            self.send_x2[0, y, m] = (self.both(u, right, y, m) + self.got_x1[slot, 0, y, m].astype(f32)).astype(bf16)
            self.send_x2[1, y, m] = self.both(u, left, y, m).astype(bf16)

        def second(y, m):
            self.send_x2[0, y, m] = self.both(u, right, y, m).astype(bf16)
            self.send_x2[1, y, m] = (self.both(u, left, y, m) + self.got_x1[slot, 1, y - half, m].astype(f32)).astype(bf16)

        self.over(first, 0, half)
        self.over(second, half, Y)
        for side in range(2):
            self.send("x2", u, self.send_x2.at[side], self.got_x2.at[slot, side], here.along_x((1, 3)[side]))

    def start_y(self, u):
        here, slot = self.here, lax.rem(u, 2)
        wait(self.got_x2.at[slot], self.got["x2"].at[u])
        wait(self.got_x2.at[slot], self.sent["x2"].at[u])
        wait(self.got_p.at[lax.rem(u, 3)], self.sent["p"].at[u])

        def total(y, m):
            return self.both(u, here.x, y, m) + self.got_x2[slot, 0, y, m].astype(f32) + self.got_x2[slot, 1, y, m].astype(f32)

        def work(y, m):
            self.send_y[y, m] = total(y, m).astype(bf16)

        def own(_, m):
            self.kept_y[m] = total(here.y, m)

        self.over(work)
        self.over(own, 0, 1)
        for k in (1, 3, 2):
            self.send("y", u, self.send_y.at[lax.rem(here.y + k, Y)], self.got_y.at[slot, here.y], here.along_y(k))

    def start_z(self, u):
        z, here, slot = self.z, self.here, lax.rem(u, 2)
        wait(self.got_y.at[slot, pl.ds(0, Y - 1)], self.got["y"].at[u])
        wait(self.got_y.at[slot, pl.ds(0, Y - 1)], self.sent["y"].at[u])

        def work(_, m):
            total = self.kept_y[m]
            for k in range(1, Y):
                total += self.got_y[slot, lax.rem(here.y + k, Y), m].astype(f32)
            self.kept_z[m] = total
            self.send_z[m] = total.astype(bf16)

        self.over(work, 0, 1)

        def send(k, _):
            to = lax.rem(here.z + k, z.Z)
            pl.when(to < z.active)(lambda: self.send("z", u, self.send_z.at[:, at(to * 16, 16), :], self.got_z.at[u, here.z], here.along_z(k)))
            return 0

        lax.fori_loop(1, z.Z, send, 0)

    def if_active(self, yes, no):
        pl.when(self.here.z < self.z.active)(yes)
        pl.when(self.here.z >= self.z.active)(no)

    def wait_pieces(self, u, n, sem):
        if n:
            wait(self.got_z.at[u, pl.ds(0, n)], sem.at[u])

    def start_az(self, u):
        z, here = self.z, self.here

        def yes():
            self.wait_pieces(u, z.active - 1, self.sent["z"])
            self.wait_pieces(u, z.Z - 1, self.got["z"])
            rows = at(here.z * 16, 16)
            total = self.kept_z[:, rows, :]
            for k in range(1, z.Z):
                total += self.got_z[u, lax.rem(here.z + k, z.Z)].astype(f32)
            self.fin[u, here.y, :, rows, :] = total.astype(bf16)
            mine = self.fin.at[u, here.y, :, rows, :]

            def send(k, _):
                self.send("az", u, mine, mine, here.along_z(k))
                return 0

            lax.fori_loop(1, z.Z, send, 0)

        self.if_active(yes, lambda: self.wait_pieces(u, z.active, self.sent["z"]))

    def start_ay(self, u):
        z, here = self.z, self.here
        self.if_active(lambda: self.wait_pieces(u, z.active - 1, self.got["az"]), lambda: self.wait_pieces(u, z.active, self.got["az"]))
        share = self.fin.at[u, here.y]
        for k in (1, 3, 2):
            self.send("ay", u, share, share, here.along_y(k))

    def place(self, u):
        nb = self.z.NB
        return (1, u) if self.layer_first else (1 - lax.div(u + nb - 1, nb), lax.rem(u + nb - 1, nb))

    def start_f(self, u):
        z, c = self.z, self.here.c
        layer, j = self.place(u)
        wait(self.fin.at[u, pl.ds(0, Y - 1)], self.got["ay"].at[u])
        for m in range(2):
            for y in range(Y):
                out = self.outs[m].at[layer, :, at((y * z.NB + j) * LANES, LANES, LANES)]
                pltpu.make_async_copy(self.fin.at[u, y, m], out, self.out_sem.at[m, u]).start()
        self.down[u, c] = self.fin[u, :, 2]
        self.send("f", u, self.fin.at[u, :, 2], self.down.at[u, c], self.here.partner())

    def finish(self, u):
        z, c = self.z, self.here.c
        layer, j = self.place(u)
        wait(self.down.at[u, 0], self.got["f"].at[u])
        slot = lax.rem(u, 2)
        pl.when(u > 1)(lambda: self.turned_out(u - 2, "wait"))
        self.turned[slot] = self.down[u].reshape(z.D, LANES).T
        self.turned_out(u, "start")

    def turned_out(self, u, what):
        z, c = self.z, self.here.c
        layer, j = self.place(u)
        for half in range(2):
            row = 2 * j + half

            @pl.when(lax.div(row, z.NB) == c)
            def _(half=half, row=row):
                out = self.outs[2].at[layer, at(lax.rem(row, z.NB) * 64, 64), :]
                getattr(pltpu.make_async_copy(self.turned.at[lax.rem(u, 2), pl.ds(half * 64, 64), :], out, self.turned_sem.at[lax.rem(u, 2), half]), what)()

    def end(self):
        z = self.z

        def one(u, _):
            self.if_active(lambda: self.wait_pieces(u, z.Z - 1, self.sent["az"]), lambda: None)
            wait(self.fin.at[u, pl.ds(0, Y - 1)], self.sent["ay"].at[u])
            wait(self.down.at[u, 0], self.sent["f"].at[u])
            for m in range(2):
                wait(self.down.at[u, 0], self.out_sem.at[m, u])
            return 0

        lax.fori_loop(0, self.units, one, 0)
        for u in range(max(0, self.units - 2), self.units):
            self.turned_out(u, "wait")


def backward_kernel(z, first, *refs):
    T, TC, T3, NB, FB, D = z.T, z.TC, z.T3, z.NB, z.FB, z.D
    here = Here(z)
    refs = list(refs)

    def take(n):
        out, refs[:] = refs[:n], refs[n:]
        return out

    h_in, dh_in, w0, w1, w2 = take(5)
    if not first:
        left_in, by_up_in, by_gate_in, act_in = take(4)
        take(3)
    dx_out, *outs = take(4)
    spill = take(1)[0]
    left_out = take(1)[0] if first else None
    dx_buf, h_buf, a_t, dh, dh_t, wg, wu, wd, work = take(9)
    ld_sem, dh_sem, w_sem, sp_sem, s3_sem, o_sem, left_sem = take(7)
    if first:
        a = take(1)[0]
    else:
        saved, saved_sem, act_sem = take(3)
    fetch = Fetch(z, here, (w0.at[1], w1.at[1], w2.at[1]), (wg, wu, wd), take(len(Fetch.scratch(z)))) if first else None
    base = 0 if first else 1
    units = NB - 1 if first else NB + 1
    reduce = Reduce(z, here, units, first, outs, refs)
    met = meet(reduce.peers())
    whole = pltpu.make_async_copy(dh_in, dh, dh_sem)
    whole.start()

    def load_h(i):
        return pltpu.make_async_copy(h_in.at[at(i * T3, T3), :], h_buf.at[lax.rem(i, 2)], ld_sem.at[lax.rem(i, 2)])

    load_h(0).start()

    def loads(j):
        return [pltpu.make_async_copy(src.at[j], dst.at[j], w_sem.at[k, j]) for k, (src, dst) in enumerate(((w0, wg), (w1, wu), (w2, wd)))]

    TS, slots = z.TS, 3

    def load_saved(q):
        j, rows, slot = lax.div(q, T // TS), at(lax.rem(q, T // TS) * TS, TS), lax.rem(q, slots)
        return [pltpu.make_async_copy(v.at[j, rows, :], saved.at[slot, k], saved_sem.at[k, slot]) for k, v in enumerate((by_up_in, by_gate_in))]

    def load_act(j):
        return pltpu.make_async_copy(act_in.at[j], work.at[pl.ds(0, T), :], act_sem)

    if first:
        fetch.begin_local()
        met()
        fetch.begin()
    else:
        left = pltpu.make_async_copy(left_in, reduce.stage.at[0], left_sem)
        left.start()
        for j in range(NB):
            start(loads(j)[2:])
        for q in range(2):
            start(load_saved(q))
        for j in range(NB):
            start(loads(j)[:2])
    whole.wait()
    n3 = T // T3

    def prepare(i, _):
        rows = at(i * T3, T3, 128)
        pl.when(i + 1 < n3)(lambda: load_h(i + 1).start())
        load_h(i).wait()
        value = normed(h_buf[lax.rem(i, 2)].astype(f32))[0]
        if first:
            a[rows, :] = value
        a_t[:, rows] = value.T
        dh_t[:, rows] = dh[rows, :].T
        return 0

    if not first:
        met()
        left.wait()
        reduce.start_p(0)
    lax.fori_loop(0, n3, prepare, 0)
    if first:
        fetch.head()

    def product(k, rows, cols):
        return work.at[at(k * T + rows.start, rows.size), cols]

    def spills(j):
        return [pltpu.make_async_copy(work.at[pl.ds((1 + k) * T, T), :], spill.at[k, j], sp_sem.at[k]) for k in range(2)]

    def spilled(j):
        for copy in spills(j):
            copy.wait()

    def step(name, u):
        do = getattr(reduce, "start_" + name)
        if isinstance(u, int):
            if 0 <= u < units:
                do(u)
        else:
            pl.when(jnp.logical_and(u >= 0, u < units))(lambda: do(u))

    def halfway(i, n, before, after):
        if n == 1:
            before()
            after()
        else:
            pl.when(i == 0)(before)
            pl.when(i == n // 2)(after)

    def block(j, _):
        u = j + base - 1
        if first:
            fetch.serve_a(j)
        else:
            load_act(j).start()
            loads(j)[2].wait()
        pl.when(j > 0)(lambda: spilled(j - 1))

        def before():
            step("ay", u - 3)
            step("z", u - 2)

        def piece(i, _):
            halfway(i, T // TS, before, lambda: step("x1", u))
            q, rows = j * (T // TS) + i, at(i * TS, TS)
            pl.when(q + 2 < NB * (T // TS))(lambda: start(load_saved(q + 2)))
            for copy in load_saved(q):
                copy.wait()
            by_act = dot(dh[rows, :], wd[j], ((1,), (1,))).astype(bf16).astype(f32)
            slot = lax.rem(q, slots)
            product(1, rows, slice(None))[...] = (by_act * saved[slot, 1]).astype(bf16)
            product(2, rows, slice(None))[...] = (by_act * saved[slot, 0]).astype(bf16)
            return 0

        def chunk(i, _):
            halfway(i, T // TC, before, lambda: step("x1", u))
            rows = at(i * TC, TC)
            for half in range(2):
                cols = slice(half * FB // 2, (half + 1) * FB // 2)
                gate, up = dot(a[rows, :], wg[j, :, cols]), dot(a[rows, :], wu[j, :, cols])
                by_act = dot(dh[rows, :], wd[j, cols, :], ((1,), (1,))).astype(bf16).astype(f32)
                sig = 1.0 / (1.0 + jnp.exp(-gate))
                silu = gate * sig
                product(0, rows, cols)[...] = (silu * up).astype(bf16)
                product(1, rows, cols)[...] = (by_act * up * (sig + silu * (1.0 - sig))).astype(bf16)
                product(2, rows, cols)[...] = (by_act * silu).astype(bf16)
            return 0

        if first:
            lax.fori_loop(0, T // TC, chunk, 0)
        else:
            lax.fori_loop(0, T // TS, piece, 0)
            load_act(j).wait()
        start(spills(j))
        stage, slot, m = reduce.stage, lax.rem(j + base, 2), D // 2

        def rows_of(i, _):
            def before():
                if first:
                    fetch.serve_b(j)
                step("y", u - 1)
                step("az", u - 2)

            halfway(i, 2, before, lambda: step("x2", u))
            rows = at(i * m, m)
            gates = dot(a_t[rows, :], work[pl.ds(T, T), :]).astype(bf16)
            ups = dot(a_t[rows, :], work[pl.ds(2 * T, T), :]).astype(bf16)
            downs = dot(dh_t[rows, :], work[pl.ds(0, T), :]).astype(bf16)
            for y in range(Y):
                lanes = slice(y * LANES, (y + 1) * LANES)
                for x in range(X // 2):
                    for c in range(CORES):
                        part = slice((x * CORES + c) * z.h, (x * CORES + c + 1) * z.h)
                        stage[slot, i * (X // 2) + x, c, y, 0] = gates[part, lanes]
                        stage[slot, i * (X // 2) + x, c, y, 1] = ups[part, lanes]
                for x in range(X):
                    stage[slot, x, i, y, 2] = downs[y * z.h : (y + 1) * z.h, x * LANES : (x + 1) * LANES]
            return 0

        lax.fori_loop(0, 2, rows_of, 0)
        step("p", j + base)
        return 0

    lax.fori_loop(0, NB, block, 0)
    if first:
        left = pltpu.make_async_copy(reduce.stage.at[(NB - 1) % 2], left_out, left_sem)
        left.start()
    spilled(NB - 1)

    def load_3(i):
        slot, rows = lax.rem(i, 2), at(i * T3, T3)
        out = [load_h(i)]
        for k in range(2):
            for j in range(NB):
                out.append(pltpu.make_async_copy(spill.at[k, j, rows, :], work.at[at(((slot * 2 + k) * NB + j) * T3, T3), :], s3_sem.at[slot]))
        return out

    def store_3(i):
        return pltpu.make_async_copy(dx_buf.at[lax.rem(i, 2)], dx_out.at[at(i * T3, T3), :], o_sem.at[lax.rem(i, 2)])

    start(load_3(0))
    u = NB + base - 1
    todo = {
        0: [("ay", u - 3), ("z", u - 2)],
        1: [("x1", u), ("az", u - 2)],
        2: [("y", u - 1)],
        3: [("x2", u), ("ay", u - 2)],
        4: [("z", u - 1)],
        5: [("az", u - 1)],
        6: [("y", u), ("ay", u - 1)],
    }

    def complete(i, _):
        reduce.start_f(i)
        return 0

    def turn(i, _):
        reduce.finish(i)
        return 0

    def rows_back(i, _):
        slot, rows = lax.rem(i, 2), at(i * T3, T3)
        pl.when(i + 1 < n3)(lambda: start(load_3(i + 1)))
        for when, steps in todo.items():

            def now(steps=steps):
                for each in steps:
                    step(*each)

            pl.when(i == when)(now)

        @pl.when(i == 6)
        def _():
            lax.fori_loop(0, u - 1, complete, 0)

        @pl.when(i == 7)
        def _():
            lax.fori_loop(0, u - 1, turn, 0)

        if not first:

            @pl.when(i == 0)
            def _():
                for j in range(NB):
                    for copy in loads(j)[:2]:
                        copy.wait()

        load_h(i).wait()
        wait(work.at[at(slot * 2 * NB * T3, 2 * NB * T3), :], s3_sem.at[slot])
        pl.when(i > 1)(lambda: store_3(i - 2).wait())
        back = []
        for k, w in ((0, wg), (1, wu)):
            total = None
            for j in range(NB):
                part = dot(work[at(((slot * 2 + k) * NB + j) * T3, T3), :], w[j], ((1,), (1,)))
                total = part if total is None else total + part
            back.append(total.astype(bf16))
        by_a = (back[0] + back[1]).astype(f32)
        wide = h_buf[slot].astype(f32)
        square = jnp.mean(wide * wide, -1, keepdims=True) + 1e-6
        scale = lax.rsqrt(square)
        by_scale = jnp.sum(by_a * wide, -1, keepdims=True)
        by_square = by_scale * (-0.5 * scale / square) * (2.0 / D)
        dx_buf[slot] = dh[rows, :] + (by_a * scale + by_square * wide).astype(bf16)
        store_3(i).start()
        return 0

    lax.fori_loop(0, n3, rows_back, 0)
    assert n3 == 8
    for name in ("z", "az"):
        step(name, u)
    reduce.start_f(u - 1)
    step("ay", u)
    reduce.finish(u - 1)
    if u < units:
        reduce.start_f(u)
        reduce.finish(u)
    reduce.end()
    if first:
        fetch.end()
        left.wait()
    for i in range(max(0, n3 - 2), n3):
        store_3(i).wait()


def call(body, out, n_in, scratch, number, aliases=()):
    return pl.pallas_call(
        body,
        out_shape=out,
        in_specs=[pl.BlockSpec(memory_space=HBM)] * n_in,
        out_specs=[pl.BlockSpec(memory_space=HBM)] * len(out),
        scratch_shapes=scratch,
        input_output_aliases=dict(aliases),
        compiler_params=pltpu.CompilerParams(collective_id=number, has_side_effects=True, vmem_limit_bytes=66_900_000),
    )


def forward(z, x, shards):
    S = jax.ShapeDtypeStruct
    wide, tall, tokens, hidden, piece = (z.NB, z.D, z.FB), (z.NB, z.FB, z.D), (z.T, z.D), (z.NB, z.T, z.FB), (2, z.TC, z.FB)
    scratch = [VMEM(tokens, bf16), VMEM(tokens, f32), VMEM(tokens, bf16), VMEM(piece, bf16), VMEM(piece, f32), VMEM(piece, f32)]
    scratch += [VMEM(wide, bf16), VMEM(wide, bf16), VMEM(tall, bf16), DMA, DMA((3,)), DMA, DMA((3, 2))] + Fetch.scratch(z)
    out = [S(tokens, bf16), S(wide, bf16), S(wide, bf16), S(tall, bf16), S(hidden, f32), S(hidden, f32), S(hidden, bf16)]
    h, wg, wu, wd, *kept = call(functools.partial(forward_kernel, z), out, 4, scratch, 0)(x, *shards)
    return h, (wg, wu, wd), kept


def backward(z, h, dh, w, more):
    S = jax.ShapeDtypeStruct
    first = not more
    wide, tall, tokens = (z.NB, z.D, z.FB), (z.NB, z.FB, z.D), (z.T, z.D)
    units = z.NB - 1 if first else z.NB + 1
    scratch = [VMEM((2, z.T3, z.D), bf16), VMEM((2, z.T3, z.D), bf16)]
    scratch += [VMEM(tokens[::-1], bf16), VMEM(tokens, bf16), VMEM(tokens[::-1], bf16)]
    scratch += [VMEM(wide, bf16), VMEM(wide, bf16), VMEM(tall, bf16), VMEM((max(3 * z.T, 4 * z.NB * z.T3), z.FB), bf16)]
    scratch += [DMA((2,)), DMA, DMA((3, z.NB)), DMA((2,)), DMA((2,)), DMA((2,)), DMA]
    if first:
        scratch += [VMEM(tokens, bf16)] + Fetch.scratch(z)
    else:
        scratch += [VMEM((3, 2, z.TS, z.FB), f32), DMA((2, 3)), DMA]
    scratch += Reduce.scratch(z, units)
    grads = [S((2, z.h, z.F), bf16), S((2, z.h, z.F), bf16), S((2, z.F // (X * CORES), z.D), bf16)]
    out = [S(tokens, bf16), *grads, S((2, z.NB, z.T, z.FB), bf16)]
    if first:
        out.append(S((X, CORES, *z.unit), bf16))
    args = (h, dh, *w, *more)
    aliases = {} if first else {len(args) - 3 + i: 1 + i for i in range(3)}
    dx, g, u, d, _, *left = call(functools.partial(backward_kernel, z, first), out, len(args), scratch, 1 if first else 2, aliases)(*args)
    return dx, (g, u, d), left


def solution(mesh):
    def step(x, dy, *weights):
        z = Sizes(mesh, x.shape[1], x.shape[2], weights[0].shape[2])
        h, w, kept = forward(z, x[0], weights)
        dh, grads, left = backward(z, h, dy[0], weights, ())
        dx, grads, _ = backward(z, x[0], dh, w, (*left, kept[0], kept[1], kept[2], *grads))
        return dx[None], *grads

    states, cut = P(("rep", "r", "s"), None, None), P(None, "s", None)
    return jax.shard_map(
        step,
        mesh=mesh,
        in_specs=(states, states) + (cut,) * 3,
        out_specs=(states,) + (P("rep", "s", None),) * 3,
        check_vma=False,
    )
```

time: 387 us -> 353 us (0.912)
  local copies, waits for them, and re-layouts: 26.2 us -> 7.34 us
  other arithmetic: 8.36 us -> 0 us
  Pallas kernels: 351 us -> 344 us
    reshape x3 -> x0, local copies, waits for them, and re-layouts: 9.3 us -> none  [the longest x1 5.11 us: gradients(): down = down.transpose(0, 2, 6, 1, 3, 4, 5).reshape(2, z.NB * LANES, z.D)]
    pallas_call x2, Pallas kernels: 279 us -> 274 us  [backward(): call(functools.partial(backward_kernel, z, first), out, len(args), scratc...]
    unnamed x8 -> x10, local copies, waits for them, and re-layouts: 12.4 us -> 7.34 us
where the time goes in v3:
time: 353 us; the launch traced here: 352 us
  Pallas kernels  344 us (97%)
  local copies, waits for them, and re-layouts  7.34 us (2%)
    pallas_call x2, Pallas kernels, backward(): call(functools.partial(backward_kernel, z, first), out, len(args), scratc...  274 us
    pallas_call x1, Pallas kernels, forward(): call(functools.partial(forward_kernel, z), out, 4, scratch, 0)(x, *shards)  70.4 us
    unnamed x10, local copies, waits for them, and re-layouts  7.34 us

profile of v3, /device:TPU:1, one launch (start us, length us, event | category | flops | bytes accessed | tf_op | source)
XLA Modules:
  0.0 352.4 jit_solution(14191320406177457737)
XLA Ops:
  0.6 70.4 %shard_map.84 = (bf16[2048,896]{1,0:T(8,128)(2,1)}, bf16[5,896,512]{2,1,0:T(8,128)(2,1)}, bf16[5,896,512]{2,1,0:T(8,128)(2,1)}, bf16[5,512,896]{2,1,0:T(8,128)(2...) custom-call(bf16[2048,896]{1,0:T(8,128)(2,1)} %bitcast.3, ...), custom_call_target="tpu_custom_call" | custom-call | tf_op jit(solution)/shard_map/pallas_call | solution.py:852
  71.1 140.0 %shard_map.85 = (bf16[2048,896]{1,0:T(8,128)(2,1)}, bf16[2,112,2560]{2,1,0:T(8,128)(2,1)}, bf16[2,112,2560]{2,1,0:T(8,128)(2,1)}, bf16[2,320,896]{2,1,0:T(8,128)...) custom-call(bf16[2048,896]{1,0:T(8,128)(2,1)} %get-tuple-element.20.refs_0_, ...), custom_call_target="tpu_custom_call" | custom-call | tf_op jit(solution)/shard_map/pallas_call | solution.py:876
  211.1 133.9 %shard_map.86 = (bf16[2048,896]{1,0:T(8,128)(2,1)}, bf16[2,112,2560]{2,1,0:T(8,128)(2,1)}, bf16[2,112,2560]{2,1,0:T(8,128)(2,1)}, bf16[2,320,896]{2,1,0:T(8,128)(2,1)}, bf16[2,5,2048,512]{3,2,1,0:T(8,128)(2,1)}) custom-call(bf16[2048,896]{1,0:T(8,128)(2,1)} %bitcast.4, ...), custom_call_target="tpu_custom_call", output_to_operand_aliasing={{1}: (9, {}), {2}: (10, {}), {3}: (11, {})} | custom-call | tf_op jit(solution)/shard_map/pallas_call | solution.py:876
  345.1 0.0 copy-start
  345.1 0.0 copy-start.1
  345.1 4.3 %copy.19 = bf16[1,2048,896]{2,1,0:T(8,128)(2,1)} copy(bf16[1,2048,896]{2,1,0:T(8,128)(2,1)} %bitcast.5) | data formatting | bytes 7340032
  349.4 0.0 copy-done
  349.4 0.0 copy-start.2
  349.4 1.0 copy.20
  350.4 0.0 copy-done.1
  350.4 1.0 copy.21
  351.4 0.0 copy-done.2
  351.4 1.0 copy.22
Async XLA Ops:
  345.1 4.3 %copy-start = (bf16[2,112,2560]{2,1,0:T(8,128)(2,1)S(1)}, bf16[2,112,2560]{2,1,0:T(8,128)(2,1)}, u32[]{:S(2)}) copy-start(bf16[2,112,2560]{2,1,0:T(8,128)(2,1)} %get-tuple-element.41) | copy-start | bytes 3440644
  345.1 5.3 %copy-start.1 = (bf16[2,112,2560]{2,1,0:T(8,128)(2,1)S(1)}, bf16[2,112,2560]{2,1,0:T(8,128)(2,1)}, u32[]{:S(2)}) copy-start(bf16[2,112,2560]{2,1,0:T(8,128)(2,1)} %get-tuple-element.42) | copy-start | bytes 3440644
  349.4 2.0 copy-start.2

commit v4 on v3

v4 whole, which is shorter than its diff:
```python
import functools

import jax
import jax.numpy as jnp
from jax import lax
from jax.experimental import pallas as pl
from jax.experimental.pallas import tpu as pltpu
from jax.sharding import PartitionSpec as P

f32, bf16 = jnp.float32, jnp.bfloat16
MESH = pl.DeviceIdType.MESH
LANES = 128
X, CORES, Y = 4, 2, 4
HBM, VMEM, DMA = pl.ANY, pltpu.VMEM, pltpu.SemaphoreType.DMA


def dot(a, b, dims=((1,), (0,))):
    return lax.dot_general(a, b, (dims, ((), ())), preferred_element_type=f32)


def at(start, size, multiple=16):
    return pl.ds(pl.multiple_of(start, multiple) if not isinstance(start, int) else start, size)


ALL = slice(None)
LEFT, RIGHT, FAR = 3, 1, 2
SIDES = (RIGHT, LEFT)


def loop(begin, end, body):
    def one(i, carry):
        body(i)
        return carry

    lax.fori_loop(begin, end, one, 0)


def odd(i):
    return lax.rem(i, 2)


class Sizes:
    chunk, piece, rows = 1024, 512, 256

    def __init__(self, mesh, tokens, d, ff):
        self.R = mesh.shape["r"]
        self.Z = self.R // Y
        self.T, self.D, self.F = tokens, d, ff
        self.NB = ff // (X * LANES)
        self.FB = X * LANES
        self.h = d // (X * CORES)
        self.TC = min(self.chunk, tokens)
        self.T3 = min(self.rows, tokens)
        self.TS = min(self.piece, tokens)
        self.unit = (Y, 3, self.h, LANES)
        self.active = self.h // 16
        self.halves = (slice(0, self.FB // 2), slice(self.FB // 2, self.FB))
        self.early = self.NB // 2
        assert self.h % 16 == 0 and self.active <= self.Z and mesh.shape["s"] == X * CORES


class Here:
    def __init__(self, z):
        s, self.r = lax.axis_index("s"), lax.axis_index("r")
        self.x, self.c = lax.div(s, CORES), lax.rem(s, CORES)
        self.y, self.z, self.Z = lax.div(self.r, z.Z), lax.rem(self.r, z.Z), z.Z
        self.R = z.R

    def partner(self):
        return {"s": self.x * CORES + 1 - self.c}

    def along_x(self, k):
        return {"s": lax.rem(self.x + k, X) * CORES + self.c}

    def along_y(self, k):
        return {"r": lax.rem(self.y + k, Y) * self.Z + self.z}

    def right(self):
        return lax.rem(self.x + RIGHT, X)

    def left(self):
        return lax.rem(self.x + LEFT, X)

    def along_z(self, k):
        return {"r": self.y * self.Z + lax.rem(self.z + k, self.Z)}


def remote(src, dst, sent, got, where):
    return pltpu.make_async_remote_copy(src_ref=src, dst_ref=dst, send_sem=sent, recv_sem=got, device_id=where, device_id_type=MESH)


def start(copies):
    for copy in copies:
        copy.start()


def wait(ref, sem):
    pltpu.make_async_copy(ref, ref, sem).wait()


def meet(peers):
    barrier = pltpu.get_barrier_semaphore()
    for peer in peers:
        pl.semaphore_signal(barrier, inc=1, device_id=peer, device_id_type=MESH)
    return lambda: pl.semaphore_wait(barrier, len(peers))


class Fetch:
    PHASES = ("a1", "a2", "b1", "b2", "c", "d1", "d2", "e")

    def __init__(self, z, here, shards, w, sems, begin, end):
        self.z, self.here, self.shards, self.w, self.first, self.last = z, here, shards, w, begin, end
        self.local, self.local_d, self.pair, self.pair_sent = sems[:4]
        self.got = dict(zip(self.PHASES, sems[4::2], strict=True))
        self.sent = dict(zip(self.PHASES, sems[5::2], strict=True))
        self.parts = [[k for k in range(z.NB) if begin <= (c * z.NB + k) // 2 < end] for c in range(CORES)]

    @classmethod
    def scratch(cls, z):
        return [DMA((z.NB,)), DMA, DMA, DMA] + [DMA((z.NB,)) for _ in range(2 * len(cls.PHASES))]

    def peers(self):
        here = self.here
        return [here.partner()] + [here.along_x(k) for k in SIDES] + [here.along_y(k) for k in SIDES]

    def own(self, j):
        z, here = self.z, self.here
        for shard, w in zip(self.shards[:2], self.w[:2], strict=True):
            for l in range(X):
                slot = w.at[j, self.rows(here.x), pl.ds(l * LANES, LANES)]
                pltpu.make_async_copy(shard.at[:, at((l * z.NB + j) * LANES, LANES, LANES)], slot, self.local.at[j]).start()

    def each_core(self, do):
        for c in range(CORES):
            pl.when(self.here.c == c)(lambda c=c: do(self.parts[c], self.parts[1 - c]))

    def part(self, k):
        z, here = self.z, self.here
        place = here.c * z.NB + k
        return self.shards[2].at[pl.ds(64 * k, 64), :], self.w[2].at[lax.div(place, 2), at(here.x * LANES + odd(place) * 64, 64), :]

    def rows(self, x):
        return at(x * (CORES * self.z.h) + self.here.c * self.z.h, self.z.h)

    def lanes(self, y):
        return at(y * LANES, LANES, LANES)

    def down(self, x, begin=0, size=64):
        return at(x * LANES + self.here.c * 64 + begin, size)

    def send(self, phase, j, w, rows, lanes, where):
        slot = self.w[w].at[j, rows, lanes]
        remote(slot, slot, self.sent[phase].at[j], self.got[phase].at[j], where).start()

    def begin_local(self):
        for j in range(self.first, self.last):
            self.own(j)

        def do(mine, _):
            for k in mine:
                pltpu.make_async_copy(*self.part(k), self.local_d).start()

        self.each_core(do)

    def begin_pair(self):
        def do(mine, _):
            for k in mine:
                src, slot = self.part(k)
                remote(src, slot, self.pair_sent, self.pair, self.here.partner()).start()

        self.each_core(do)

    def wait_parts(self, n, sem):
        if n:
            wait(self.halves(0, n), sem)

    def end_pair(self):
        def do(mine, other):
            self.wait_parts(len(mine), self.local_d)
            self.wait_parts(len(other), self.pair)

        self.each_core(do)

    def start_a1(self, j, alone=False):
        here = self.here
        wait(self.pieces(j, 8), self.local.at[j])
        for k in SIDES:
            for w in range(2):
                self.send("a1", j, w, self.rows(here.x), ALL if alone else self.lanes(here.y), here.along_x(k))

    def start_d1(self, j):
        for k in SIDES:
            self.send("d1", j, 2, self.down(self.here.x), ALL, self.here.along_x(k))

    def start_a2(self, j, alone=False):
        here = self.here
        wait(self.pieces(j, 16 if alone else 4), self.got["a1"].at[j])
        lanes = ALL if alone else self.lanes(here.y)
        self.send("a2", j, 0, self.rows(here.left()), lanes, here.along_x(RIGHT))
        self.send("a2", j, 1, self.rows(here.right()), lanes, here.along_x(LEFT))

    def start_d2(self, j):
        here = self.here
        wait(self.halves(j, 2), self.got["d1"].at[j])
        self.send("d2", j, 2, self.down(here.left(), 0, 32), ALL, here.along_x(RIGHT))
        self.send("d2", j, 2, self.down(here.right(), 32, 32), ALL, here.along_x(LEFT))

    def start_b1(self, j):
        here = self.here
        wait(self.pieces(j, 2), self.got["a2"].at[j])
        for k in SIDES:
            for m in range(1, X):
                for w in range(2):
                    self.send("b1", j, w, self.rows(lax.rem(here.x + m, X)), self.lanes(here.y), here.along_y(k))

    def start_b2(self, j):
        here = self.here
        wait(self.pieces(j, 12), self.got["b1"].at[j])
        for m in range(1, X):
            rows = self.rows(lax.rem(here.x + m, X))
            self.send("b2", j, 0, rows, self.lanes(lax.rem(here.y + LEFT, Y)), here.along_y(RIGHT))
            self.send("b2", j, 1, rows, self.lanes(lax.rem(here.y + RIGHT, Y)), here.along_y(LEFT))

    def start_c(self, j, alone=False):
        if alone:
            wait(self.pieces(j, 8), self.got["a2"].at[j])
        else:
            wait(self.pieces(j, 6), self.got["b2"].at[j])
        for w in range(2):
            for x in range(X):
                self.send("c", j, w, self.rows(x), ALL, self.here.partner())

    def start_e(self, j):
        wait(self.halves(j, 1), self.got["d2"].at[j])
        for m in range(1, X):
            self.send("e", j, 2, self.down(lax.rem(self.here.x + m, X)), ALL, self.here.partner())

    def pieces(self, j, n):
        high = 6 if n % 6 == 0 else min(n, 8)
        return self.w[0].at[j, pl.ds(0, high * self.z.h), pl.ds(0, n // high * LANES)]

    def halves(self, j, n):
        return self.w[2].at[j, pl.ds(0, 64 * n), :]

    def ready(self, j):
        wait(self.w[0].at[j], self.got["c"].at[j])
        wait(self.halves(j, 3), self.got["e"].at[j])

    def serve_a(self, j):
        @self.if_mine(j + 1)
        def _():
            self.start_b2(j + 1)
            self.start_d2(j + 1)

        @self.if_mine(j + 2)
        def _():
            self.start_b1(j + 2)
            self.start_d1(j + 2)

        self.if_mine(j + 3)(lambda: self.start_a1(j + 3))

    def serve_b(self, j):
        @self.if_mine(j + 1)
        def _():
            self.start_c(j + 1)
            self.start_e(j + 1)

        self.if_mine(j + 3)(lambda: self.start_a2(j + 3))

    def if_mine(self, j):
        return pl.when(jnp.logical_and(j >= self.first, j < self.last))

    def end(self, alone):
        self.each_core(lambda mine, _: self.wait_parts(len(mine), self.pair_sent))

        def drain(j, alone=False):
            wait(self.pieces(j, 16 if alone else 4), self.sent["a1"].at[j])
            wait(self.pieces(j, 8 if alone else 2), self.sent["a2"].at[j])
            if not alone:
                wait(self.pieces(j, 12), self.sent["b1"].at[j])
                wait(self.pieces(j, 6), self.sent["b2"].at[j])
            wait(self.halves(j, 2), self.sent["d1"].at[j])
            wait(self.halves(j, 1), self.sent["d2"].at[j])
            wait(self.w[0].at[j], self.sent["c"].at[j])
            wait(self.halves(j, 3), self.sent["e"].at[j])

        for j in alone:
            drain(j, True)
        loop(self.first + len(alone), self.last, drain)


def normed(wide):
    scale = lax.rsqrt(jnp.mean(wide * wide, -1, keepdims=True) + 1e-6)
    return (wide * scale).astype(bf16), scale


def forward_kernel(z, *refs):
    refs = list(refs)

    def take(n):
        out, refs[:] = refs[:n], refs[n:]
        return out

    x_in, *shards = take(4)
    h_out, *w_out = take(4)
    kept_out, next_out = take(3), take(3)
    a, acc, xs = take(3)
    parts, w, w_next = take(3), take(3), take(3)
    act, by_up, by_gate = parts
    x_sem, out_sem, next_sem, h_sem, keep_sem = take(5)
    n_sems = len(Fetch.scratch(z))
    here = Here(z)
    fetch = Fetch(z, here, [v.at[0] for v in shards], w, take(n_sems), 0, z.NB)
    later = Fetch(z, here, [v.at[1] for v in shards], w_next, take(n_sems), 0, z.early)
    early = range(z.early)
    met = meet(fetch.peers())
    fetch.begin_local()
    load = pltpu.make_async_copy(x_in, xs, x_sem)
    load.start()
    met()
    fetch.begin_pair()
    fetch.start_a1(1)
    fetch.start_a1(0, True)
    fetch.end_pair()
    fetch.start_d1(0)
    fetch.start_d1(1)
    fetch.start_a1(2)
    load.wait()

    def prepare(i):
        rows = at(i * z.T3, z.T3)
        a[rows, :] = normed(xs[rows, :].astype(f32))[0]
        acc[rows, :] = jnp.zeros((z.T3, z.D), f32)

    loop(0, z.T // z.T3, prepare)
    fetch.start_a2(1)
    fetch.start_a2(0, True)
    fetch.start_b1(1)
    fetch.start_d2(0)
    fetch.start_c(0, True)
    fetch.start_e(0)
    fetch.start_a2(2)
    n = z.T // z.TC

    def keep(j, i):
        slot = odd(i)
        return [pltpu.make_async_copy(v.at[slot], o.at[j, at(i * z.TC, z.TC), :], keep_sem.at[k, slot]) for k, (v, o) in enumerate(zip(parts, kept_out, strict=True))]

    def kept(j, i):
        for copy in keep(j, i):
            copy.wait()

    def prefetch(j):
        @pl.when(j == 0)
        def _():
            later.begin_local()
            later.begin_pair()

        @pl.when(j == 1)
        def _():
            later.end_pair()
            later.start_a1(0, True)
            later.start_d1(0)

        @pl.when(j == 2)
        def _():
            later.start_a2(0, True)
            later.start_d2(0)
            for e in early[1:]:
                later.start_a1(e, True)
                later.start_d1(e)

        @pl.when(j == 3)
        def _():
            later.start_c(0, True)
            later.start_e(0)
            for e in early[1:]:
                later.start_a2(e, True)
                later.start_d2(e)

        @pl.when(j == 4)
        def _():
            for e in early[1:]:
                later.start_c(e, True)
                later.start_e(e)

    def block(j):
        fetch.serve_a(j)
        fetch.ready(j)
        start([pltpu.make_async_copy(v.at[j], o.at[j], out_sem.at[k]) for k, (v, o) in enumerate(zip(w, w_out, strict=True))])

        def chunk(i):
            @pl.when(i == n // 2)
            def _():
                fetch.serve_b(j)
                prefetch(j)

            pl.when(j * n + i > 1)(lambda: kept(j, i))
            rows, slot = at(i * z.TC, z.TC), odd(i)
            for cols in z.halves:
                gate, up = dot(a[rows, :], w[0][j, :, cols]), dot(a[rows, :], w[1][j, :, cols])
                sig = 1.0 / (1.0 + jnp.exp(-gate))
                silu = gate * sig
                act[slot, :, cols] = (silu * up).astype(bf16)
                by_up[slot, :, cols] = silu
                by_gate[slot, :, cols] = up * (sig + silu * (1.0 - sig))
            acc[rows, :] += dot(act[slot], w[2][j])
            start(keep(j, i))

        loop(0, n, chunk)

    loop(0, z.NB, block)

    def finish(i):
        rows = at(i * z.T3, z.T3)
        xs[rows, :] = xs[rows, :] + acc[rows, :].astype(bf16)

    loop(0, z.T // z.T3, finish)
    store = pltpu.make_async_copy(xs, h_out, h_sem)
    store.start()
    for e in early:
        later.ready(e)
    handed = [pltpu.make_async_copy(v, o, next_sem.at[k]) for k, (v, o) in enumerate(zip(w_next, next_out, strict=True))]
    start(handed)
    for i in range(2):
        kept(z.NB - 1, n - 2 + i)
    for k, v in enumerate(w):
        wait(v, out_sem.at[k])
    fetch.end((0,))
    later.end(early)
    store.wait()
    for copy in handed:
        copy.wait()


class Reduce:
    PHASES = ("p", "x1", "x2", "y", "z", "az", "ay", "f")

    def __init__(self, z, here, units, layer_first, outs, refs):
        self.z, self.here, self.units, self.layer_first, self.outs = z, here, units, layer_first, outs
        (self.stage, self.got_p, self.got_x1, self.got_x2, self.got_y, self.got_z, self.send_x1, self.send_x2, self.send_y, self.send_z, *refs) = refs
        (self.kept_x, self.kept_y, self.kept_z, self.fin, self.down, self.turned, self.out_sem, self.turned_sem, *refs) = refs
        self.got = dict(zip(self.PHASES, refs[::2], strict=True))
        self.sent = dict(zip(self.PHASES, refs[1::2], strict=True))

    @classmethod
    def scratch(cls, z, units):
        unit, share = z.unit, z.unit[1:]
        data = [(2, X, CORES, *unit), (3, X, *unit), (2, 2, Y // 2, *share), (2, 2, *unit), (2, *unit), (units, z.Z, 3, 16, LANES)]
        data += [unit, (2, 2, *unit), unit, share]
        wide = [(2, *unit), share, share]
        return (
            [VMEM(shape, bf16) for shape in data]
            + [VMEM(shape, f32) for shape in wide]
            + [VMEM((units, *unit), bf16), VMEM((units, CORES, Y, z.h, LANES), bf16), VMEM((2, LANES, z.D), bf16)]
            + [DMA((2, units)), DMA((2, 2))]
            + [DMA((units,)) for _ in range(2 * len(cls.PHASES))]
        )

    def peers(self):
        here = self.here
        return (
            [here.partner()] + [here.along_x(k) for k in SIDES] + [here.along_y(k) for k in range(1, Y)] + [here.along_z(k) for k in range(1, here.Z)]
        )

    def send(self, phase, u, src, dst, where):
        remote(src, dst, self.sent[phase].at[u], self.got[phase].at[u], where).start()

    def over(self, work, begin=0, end=Y):
        matrices = len(self.outs)
        loop(begin * matrices, end * matrices, lambda i: work(lax.div(i, matrices), lax.rem(i, matrices)))

    def start_p(self, u):
        here = self.here
        for x in range(X):
            self.send("p", u, self.stage.at[odd(u), x, 1 - here.c], self.got_p.at[lax.rem(u, 3), x], here.partner())

    def both(self, u, x, y, m):
        return self.stage[odd(u), x, self.here.c, y, m].astype(f32) + self.got_p[lax.rem(u, 3), x, y, m].astype(f32)

    def start_x1(self, u):
        here, half, slot = self.here, Y // 2, odd(u)
        wait(self.got_p.at[lax.rem(u, 3)], self.got["p"].at[u])
        far = lax.rem(here.x + FAR, X)

        def work(y, m):
            self.send_x1[y, m] = self.both(u, far, y, m).astype(bf16)

        self.over(work)
        for side in range(2):
            self.send("x1", u, self.send_x1.at[pl.ds(side * half, half)], self.got_x1.at[slot, side], here.along_x(SIDES[side]))

    def start_x2(self, u):
        here, half, slot = self.here, Y // 2, odd(u)
        wait(self.got_x1.at[slot], self.got["x1"].at[u])
        wait(self.got_x1.at[slot], self.sent["x1"].at[u])
        wait(self.got_p.at[lax.rem(u, 3)], self.sent["p"].at[u])
        right, left = here.right(), here.left()

        def first(y, m):
            self.send_x2[slot, 0, y, m] = (self.both(u, right, y, m) + self.got_x1[slot, 0, y, m].astype(f32)).astype(bf16)
            self.send_x2[slot, 1, y, m] = self.both(u, left, y, m).astype(bf16)
            self.kept_x[slot, y, m] = self.both(u, here.x, y, m)

        def second(y, m):
            self.send_x2[slot, 0, y, m] = self.both(u, right, y, m).astype(bf16)
            self.send_x2[slot, 1, y, m] = (self.both(u, left, y, m) + self.got_x1[slot, 1, y - half, m].astype(f32)).astype(bf16)
            self.kept_x[slot, y, m] = self.both(u, here.x, y, m)

        self.over(first, 0, half)
        self.over(second, half, Y)
        for side in range(2):
            self.send("x2", u, self.send_x2.at[slot, side], self.got_x2.at[slot, side], here.along_x(SIDES[side]))

    def start_y(self, u):
        here, slot = self.here, odd(u)
        wait(self.got_x2.at[slot], self.got["x2"].at[u])
        wait(self.got_x2.at[slot], self.sent["x2"].at[u])

        def total(y, m):
            return self.kept_x[slot, y, m] + self.got_x2[slot, 0, y, m].astype(f32) + self.got_x2[slot, 1, y, m].astype(f32)

        def work(y, m):
            self.send_y[y, m] = total(y, m).astype(bf16)

        def own(_, m):
            self.kept_y[m] = total(here.y, m)

        self.over(work)
        self.over(own, 0, 1)
        for k in (*SIDES, FAR):
            self.send("y", u, self.send_y.at[lax.rem(here.y + k, Y)], self.got_y.at[slot, here.y], here.along_y(k))

    def start_z(self, u):
        z, here, slot = self.z, self.here, odd(u)
        wait(self.got_y.at[slot, pl.ds(0, Y - 1)], self.got["y"].at[u])
        wait(self.got_y.at[slot, pl.ds(0, Y - 1)], self.sent["y"].at[u])

        def work(_, m):
            total = self.kept_y[m]
            for k in range(1, Y):
                total += self.got_y[slot, lax.rem(here.y + k, Y), m].astype(f32)
            self.kept_z[m] = total
            self.send_z[m] = total.astype(bf16)

        self.over(work, 0, 1)

        def send(k):
            to = lax.rem(here.z + k, z.Z)
            pl.when(to < z.active)(lambda: self.send("z", u, self.send_z.at[:, at(to * 16, 16), :], self.got_z.at[u, here.z], here.along_z(k)))

        loop(1, z.Z, send)

    def if_active(self, yes, no):
        pl.when(self.here.z < self.z.active)(yes)
        pl.when(self.here.z >= self.z.active)(no)

    def wait_pieces(self, u, n, sem):
        if n:
            wait(self.got_z.at[u, pl.ds(0, n)], sem.at[u])

    def start_az(self, u):
        z, here = self.z, self.here

        def yes():
            self.wait_pieces(u, z.active - 1, self.sent["z"])
            self.wait_pieces(u, z.Z - 1, self.got["z"])
            rows = at(here.z * 16, 16)
            total = self.kept_z[:, rows, :]
            for k in range(1, z.Z):
                total += self.got_z[u, lax.rem(here.z + k, z.Z)].astype(f32)
            self.fin[u, here.y, :, rows, :] = total.astype(bf16)
            mine = self.fin.at[u, here.y, :, rows, :]

            loop(1, z.Z, lambda k: self.send("az", u, mine, mine, here.along_z(k)))

        self.if_active(yes, lambda: self.wait_pieces(u, z.active, self.sent["z"]))

    def start_ay(self, u):
        z, here = self.z, self.here
        self.if_active(lambda: self.wait_pieces(u, z.active - 1, self.got["az"]), lambda: self.wait_pieces(u, z.active, self.got["az"]))
        share = self.fin.at[u, here.y]
        for k in (*SIDES, FAR):
            self.send("ay", u, share, share, here.along_y(k))

    def place(self, u):
        nb = self.z.NB
        return (1, u) if self.layer_first else (1 - lax.div(u + nb - 1, nb), lax.rem(u + nb - 1, nb))

    def start_f(self, u):
        z, c = self.z, self.here.c
        layer, j = self.place(u)
        wait(self.fin.at[u, pl.ds(0, Y - 1)], self.got["ay"].at[u])
        for m in range(2):
            for y in range(Y):
                out = self.outs[m].at[layer, :, at((y * z.NB + j) * LANES, LANES, LANES)]
                pltpu.make_async_copy(self.fin.at[u, y, m], out, self.out_sem.at[m, u]).start()
        self.down[u, c] = self.fin[u, :, 2]
        self.send("f", u, self.fin.at[u, :, 2], self.down.at[u, c], self.here.partner())

    def finish(self, u):
        z, c = self.z, self.here.c
        layer, j = self.place(u)
        wait(self.down.at[u, 0], self.got["f"].at[u])
        slot = odd(u)
        pl.when(u > 1)(lambda: self.turned_out(u - 2, "wait"))
        self.turned[slot] = self.down[u].reshape(z.D, LANES).T
        self.turned_out(u, "start")

    def turned_out(self, u, what):
        z, c = self.z, self.here.c
        layer, j = self.place(u)
        for half in range(2):
            row = 2 * j + half

            @pl.when(lax.div(row, z.NB) == c)
            def _(half=half, row=row):
                out = self.outs[2].at[layer, at(lax.rem(row, z.NB) * 64, 64), :]
                getattr(pltpu.make_async_copy(self.turned.at[odd(u), pl.ds(half * 64, 64), :], out, self.turned_sem.at[odd(u), half]), what)()

    def end(self):
        z = self.z

        def one(u):
            self.if_active(lambda: self.wait_pieces(u, z.Z - 1, self.sent["az"]), lambda: None)
            wait(self.fin.at[u, pl.ds(0, Y - 1)], self.sent["ay"].at[u])
            wait(self.down.at[u, 0], self.sent["f"].at[u])
            for m in range(2):
                wait(self.down.at[u, 0], self.out_sem.at[m, u])

        loop(0, self.units, one)
        for u in range(max(0, self.units - 2), self.units):
            self.turned_out(u, "wait")


def backward_kernel(z, first, *refs):
    T, TC, T3, NB, FB, D = z.T, z.TC, z.T3, z.NB, z.FB, z.D
    here = Here(z)
    refs = list(refs)

    def take(n):
        out, refs[:] = refs[:n], refs[n:]
        return out

    h_in, dh_in, w0, w1, w2 = take(5)
    if first:
        early_in = take(3)
    else:
        left_in, by_up_in, by_gate_in, act_in = take(4)
        take(3)
    dx_out, *outs = take(4)
    spill = take(1)[0]
    if first:
        left_out = take(1)[0]
    dx_buf, h_buf, a_t, dh, dh_t, wg, wu, wd, work = take(9)
    ld_sem, dh_sem, w_sem, sp_sem, s3_sem, o_sem, left_sem = take(7)
    if first:
        a = take(1)[0]
    else:
        saved, saved_sem, act_sem = take(3)
    if first:
        fetch = Fetch(z, here, (w0.at[1], w1.at[1], w2.at[1]), (wg, wu, wd), take(len(Fetch.scratch(z))), z.early, NB)
        w0, w1, w2 = early_in
    base = 0 if first else 1
    units = NB - 1 if first else NB + 1
    reduce = Reduce(z, here, units, first, outs, refs)
    met = meet(reduce.peers())
    whole = pltpu.make_async_copy(dh_in, dh, dh_sem)
    whole.start()

    def load_h(i):
        return pltpu.make_async_copy(h_in.at[at(i * T3, T3), :], h_buf.at[odd(i)], ld_sem.at[odd(i)])

    load_h(0).start()

    def loads(j):
        return [pltpu.make_async_copy(src.at[j], dst.at[j], w_sem.at[k, j]) for k, (src, dst) in enumerate(((w0, wg), (w1, wu), (w2, wd)))]

    TS, slots = z.TS, 3

    def load_saved(q):
        j, rows, slot = lax.div(q, T // TS), at(lax.rem(q, T // TS) * TS, TS), lax.rem(q, slots)
        return [pltpu.make_async_copy(v.at[j, rows, :], saved.at[slot, k], saved_sem.at[k, slot]) for k, v in enumerate((by_up_in, by_gate_in))]

    def load_act(j):
        return pltpu.make_async_copy(act_in.at[j], work.at[pl.ds(0, T), :], act_sem)

    if first:
        for j in range(z.early):
            start(loads(j))
        fetch.begin_local()
        met()
        fetch.begin_pair()
        fetch.start_a1(z.early)
    else:
        left = pltpu.make_async_copy(left_in, reduce.stage.at[0], left_sem)
        left.start()
        for j in range(NB):
            start(loads(j)[2:])
        for q in range(2):
            start(load_saved(q))
        for j in range(NB):
            start(loads(j)[:2])
    whole.wait()
    n3 = T // T3

    def prepare(i):
        rows = at(i * T3, T3, LANES)
        pl.when(i + 1 < n3)(lambda: load_h(i + 1).start())
        load_h(i).wait()
        value = normed(h_buf[odd(i)].astype(f32))[0]
        if first:
            a[rows, :] = value
        a_t[:, rows] = value.T
        dh_t[:, rows] = dh[rows, :].T

    if not first:
        met()
        left.wait()
        reduce.start_p(0)
    loop(0, n3, prepare)
    if first:
        fetch.end_pair()
        fetch.start_a2(z.early)

    def product(k, rows, cols):
        return work.at[at(k * T + rows.start, rows.size), cols]

    def spills(j):
        return [pltpu.make_async_copy(work.at[pl.ds((1 + k) * T, T), :], spill.at[k, j], sp_sem.at[k]) for k in range(2)]

    def spilled(j):
        for copy in spills(j):
            copy.wait()

    def step(name, u):
        do = getattr(reduce, "start_" + name)
        if isinstance(u, int):
            if 0 <= u < units:
                do(u)
        else:
            pl.when(jnp.logical_and(u >= 0, u < units))(lambda: do(u))

    def halfway(i, n, before, after):
        if n == 1:
            before()
            after()
        else:
            pl.when(i == 0)(before)
            pl.when(i == n // 2)(after)

    def loaded(j):
        for copy in loads(j):
            copy.wait()

    def block(j):
        u = j + base - 1
        if first:
            fetch.serve_a(j)
            pl.when(j < z.early)(lambda: loaded(j))
            pl.when(j >= z.early)(lambda: fetch.ready(j))
        else:
            load_act(j).start()
            loads(j)[2].wait()
        pl.when(j > 0)(lambda: spilled(j - 1))

        def at_0():
            if first:
                step("ay", u - 3)
                step("z", u - 2)
            else:
                step("x2", u - 1)
                step("ay", u - 4)

        def at_1():
            if first:
                step("x1", u)
            else:
                step("z", u - 3)

        def at_2():
            if first:
                fetch.serve_b(j)
                step("y", u - 1)
                step("az", u - 2)
            else:
                step("y", u - 2)
                step("x1", u)

        def at_3():
            if first:
                step("x2", u)
            else:
                step("az", u - 3)

        def piece(i):
            halfway(i, T // TS, at_0, at_1)
            q, rows = j * (T // TS) + i, at(i * TS, TS)
            pl.when(q + 2 < NB * (T // TS))(lambda: start(load_saved(q + 2)))
            for copy in load_saved(q):
                copy.wait()
            by_act = dot(dh[rows, :], wd[j], ((1,), (1,))).astype(bf16).astype(f32)
            slot = lax.rem(q, slots)
            product(1, rows, ALL)[...] = (by_act * saved[slot, 1]).astype(bf16)
            product(2, rows, ALL)[...] = (by_act * saved[slot, 0]).astype(bf16)

        def chunk(i):
            halfway(i, T // TC, at_0, at_1)
            rows = at(i * TC, TC)
            for cols in z.halves:
                gate, up = dot(a[rows, :], wg[j, :, cols]), dot(a[rows, :], wu[j, :, cols])
                by_act = dot(dh[rows, :], wd[j, cols, :], ((1,), (1,))).astype(bf16).astype(f32)
                sig = 1.0 / (1.0 + jnp.exp(-gate))
                silu = gate * sig
                product(0, rows, cols)[...] = (silu * up).astype(bf16)
                product(1, rows, cols)[...] = (by_act * up * (sig + silu * (1.0 - sig))).astype(bf16)
                product(2, rows, cols)[...] = (by_act * silu).astype(bf16)

        if first:
            loop(0, T // TC, chunk)
        else:
            loop(0, T // TS, piece)
            load_act(j).wait()
        start(spills(j))
        stage, slot, m = reduce.stage, odd(j + base), D // 2

        def rows_of(i):
            halfway(i, 2, at_2, at_3)
            rows = at(i * m, m)
            gates = dot(a_t[rows, :], work[pl.ds(T, T), :]).astype(bf16)
            ups = dot(a_t[rows, :], work[pl.ds(2 * T, T), :]).astype(bf16)
            downs = dot(dh_t[rows, :], work[pl.ds(0, T), :]).astype(bf16)
            for y in range(Y):
                lanes = slice(y * LANES, (y + 1) * LANES)
                for x in range(X // 2):
                    for c in range(CORES):
                        part = slice((x * CORES + c) * z.h, (x * CORES + c + 1) * z.h)
                        stage[slot, i * (X // 2) + x, c, y, 0] = gates[part, lanes]
                        stage[slot, i * (X // 2) + x, c, y, 1] = ups[part, lanes]
                for x in range(X):
                    stage[slot, x, i, y, 2] = downs[y * z.h : (y + 1) * z.h, x * LANES : (x + 1) * LANES]

        loop(0, 2, rows_of)
        step("p", j + base)

    loop(0, NB, block)
    if first:
        left = pltpu.make_async_copy(reduce.stage.at[(NB - 1) % 2], left_out, left_sem)
        left.start()
    spilled(NB - 1)

    def load_3(i):
        slot, rows = odd(i), at(i * T3, T3)
        out = [load_h(i)]
        for k in range(2):
            for j in range(NB):
                out.append(pltpu.make_async_copy(spill.at[k, j, rows, :], work.at[at(((slot * 2 + k) * NB + j) * T3, T3), :], s3_sem.at[slot]))
        return out

    def store_3(i):
        return pltpu.make_async_copy(dx_buf.at[odd(i)], dx_out.at[at(i * T3, T3), :], o_sem.at[odd(i)])

    start(load_3(0))
    u = NB + base - 1
    if first:
        todo = [
            [("ay", u - 3), ("z", u - 2)],
            [("az", u - 2)],
            [("y", u - 1)],
            [("ay", u - 2)],
            [("z", u - 1)],
            [("az", u - 1)],
            [("ay", u - 1)],
        ]
        rest = []
    else:
        todo = [
            [("x2", u - 1), ("ay", u - 4)],
            [("z", u - 3), ("y", u - 2), ("x1", u)],
            [],
            [("az", u - 3)],
            [("z", u - 2)],
            [("x2", u), ("y", u - 1), ("ay", u - 3)],
            [("az", u - 2)],
        ]
        rest = [("ay", u - 2), ("z", u - 1), ("y", u), ("az", u - 1), ("z", u), ("ay", u - 1), ("az", u), ("ay", u)]

    done = u - 1 if first else u - 3

    def rows_back(i):
        slot, rows = odd(i), at(i * T3, T3)
        pl.when(i + 1 < n3)(lambda: start(load_3(i + 1)))
        for when, steps in enumerate(todo):

            def now(steps=steps):
                for each in steps:
                    step(*each)

            pl.when(i == when)(now)

        @pl.when(i == n3 - 2)
        def _():
            loop(0, done, reduce.start_f)

        @pl.when(i == n3 - 1)
        def _():
            loop(0, done, reduce.finish)

        if not first:

            @pl.when(i == 0)
            def _():
                for j in range(NB):
                    for copy in loads(j)[:2]:
                        copy.wait()

        load_h(i).wait()
        wait(work.at[at(slot * 2 * NB * T3, 2 * NB * T3), :], s3_sem.at[slot])
        pl.when(i > 1)(lambda: store_3(i - 2).wait())
        back = []
        for k, w in ((0, wg), (1, wu)):
            total = None
            for j in range(NB):
                part = dot(work[at(((slot * 2 + k) * NB + j) * T3, T3), :], w[j], ((1,), (1,)))
                total = part if total is None else total + part
            back.append(total.astype(bf16))
        by_a = (back[0] + back[1]).astype(f32)
        wide = h_buf[slot].astype(f32)
        square = jnp.mean(wide * wide, -1, keepdims=True) + 1e-6
        scale = lax.rsqrt(square)
        by_scale = jnp.sum(by_a * wide, -1, keepdims=True)
        by_square = by_scale * (-0.5 * scale / square) * (2.0 / D)
        dx_buf[slot] = dh[rows, :] + (by_a * scale + by_square * wide).astype(bf16)
        store_3(i).start()

    loop(0, n3, rows_back)
    assert n3 == 8
    for each in rest:
        step(*each)
    for v in range(max(done, 0), units):
        reduce.start_f(v)
    for v in range(max(done, 0), units):
        reduce.finish(v)
    reduce.end()
    if first:
        fetch.end(())
        left.wait()
    for i in range(max(0, n3 - 2), n3):
        store_3(i).wait()


def call(body, out, n_in, scratch, number, aliases=()):
    return pl.pallas_call(
        body,
        out_shape=out,
        in_specs=[pl.BlockSpec(memory_space=HBM)] * n_in,
        out_specs=[pl.BlockSpec(memory_space=HBM)] * len(out),
        scratch_shapes=scratch,
        input_output_aliases=dict(aliases),
        compiler_params=pltpu.CompilerParams(collective_id=number, has_side_effects=True, vmem_limit_bytes=66_900_000),
    )


def forward(z, x, shards):
    S = jax.ShapeDtypeStruct
    wide, tall, tokens, hidden, piece = (z.NB, z.D, z.FB), (z.NB, z.FB, z.D), (z.T, z.D), (z.NB, z.T, z.FB), (2, z.TC, z.FB)
    scratch = [VMEM(tokens, bf16), VMEM(tokens, f32), VMEM(tokens, bf16), VMEM(piece, bf16), VMEM(piece, f32), VMEM(piece, f32)]
    early = [(z.early, *shape[1:]) for shape in (wide, wide, tall)]
    scratch += [VMEM(shape, bf16) for shape in (wide, wide, tall, *early)]
    scratch += [DMA, DMA((3,)), DMA((3,)), DMA, DMA((3, 2))] + Fetch.scratch(z) + Fetch.scratch(z)
    out = [S(tokens, bf16), S(wide, bf16), S(wide, bf16), S(tall, bf16), S(hidden, bf16), S(hidden, f32), S(hidden, f32)]
    out += [S(shape, bf16) for shape in early]
    h, *out = call(functools.partial(forward_kernel, z), out, 4, scratch, 0)(x, *shards)
    return h, out[:3], out[3:6], out[6:]


def backward(z, h, dh, w, more, first):
    S = jax.ShapeDtypeStruct
    wide, tall, tokens = (z.NB, z.D, z.FB), (z.NB, z.FB, z.D), (z.T, z.D)
    units = z.NB - 1 if first else z.NB + 1
    scratch = [VMEM((2, z.T3, z.D), bf16), VMEM((2, z.T3, z.D), bf16)]
    scratch += [VMEM(tokens[::-1], bf16), VMEM(tokens, bf16), VMEM(tokens[::-1], bf16)]
    scratch += [VMEM(wide, bf16), VMEM(wide, bf16), VMEM(tall, bf16), VMEM((max(3 * z.T, 4 * z.NB * z.T3), z.FB), bf16)]
    scratch += [DMA((2,)), DMA, DMA((3, z.NB)), DMA((2,)), DMA((2,)), DMA((2,)), DMA]
    if first:
        scratch += [VMEM(tokens, bf16)] + Fetch.scratch(z)
    else:
        scratch += [VMEM((3, 2, z.TS, z.FB), f32), DMA((2, 3)), DMA]
    scratch += Reduce.scratch(z, units)
    grads = [S((2, z.h, z.F), bf16), S((2, z.h, z.F), bf16), S((2, z.F // (X * CORES), z.D), bf16)]
    out = [S(tokens, bf16), *grads, S((2, z.NB, z.T, z.FB), bf16)]
    if first:
        out.append(S((X, CORES, *z.unit), bf16))
    args = (h, dh, *w, *more)
    aliases = {} if first else {len(args) - 3 + i: 1 + i for i in range(3)}
    dx, g, u, d, _, *left = call(functools.partial(backward_kernel, z, first), out, len(args), scratch, 1 if first else 2, aliases)(*args)
    return dx, (g, u, d), left


def solution(mesh):
    def step(x, dy, *weights):
        z = Sizes(mesh, x.shape[1], x.shape[2], weights[0].shape[2])
        h, w, (act, by_up, by_gate), early = forward(z, x[0], weights)
        dh, grads, left = backward(z, h, dy[0], weights, early, True)
        dx, grads, _ = backward(z, x[0], dh, w, (*left, by_up, by_gate, act, *grads), False)
        return dx[None], *grads

    states, cut = P(("rep", "r", "s"), None, None), P(None, "s", None)
    return jax.shard_map(
        step,
        mesh=mesh,
        in_specs=(states, states) + (cut,) * 3,
        out_specs=(states,) + (P("rep", "s", None),) * 3,
        check_vma=False,
    )
```

time: 353 us -> 360 us (1.020)
  Pallas kernels: 344 us -> 351 us
    pallas_call x1, Pallas kernels: 70.4 us -> 84.3 us  [forward(): call(functools.partial(forward_kernel, z), out, 4, scratch, 0)(x, *shards)]
    pallas_call x2, Pallas kernels: 274 us -> 267 us  [backward(): call(functools.partial(backward_kernel, z, first), out, len(args), scratc...]
where the time goes in v4:
time: 360 us; the launch traced here: 359 us
  Pallas kernels  351 us (98%)
  local copies, waits for them, and re-layouts  7.94 us (2%)
    pallas_call x2, Pallas kernels, backward(): call(functools.partial(backward_kernel, z, first), out, len(args), scratc...  267 us
    pallas_call x1, Pallas kernels, forward(): call(functools.partial(forward_kernel, z), out, 4, scratch, 0)(x, *shards)  84.3 us
    unnamed x10, local copies, waits for them, and re-layouts  7.94 us

profile of v4, /device:TPU:1, one launch (start us, length us, event | category | flops | bytes accessed | tf_op | source)
XLA Modules:
  0.0 359.4 jit_solution(10236867482441031039)
XLA Ops:
  0.6 84.3 %shard_map.84 = (bf16[2048,896]{1,0:T(8,128)(2,1)}, bf16[5,896,512]{2,1,0:T(8,128)(2,1)}, bf16[5,896,512]{2,1,0:T(8,128)(2,1)}, bf16[5,512,896]{2,1,0:T(8,128)(2...) custom-call(bf16[2048,896]{1,0:T(8,128)(2,1)} %bitcast.3, ...), custom_call_target="tpu_custom_call" | custom-call | tf_op jit(solution)/shard_map/pallas_call | solution.py:973
  85.0 131.8 %shard_map.85 = (bf16[2048,896]{1,0:T(8,128)(2,1)}, bf16[2,112,2560]{2,1,0:T(8,128)(2,1)}, bf16[2,112,2560]{2,1,0:T(8,128)(2,1)}, bf16[2,320,896]{2,1,0:T(8,128)...) custom-call(bf16[2048,896]{1,0:T(8,128)(2,1)} %get-tuple-element.23.refs_0_, ...), custom_call_target="tpu_custom_call" | custom-call | tf_op jit(solution)/shard_map/pallas_call | solution.py:996
  216.7 134.8 %shard_map.86 = (bf16[2048,896]{1,0:T(8,128)(2,1)}, bf16[2,112,2560]{2,1,0:T(8,128)(2,1)}, bf16[2,112,2560]{2,1,0:T(8,128)(2,1)}, bf16[2,320,896]{2,1,0:T(8,128)(2,1)}, bf16[2,5,2048,512]{3,2,1,0:T(8,128)(2,1)}) custom-call(bf16[2048,896]{1,0:T(8,128)(2,1)} %bitcast.4, ...), custom_call_target="tpu_custom_call", output_to_operand_aliasing={{1}: (9, {}), {2}: (10, {}), {3}: (11, {})} | custom-call | tf_op jit(solution)/shard_map/pallas_call | solution.py:996
  351.5 0.0 copy-start
  351.5 4.3 %copy.19 = bf16[1,2048,896]{2,1,0:T(8,128)(2,1)} copy(bf16[1,2048,896]{2,1,0:T(8,128)(2,1)} %bitcast.5) | data formatting | bytes 7340032
  355.8 0.0 copy-done
  355.8 0.0 copy-start.1
  355.8 0.0 copy-start.2
  355.8 1.0 copy.20
  356.8 0.7 copy-done.1
  357.4 1.0 copy.21
  358.4 0.0 copy-done.2
  358.4 1.0 copy.22
Async XLA Ops:
  351.5 4.3 %copy-start = (bf16[2,112,2560]{2,1,0:T(8,128)(2,1)S(1)}, bf16[2,112,2560]{2,1,0:T(8,128)(2,1)}, u32[]{:S(2)}) copy-start(bf16[2,112,2560]{2,1,0:T(8,128)(2,1)} %get-tuple-element.47) | copy-start | bytes 3440644
  355.8 1.7 copy-start.1
  355.8 2.7 copy-start.2

commit v5 on v4

--- a/solution.py
+++ b/solution.py
@@ -103,6 +103,22 @@
     for peer in peers:
         pl.semaphore_signal(barrier, inc=1, device_id=peer, device_id_type=MESH)
     return lambda: pl.semaphore_wait(barrier, len(peers))
+
+
+FETCHES = (
+    "a10,a11,a12,d10,a21,a20",
+    "a22,b11,d20,d11,c0,b12,e0",
+    "a13,d12,b21,d21,a23,d13",
+    "e1,c1,a14,b13,d22,d14",
+    "a24,d23,b22,La11,e2",
+    "c2,d24,Ld10,Ld11,b23,b14",
+    "e3",
+    "c3,b24,La10",
+    "e4,La21,c4,Ld21",
+    "Ld20",
+    "La20,Lc1,Le1",
+    "Le0,Lc0",
+)
 
 
 class Fetch:
@@ -319,12 +335,19 @@
     load.start()
     met()
     fetch.begin_pair()
-    fetch.start_a1(1)
-    fetch.start_a1(0, True)
-    fetch.end_pair()
-    fetch.start_d1(0)
-    fetch.start_d1(1)
-    fetch.start_a1(2)
+
+    def fetches(slot):
+        for item in FETCHES[slot].split(","):
+            who, phase, j = (later if item[0] == "L" else fetch), item.strip("L")[:-1], int(item[-1])
+            if phase == "d1" and j == 0:
+                who.end_pair()
+            do = getattr(who, "start_" + phase)
+            if phase in ("a1", "a2", "c"):
+                do(j, alone=who is later or j == 0)
+            else:
+                do(j)
+
+    fetches(0)
     load.wait()
 
     def prepare(i):
@@ -333,13 +356,7 @@
         acc[rows, :] = jnp.zeros((z.T3, z.D), f32)
 
     loop(0, z.T // z.T3, prepare)
-    fetch.start_a2(1)
-    fetch.start_a2(0, True)
-    fetch.start_b1(1)
-    fetch.start_d2(0)
-    fetch.start_c(0, True)
-    fetch.start_e(0)
-    fetch.start_a2(2)
+    fetches(1)
     n = z.T // z.TC
 
     def keep(j, i):
@@ -350,50 +367,25 @@
         for copy in keep(j, i):
             copy.wait()
 
-    def prefetch(j):
-        @pl.when(j == 0)
-        def _():
-            later.begin_local()
-            later.begin_pair()
-
-        @pl.when(j == 1)
-        def _():
-            later.end_pair()
-            later.start_a1(0, True)
-            later.start_d1(0)
-
-        @pl.when(j == 2)
-        def _():
-            later.start_a2(0, True)
-            later.start_d2(0)
-            for e in early[1:]:
-                later.start_a1(e, True)
-                later.start_d1(e)
-
-        @pl.when(j == 3)
-        def _():
-            later.start_c(0, True)
-            later.start_e(0)
-            for e in early[1:]:
-                later.start_a2(e, True)
-                later.start_d2(e)
-
-        @pl.when(j == 4)
-        def _():
-            for e in early[1:]:
-                later.start_c(e, True)
-                later.start_e(e)
+    def serve(j, middle):
+        for b in range(z.NB):
+            pl.when(j == b)(lambda b=b: fetches(2 + 2 * b + middle))
 
     def block(j):
-        fetch.serve_a(j)
+        serve(j, 0)
         fetch.ready(j)
         start([pltpu.make_async_copy(v.at[j], o.at[j], out_sem.at[k]) for k, (v, o) in enumerate(zip(w, w_out, strict=True))])
 
         def chunk(i):
             @pl.when(i == n // 2)
             def _():
-                fetch.serve_b(j)
-                prefetch(j)
+                serve(j, 1)
+
+                @pl.when(j == 0)
+                def _():
+                    later.begin_local()
+                    later.begin_pair()
+
 
             pl.when(j * n + i > 1)(lambda: kept(j, i))
             rows, slot = at(i * z.TC, z.TC), odd(i)
@@ -436,10 +428,10 @@
 class Reduce:
     PHASES = ("p", "x1", "x2", "y", "z", "az", "ay", "f")
 
-    def __init__(self, z, here, units, layer_first, outs, refs):
-        self.z, self.here, self.units, self.layer_first, self.outs = z, here, units, layer_first, outs
+    def __init__(self, z, here, units, base, outs, refs):
+        self.z, self.here, self.units, self.base, self.outs = z, here, units, base, outs
         (self.stage, self.got_p, self.got_x1, self.got_x2, self.got_y, self.got_z, self.send_x1, self.send_x2, self.send_y, self.send_z, *refs) = refs
-        (self.kept_x, self.kept_y, self.kept_z, self.fin, self.down, self.turned, self.out_sem, self.turned_sem, *refs) = refs
+        (self.kept_x, self.kept_y, self.kept_z, self.fin, self.down, self.turned, self.out_sem, self.turned_sem, self.piece_sem, *refs) = refs
         self.got = dict(zip(self.PHASES, refs[::2], strict=True))
         self.sent = dict(zip(self.PHASES, refs[1::2], strict=True))
 
@@ -453,8 +445,8 @@
             [VMEM(shape, bf16) for shape in data]
             + [VMEM(shape, f32) for shape in wide]
             + [VMEM((units, *unit), bf16), VMEM((units, CORES, Y, z.h, LANES), bf16), VMEM((2, LANES, z.D), bf16)]
-            + [DMA((2, units)), DMA((2, 2))]
-            + [DMA((units,)) for _ in range(2 * len(cls.PHASES))]
+            + [DMA((2, units)), DMA((2, 2)), DMA]
+            + [DMA((units + 3,)) for _ in range(2 * len(cls.PHASES))]
         )
 
     def peers(self):
@@ -463,91 +455,97 @@
             [here.partner()] + [here.along_x(k) for k in SIDES] + [here.along_y(k) for k in range(1, Y)] + [here.along_z(k) for k in range(1, here.Z)]
         )
 
-    def send(self, phase, u, src, dst, where):
-        remote(src, dst, self.sent[phase].at[u], self.got[phase].at[u], where).start()
-
-    def over(self, work, begin=0, end=Y):
-        matrices = len(self.outs)
-        loop(begin * matrices, end * matrices, lambda i: work(lax.div(i, matrices), lax.rem(i, matrices)))
-
-    def start_p(self, u):
-        here = self.here
+    def which(self, u, m):
+        return (u, ALL) if m is None else (self.units + m, m)
+
+    def send(self, phase, i, src, dst, where):
+        remote(src, dst, self.sent[phase].at[i], self.got[phase].at[i], where).start()
+
+    def over(self, m, work, begin=0, end=Y):
+        def share(y):
+            for k in range(len(self.outs)) if m is None else (m,):
+                work(y, k)
+
+        loop(begin, end, share)
+
+    def start_p(self, u, m=None):
+        here, (i, mm) = self.here, self.which(u, m)
         for x in range(X):
-            self.send("p", u, self.stage.at[odd(u), x, 1 - here.c], self.got_p.at[lax.rem(u, 3), x], here.partner())
+            self.send("p", i, self.stage.at[odd(u), x, 1 - here.c, :, mm], self.got_p.at[lax.rem(u, 3), x, :, mm], here.partner())
 
     def both(self, u, x, y, m):
         return self.stage[odd(u), x, self.here.c, y, m].astype(f32) + self.got_p[lax.rem(u, 3), x, y, m].astype(f32)
 
-    def start_x1(self, u):
-        here, half, slot = self.here, Y // 2, odd(u)
-        wait(self.got_p.at[lax.rem(u, 3)], self.got["p"].at[u])
+    def start_x1(self, u, m=None):
+        here, half, slot, (i, mm) = self.here, Y // 2, odd(u), self.which(u, m)
+        wait(self.got_p.at[lax.rem(u, 3), :, :, mm], self.got["p"].at[i])
         far = lax.rem(here.x + FAR, X)
 
-        def work(y, m):
-            self.send_x1[y, m] = self.both(u, far, y, m).astype(bf16)
-
-        self.over(work)
+        def work(y, k):
+            self.send_x1[y, k] = self.both(u, far, y, k).astype(bf16)
+
+        self.over(m, work)
         for side in range(2):
-            self.send("x1", u, self.send_x1.at[pl.ds(side * half, half)], self.got_x1.at[slot, side], here.along_x(SIDES[side]))
-
-    def start_x2(self, u):
-        here, half, slot = self.here, Y // 2, odd(u)
-        wait(self.got_x1.at[slot], self.got["x1"].at[u])
-        wait(self.got_x1.at[slot], self.sent["x1"].at[u])
-        wait(self.got_p.at[lax.rem(u, 3)], self.sent["p"].at[u])
+            self.send("x1", i, self.send_x1.at[pl.ds(side * half, half), mm], self.got_x1.at[slot, side, :, mm], here.along_x(SIDES[side]))
+
+    def start_x2(self, u, m=None):
+        here, half, slot, (i, mm) = self.here, Y // 2, odd(u), self.which(u, m)
+        wait(self.got_x1.at[slot, :, :, mm], self.got["x1"].at[i])
+        wait(self.got_x1.at[slot, :, :, mm], self.sent["x1"].at[i])
+        wait(self.got_p.at[lax.rem(u, 3), :, :, mm], self.sent["p"].at[i])
         right, left = here.right(), here.left()
 
-        def first(y, m):
-            self.send_x2[slot, 0, y, m] = (self.both(u, right, y, m) + self.got_x1[slot, 0, y, m].astype(f32)).astype(bf16)
-            self.send_x2[slot, 1, y, m] = self.both(u, left, y, m).astype(bf16)
-            self.kept_x[slot, y, m] = self.both(u, here.x, y, m)
-
-        def second(y, m):
-            self.send_x2[slot, 0, y, m] = self.both(u, right, y, m).astype(bf16)
-            self.send_x2[slot, 1, y, m] = (self.both(u, left, y, m) + self.got_x1[slot, 1, y - half, m].astype(f32)).astype(bf16)
-            self.kept_x[slot, y, m] = self.both(u, here.x, y, m)
-
-        self.over(first, 0, half)
-        self.over(second, half, Y)
+        def first(y, k):
+            self.send_x2[slot, 0, y, k] = (self.both(u, right, y, k) + self.got_x1[slot, 0, y, k].astype(f32)).astype(bf16)
+            self.send_x2[slot, 1, y, k] = self.both(u, left, y, k).astype(bf16)
+            self.kept_x[slot, y, k] = self.both(u, here.x, y, k)
+
+        def second(y, k):
+            self.send_x2[slot, 0, y, k] = self.both(u, right, y, k).astype(bf16)
+            self.send_x2[slot, 1, y, k] = (self.both(u, left, y, k) + self.got_x1[slot, 1, y - half, k].astype(f32)).astype(bf16)
+            self.kept_x[slot, y, k] = self.both(u, here.x, y, k)
+
+        self.over(m, first, 0, half)
+        self.over(m, second, half, Y)
         for side in range(2):
-            self.send("x2", u, self.send_x2.at[slot, side], self.got_x2.at[slot, side], here.along_x(SIDES[side]))
-
-    def start_y(self, u):
-        here, slot = self.here, odd(u)
-        wait(self.got_x2.at[slot], self.got["x2"].at[u])
-        wait(self.got_x2.at[slot], self.sent["x2"].at[u])
-
-        def total(y, m):
-            return self.kept_x[slot, y, m] + self.got_x2[slot, 0, y, m].astype(f32) + self.got_x2[slot, 1, y, m].astype(f32)
-
-        def work(y, m):
-            self.send_y[y, m] = total(y, m).astype(bf16)
-
-        def own(_, m):
-            self.kept_y[m] = total(here.y, m)
-
-        self.over(work)
-        self.over(own, 0, 1)
+            self.send("x2", i, self.send_x2.at[slot, side, :, mm], self.got_x2.at[slot, side, :, mm], here.along_x(SIDES[side]))
+
+    def start_y(self, u, m=None):
+        here, slot, (i, mm) = self.here, odd(u), self.which(u, m)
+        wait(self.got_x2.at[slot, :, :, mm], self.got["x2"].at[i])
+        wait(self.got_x2.at[slot, :, :, mm], self.sent["x2"].at[i])
+
+        def total(y, k):
+            return self.kept_x[slot, y, k] + self.got_x2[slot, 0, y, k].astype(f32) + self.got_x2[slot, 1, y, k].astype(f32)
+
+        def work(y, k):
+            self.send_y[y, k] = total(y, k).astype(bf16)
+
+        def own(_, k):
+            self.kept_y[k] = total(here.y, k)
+
+        self.over(m, work)
+        self.over(m, own, 0, 1)
         for k in (*SIDES, FAR):
-            self.send("y", u, self.send_y.at[lax.rem(here.y + k, Y)], self.got_y.at[slot, here.y], here.along_y(k))
-
-    def start_z(self, u):
-        z, here, slot = self.z, self.here, odd(u)
-        wait(self.got_y.at[slot, pl.ds(0, Y - 1)], self.got["y"].at[u])
-        wait(self.got_y.at[slot, pl.ds(0, Y - 1)], self.sent["y"].at[u])
-
-        def work(_, m):
-            total = self.kept_y[m]
-            for k in range(1, Y):
-                total += self.got_y[slot, lax.rem(here.y + k, Y), m].astype(f32)
-            self.kept_z[m] = total
-            self.send_z[m] = total.astype(bf16)
-
-        self.over(work, 0, 1)
+            self.send("y", i, self.send_y.at[lax.rem(here.y + k, Y), mm], self.got_y.at[slot, here.y, mm], here.along_y(k))
+
+    def start_z(self, u, m=None):
+        z, here, slot, (i, mm) = self.z, self.here, odd(u), self.which(u, m)
+        wait(self.got_y.at[slot, pl.ds(0, Y - 1), mm], self.got["y"].at[i])
+        wait(self.got_y.at[slot, pl.ds(0, Y - 1), mm], self.sent["y"].at[i])
+
+        def work(_, k):
+            total = self.kept_y[k]
+            for place in range(1, Y):
+                total += self.got_y[slot, lax.rem(here.y + place, Y), k].astype(f32)
+            self.kept_z[k] = total
+            self.send_z[k] = total.astype(bf16)
+
+        self.over(m, work, 0, 1)
 
         def send(k):
             to = lax.rem(here.z + k, z.Z)
-            pl.when(to < z.active)(lambda: self.send("z", u, self.send_z.at[:, at(to * 16, 16), :], self.got_z.at[u, here.z], here.along_z(k)))
+            pl.when(to < z.active)(lambda: self.send("z", i, self.send_z.at[mm, at(to * 16, 16), :], self.got_z.at[u, here.z, mm], here.along_z(k)))
 
         loop(1, z.Z, send)
 
@@ -555,48 +553,82 @@
         pl.when(self.here.z < self.z.active)(yes)
         pl.when(self.here.z >= self.z.active)(no)
 
-    def wait_pieces(self, u, n, sem):
+    def wait_pieces(self, i, mm, n, sem):
         if n:
-            wait(self.got_z.at[u, pl.ds(0, n)], sem.at[u])
-
-    def start_az(self, u):
-        z, here = self.z, self.here
+            wait(self.got_z.at[0, pl.ds(0, n), mm], sem.at[i])
+
+    def mine(self, mm):
+        return self.here.y, mm, at(self.here.z * 16, 16)
+
+    def add_pieces(self, u, m):
+        z, here, (i, mm) = self.z, self.here, self.which(u, m)
+        self.wait_pieces(i, mm, z.active - 1, self.sent["z"])
+        self.wait_pieces(i, mm, z.Z - 1, self.got["z"])
+        y, mm, rows = self.mine(mm)
+        total = self.kept_z[mm, rows, :]
+        for k in range(1, z.Z):
+            total += self.got_z[u, lax.rem(here.z + k, z.Z), mm].astype(f32)
+        self.fin[u, y, mm, rows, :] = total.astype(bf16)
+
+    def send_pieces(self, u, m=None):
+        i, mm = self.which(u, m)
+        y, mm, rows = self.mine(mm)
+        piece = self.fin.at[u, y, mm, rows, :]
+        loop(1, self.z.Z, lambda k: self.send("az", i, piece, piece, self.here.along_z(k)))
+
+    def start_az(self, u, m=None):
+        i, mm = self.which(u, m)
 
         def yes():
-            self.wait_pieces(u, z.active - 1, self.sent["z"])
-            self.wait_pieces(u, z.Z - 1, self.got["z"])
-            rows = at(here.z * 16, 16)
-            total = self.kept_z[:, rows, :]
-            for k in range(1, z.Z):
-                total += self.got_z[u, lax.rem(here.z + k, z.Z)].astype(f32)
-            self.fin[u, here.y, :, rows, :] = total.astype(bf16)
-            mine = self.fin.at[u, here.y, :, rows, :]
-
-            loop(1, z.Z, lambda k: self.send("az", u, mine, mine, here.along_z(k)))
-
-        self.if_active(yes, lambda: self.wait_pieces(u, z.active, self.sent["z"]))
-
-    def start_ay(self, u):
-        z, here = self.z, self.here
-        self.if_active(lambda: self.wait_pieces(u, z.active - 1, self.got["az"]), lambda: self.wait_pieces(u, z.active, self.got["az"]))
-        share = self.fin.at[u, here.y]
+            self.add_pieces(u, m)
+            self.send_pieces(u, m)
+
+        self.if_active(yes, lambda: self.wait_pieces(i, mm, self.z.active, self.sent["z"]))
+
+    def hand_on(self, u, out):
+        def yes():
+            self.add_pieces(u, None)
+            y, mm, rows = self.mine(ALL)
+            copy = pltpu.make_async_copy(self.fin.at[u, y, mm, rows, :], out, self.piece_sem)
+            copy.start()
+            copy.wait()
+
+        self.if_active(yes, lambda: self.wait_pieces(u, ALL, self.z.active, self.sent["z"]))
+
+    def take_over(self, u, piece):
+        def yes():
+            y, mm, rows = self.mine(ALL)
+            copy = pltpu.make_async_copy(piece, self.fin.at[u, y, mm, rows, :], self.piece_sem)
+            copy.start()
+            copy.wait()
+            self.send_pieces(u)
+
+        pl.when(self.here.z < self.z.active)(yes)
+
+    def start_ay(self, u, m=None):
+        z, here, (i, mm) = self.z, self.here, self.which(u, m)
+        self.if_active(lambda: self.wait_pieces(i, mm, z.active - 1, self.got["az"]), lambda: self.wait_pieces(i, mm, z.active, self.got["az"]))
+        share = self.fin.at[u, here.y, mm]
         for k in (*SIDES, FAR):
-            self.send("ay", u, share, share, here.along_y(k))
+            self.send("ay", i, share, share, here.along_y(k))
 
     def place(self, u):
         nb = self.z.NB
-        return (1, u) if self.layer_first else (1 - lax.div(u + nb - 1, nb), lax.rem(u + nb - 1, nb))
-
-    def start_f(self, u):
-        z, c = self.z, self.here.c
+        return (1, u) if self.base == 0 else (1 - lax.div(u + nb - self.base, nb), lax.rem(u + nb - self.base, nb))
+
+    def start_f(self, u, m=None):
+        z, c, (i, mm) = self.z, self.here.c, self.which(u, m)
         layer, j = self.place(u)
-        wait(self.fin.at[u, pl.ds(0, Y - 1)], self.got["ay"].at[u])
-        for m in range(2):
+        wait(self.fin.at[u, pl.ds(0, Y - 1), mm], self.got["ay"].at[i])
+        for k in range(2) if m is None else (m,):
+            if k == 2:
+                break
             for y in range(Y):
-                out = self.outs[m].at[layer, :, at((y * z.NB + j) * LANES, LANES, LANES)]
-                pltpu.make_async_copy(self.fin.at[u, y, m], out, self.out_sem.at[m, u]).start()
-        self.down[u, c] = self.fin[u, :, 2]
-        self.send("f", u, self.fin.at[u, :, 2], self.down.at[u, c], self.here.partner())
+                out = self.outs[k].at[layer, :, at((y * z.NB + j) * LANES, LANES, LANES)]
+                pltpu.make_async_copy(self.fin.at[u, y, k], out, self.out_sem.at[k, u]).start()
+        if m in (None, 2):
+            self.down[u, c] = self.fin[u, :, 2]
+            self.send("f", u, self.fin.at[u, :, 2], self.down.at[u, c], self.here.partner())
 
     def finish(self, u):
         z, c = self.z, self.here.c
@@ -618,18 +650,23 @@
                 out = self.outs[2].at[layer, at(lax.rem(row, z.NB) * 64, 64), :]
                 getattr(pltpu.make_async_copy(self.turned.at[odd(u), pl.ds(half * 64, 64), :], out, self.turned_sem.at[odd(u), half]), what)()
 
-    def end(self):
+    def end(self, units, in_parts):
         z = self.z
 
+        def sent_back(i, mm):
+            self.if_active(lambda: self.wait_pieces(i, mm, z.Z - 1, self.sent["az"]), lambda: None)
+            wait(self.fin.at[0, pl.ds(0, Y - 1), mm], self.sent["ay"].at[i])
+
         def one(u):
-            self.if_active(lambda: self.wait_pieces(u, z.Z - 1, self.sent["az"]), lambda: None)
-            wait(self.fin.at[u, pl.ds(0, Y - 1)], self.sent["ay"].at[u])
-            wait(self.down.at[u, 0], self.sent["f"].at[u])
+            wait(self.down.at[0, 0], self.sent["f"].at[u])
             for m in range(2):
-                wait(self.down.at[u, 0], self.out_sem.at[m, u])
-
-        loop(0, self.units, one)
-        for u in range(max(0, self.units - 2), self.units):
+                wait(self.down.at[0, 0], self.out_sem.at[m, u])
+
+        loop(0, units, one)
+        loop(0, units - in_parts, lambda u: sent_back(u, ALL))
+        for m in range(len(self.outs) if in_parts else 0):
+            sent_back(self.units + m, m)
+        for u in range(max(0, units - 2), units):
             self.turned_out(u, "wait")
 
 
@@ -646,12 +683,12 @@
     if first:
         early_in = take(3)
     else:
-        left_in, by_up_in, by_gate_in, act_in = take(4)
+        left_in, piece_in, by_up_in, by_gate_in, act_in = take(5)
         take(3)
     dx_out, *outs = take(4)
     spill = take(1)[0]
     if first:
-        left_out = take(1)[0]
+        left_out, piece_out = take(2)
     dx_buf, h_buf, a_t, dh, dh_t, wg, wu, wd, work = take(9)
     ld_sem, dh_sem, w_sem, sp_sem, s3_sem, o_sem, left_sem = take(7)
     if first:
@@ -661,9 +698,9 @@
     if first:
         fetch = Fetch(z, here, (w0.at[1], w1.at[1], w2.at[1]), (wg, wu, wd), take(len(Fetch.scratch(z))), z.early, NB)
         w0, w1, w2 = early_in
-    base = 0 if first else 1
-    units = NB - 1 if first else NB + 1
-    reduce = Reduce(z, here, units, first, outs, refs)
+    base = 0 if first else 2
+    units = NB - 1 if first else NB + base
+    reduce = Reduce(z, here, units, base, outs, refs)
     met = meet(reduce.peers())
     whole = pltpu.make_async_copy(dh_in, dh, dh_sem)
     whole.start()
@@ -693,7 +730,7 @@
         fetch.begin_pair()
         fetch.start_a1(z.early)
     else:
-        left = pltpu.make_async_copy(left_in, reduce.stage.at[0], left_sem)
+        left = pltpu.make_async_copy(left_in, reduce.stage.at[1], left_sem)
         left.start()
         for j in range(NB):
             start(loads(j)[2:])
@@ -717,7 +754,8 @@
     if not first:
         met()
         left.wait()
-        reduce.start_p(0)
+        reduce.start_p(1)
+        reduce.take_over(0, piece_in)
     loop(0, n3, prepare)
     if first:
         fetch.end_pair()
@@ -733,13 +771,16 @@
         for copy in spills(j):
             copy.wait()
 
-    def step(name, u):
+    def step(name, u, m=None):
         do = getattr(reduce, "start_" + name)
+        back = name in ("ay", "az")
+        begin = 0 if first or name == "ay" else 1
+        end = units - 1 if first and back else units
         if isinstance(u, int):
-            if 0 <= u < units:
-                do(u)
+            if begin <= u < end:
+                do(u, m)
         else:
-            pl.when(jnp.logical_and(u >= 0, u < units))(lambda: do(u))
+            pl.when(jnp.logical_and(u >= begin, u < end))(lambda: do(u))
 
     def halfway(i, n, before, after):
         if n == 1:
@@ -765,33 +806,20 @@
         pl.when(j > 0)(lambda: spilled(j - 1))
 
         def at_0():
-            if first:
-                step("ay", u - 3)
-                step("z", u - 2)
-            else:
-                step("x2", u - 1)
-                step("ay", u - 4)
+            step("x2", u - 1)
 
         def at_1():
-            if first:
-                step("x1", u)
-            else:
-                step("z", u - 3)
+            step("z", u - 2)
+            step("ay", u - 3)
 
         def at_2():
             if first:
                 fetch.serve_b(j)
-                step("y", u - 1)
-                step("az", u - 2)
-            else:
-                step("y", u - 2)
-                step("x1", u)
+            step("x1", u)
 
         def at_3():
-            if first:
-                step("x2", u)
-            else:
-                step("az", u - 3)
+            step("y", u - 1)
+            step("az", u - 2)
 
         def piece(i):
             halfway(i, T // TS, at_0, at_1)
@@ -841,7 +869,15 @@
                     stage[slot, x, i, y, 2] = downs[y * z.h : (y + 1) * z.h, x * LANES : (x + 1) * LANES]
 
         loop(0, 2, rows_of)
-        step("p", j + base)
+        if first:
+            step("p", j)
+        else:
+            pl.when(j + 1 < NB)(lambda: reduce.start_p(j + base))
+
+            @pl.when(j + 1 == NB)
+            def _():
+                for m in range(3):
+                    reduce.start_p(NB + base - 1, m)
 
     loop(0, NB, block)
     if first:
@@ -863,40 +899,36 @@
     start(load_3(0))
     u = NB + base - 1
     if first:
-        todo = [
-            [("ay", u - 3), ("z", u - 2)],
-            [("az", u - 2)],
-            [("y", u - 1)],
-            [("ay", u - 2)],
-            [("z", u - 1)],
-            [("az", u - 1)],
-            [("ay", u - 1)],
-        ]
-        rest = []
+        todo = ("x2:1", "z:2,ay:3", "", "az:2,y:1", "", "ay:2,z:1", "", "")
     else:
-        todo = [
-            [("x2", u - 1), ("ay", u - 4)],
-            [("z", u - 3), ("y", u - 2), ("x1", u)],
-            [],
-            [("az", u - 3)],
-            [("z", u - 2)],
-            [("x2", u), ("y", u - 1), ("ay", u - 3)],
-            [("az", u - 2)],
-        ]
-        rest = [("ay", u - 2), ("z", u - 1), ("y", u), ("az", u - 1), ("z", u), ("ay", u - 1), ("az", u), ("ay", u)]
-
-    done = u - 1 if first else u - 3
+        todo = (
+            "x2:1,ay:3",
+            "x1.0,x1.1,z:2",
+            "x1.2",
+            "x2.0,az:2,y:1,x2.1",
+            "x2.2,ay:2",
+            "z:1,y.0,y.1",
+            "y.2,az:1,z.0,z.1",
+            "z.2,ay:1,az.0",
+            "az.1,az.2,ay.0,ay.1,ay.2",
+        )
+
+    def steps(text):
+        for item in filter(None, text.split(",")):
+            name, _, behind = item.partition(":")
+            if behind:
+                step(name, u - int(behind))
+            else:
+                name, _, m = item.partition(".")
+                step(name, u, int(m))
+
+    done = units - 2 if first else units - 4
 
     def rows_back(i):
         slot, rows = odd(i), at(i * T3, T3)
         pl.when(i + 1 < n3)(lambda: start(load_3(i + 1)))
-        for when, steps in enumerate(todo):
-
-            def now(steps=steps):
-                for each in steps:
-                    step(*each)
-
-            pl.when(i == when)(now)
+        for when, text in enumerate(todo[:n3]):
+            pl.when(i == when)(lambda text=text: steps(text))
 
         @pl.when(i == n3 - 2)
         def _():
@@ -935,13 +967,20 @@
 
     loop(0, n3, rows_back)
     assert n3 == 8
-    for each in rest:
-        step(*each)
-    for v in range(max(done, 0), units):
-        reduce.start_f(v)
-    for v in range(max(done, 0), units):
+    for text in todo[n3:]:
+        steps(text)
+    if first:
+        reduce.hand_on(units - 1, piece_out)
+    back = units - 1 if first else units
+    for v in range(done, back):
+        if first or v + 1 < back:
+            reduce.start_f(v)
+        else:
+            for m in range(3):
+                reduce.start_f(v, m)
+    for v in range(done, back):
         reduce.finish(v)
-    reduce.end()
+    reduce.end(back, 0 if first else 1)
     if first:
         fetch.end(())
         left.wait()
@@ -977,7 +1016,7 @@
 def backward(z, h, dh, w, more, first):
     S = jax.ShapeDtypeStruct
     wide, tall, tokens = (z.NB, z.D, z.FB), (z.NB, z.FB, z.D), (z.T, z.D)
-    units = z.NB - 1 if first else z.NB + 1
+    units = z.NB - 1 if first else z.NB + 2
     scratch = [VMEM((2, z.T3, z.D), bf16), VMEM((2, z.T3, z.D), bf16)]
     scratch += [VMEM(tokens[::-1], bf16), VMEM(tokens, bf16), VMEM(tokens[::-1], bf16)]
     scratch += [VMEM(wide, bf16), VMEM(wide, bf16), VMEM(tall, bf16), VMEM((max(3 * z.T, 4 * z.NB * z.T3), z.FB), bf16)]
@@ -990,7 +1029,7 @@
     grads = [S((2, z.h, z.F), bf16), S((2, z.h, z.F), bf16), S((2, z.F // (X * CORES), z.D), bf16)]
     out = [S(tokens, bf16), *grads, S((2, z.NB, z.T, z.FB), bf16)]
     if first:
-        out.append(S((X, CORES, *z.unit), bf16))
+        out += [S((X, CORES, *z.unit), bf16), S((3, 16, LANES), bf16)]
     args = (h, dh, *w, *more)
     aliases = {} if first else {len(args) - 3 + i: 1 + i for i in range(3)}
     dx, g, u, d, _, *left = call(functools.partial(backward_kernel, z, first), out, len(args), scratch, 1 if first else 2, aliases)(*args)

time: 360 us -> 334 us (0.928)
  Pallas kernels: 351 us -> 325 us
    pallas_call x1, Pallas kernels: 84.3 us -> 70.8 us  [forward(): call(functools.partial(forward_kernel, z), out, 4, scratch, 0)(x, *shards)]
    pallas_call x2, Pallas kernels: 267 us -> 255 us  [backward(): call(functools.partial(backward_kernel, z, first), out, len(args), scratc...]
where the time goes in v5:
time: 334 us
  Pallas kernels  325 us (97%)
  local copies, waits for them, and re-layouts  7.94 us (2%)
    pallas_call x2, Pallas kernels, backward(): call(functools.partial(backward_kernel, z, first), out, len(args), scratc...  255 us
    pallas_call x1, Pallas kernels, forward(): call(functools.partial(forward_kernel, z), out, 4, scratch, 0)(x, *shards)  70.8 us
    unnamed x10, local copies, waits for them, and re-layouts  7.94 us

profile of v5, /device:TPU:1, one launch (start us, length us, event | category | flops | bytes accessed | tf_op | source)
XLA Modules:
  0.0 334.1 jit_solution(11358917134056423784)
XLA Ops:
  0.6 70.8 %shard_map.84 = (bf16[2048,896]{1,0:T(8,128)(2,1)}, bf16[5,896,512]{2,1,0:T(8,128)(2,1)}, bf16[5,896,512]{2,1,0:T(8,128)(2,1)}, bf16[5,512,896]{2,1,0:T(8,128)(2...) custom-call(bf16[2048,896]{1,0:T(8,128)(2,1)} %bitcast.3, ...), custom_call_target="tpu_custom_call" | custom-call | tf_op jit(solution)/shard_map/pallas_call | solution.py:1012
  71.4 125.0 %shard_map.85 = (bf16[2048,896]{1,0:T(8,128)(2,1)}, bf16[2,112,2560]{2,1,0:T(8,128)(2,1)}, bf16[2,112,2560]{2,1,0:T(8,128)(2,1)}, bf16[2,320,896]{2,1,0:T(8,128)...) custom-call(bf16[2048,896]{1,0:T(8,128)(2,1)} %get-tuple-element.24., ...), custom_call_target="tpu_custom_call" | custom-call | tf_op jit(solution)/shard_map/pallas_call | solution.py:1035
  196.4 129.7 %shard_map.86 = (bf16[2048,896]{1,0:T(8,128)(2,1)}, bf16[2,112,2560]{2,1,0:T(8,128)(2,1)}, bf16[2,112,2560]{2,1,0:T(8,128)(2,1)}, bf16[2,320,896]{2,1,0:T(8,128)(2,1)}, bf16[2,5,2048,512]{3,2,1,0:T(8,128)(2,1)}) custom-call(bf16[2048,896]{1,0:T(8,128)(2,1)} %bitcast.4, ...), custom_call_target="tpu_custom_call", output_to_operand_aliasing={{1}: (10, {}), {2}: (11, {}), {3}: (12, {})} | custom-call | tf_op jit(solution)/shard_map/pallas_call | solution.py:1035
  326.2 0.0 copy-start
  326.2 4.3 %copy.19 = bf16[1,2048,896]{2,1,0:T(8,128)(2,1)} copy(bf16[1,2048,896]{2,1,0:T(8,128)(2,1)} %bitcast.5) | data formatting | bytes 7340032
  330.4 0.0 copy-done
  330.4 0.0 copy-start.1
  330.4 0.0 copy-start.2
  330.4 1.0 copy.20
  331.4 0.7 copy-done.1
  332.1 1.0 copy.21
  333.1 0.0 copy-done.2
  333.1 1.0 copy.22
Async XLA Ops:
  326.2 4.3 %copy-start = (bf16[2,112,2560]{2,1,0:T(8,128)(2,1)S(1)}, bf16[2,112,2560]{2,1,0:T(8,128)(2,1)}, u32[]{:S(2)}) copy-start(bf16[2,112,2560]{2,1,0:T(8,128)(2,1)} %get-tuple-element.49) | copy-start | bytes 3440644
  330.4 1.7 copy-start.1
  330.4 2.7 copy-start.2

commit v6 on v5

--- a/solution.py
+++ b/solution.py
@@ -40,7 +40,7 @@
 
 
 class Sizes:
-    chunk, piece, rows = 1024, 512, 256
+    chunk, piece, rows, slots = 1024, 512, 256, 4
 
     def __init__(self, mesh, tokens, d, ff):
         self.R = mesh.shape["r"]
@@ -106,18 +106,18 @@
 
 
 FETCHES = (
-    "a10,a11,a12,d10,a21,a20",
-    "a22,b11,d20,d11,c0,b12,e0",
-    "a13,d12,b21,d21,a23,d13",
-    "e1,c1,a14,b13,d22,d14",
-    "a24,d23,b22,La11,e2",
-    "c2,d24,Ld10,Ld11,b23,b14",
-    "e3",
-    "c3,b24,La10",
-    "e4,La21,c4,Ld21",
-    "Ld20",
-    "La20,Lc1,Le1",
-    "Le0,Lc0",
+    "a10,a11,a20,d10,b10,d11,a21",
+    "d20,a12,a14,b20,a13,e0,b11,d21,c0,a22,d12",
+    "e1,a23,d13,a24,b21,b12",
+    "d22,c1,d14,b13",
+    "d23,La11,e2,La10,b22",
+    "b23,b14,La21,d24,c2,Ld10,Ld11",
+    "e4,c3,Lb11",
+    "e3,La20,Ld21,b24",
+    "Lb10",
+    "Ld20,c4,Lb21",
+    "Lb20,Le0,Le1,Lc1",
+    "Lc0",
 )
 
 
@@ -197,21 +197,21 @@
 
         self.each_core(do)
 
-    def start_a1(self, j, alone=False):
+    def start_a1(self, j):
         here = self.here
         wait(self.pieces(j, 8), self.local.at[j])
         for k in SIDES:
             for w in range(2):
-                self.send("a1", j, w, self.rows(here.x), ALL if alone else self.lanes(here.y), here.along_x(k))
+                self.send("a1", j, w, self.rows(here.x), self.lanes(here.y), here.along_x(k))
 
     def start_d1(self, j):
         for k in SIDES:
             self.send("d1", j, 2, self.down(self.here.x), ALL, self.here.along_x(k))
 
-    def start_a2(self, j, alone=False):
+    def start_a2(self, j):
         here = self.here
-        wait(self.pieces(j, 16 if alone else 4), self.got["a1"].at[j])
-        lanes = ALL if alone else self.lanes(here.y)
+        wait(self.pieces(j, 4), self.got["a1"].at[j])
+        lanes = self.lanes(here.y)
         self.send("a2", j, 0, self.rows(here.left()), lanes, here.along_x(RIGHT))
         self.send("a2", j, 1, self.rows(here.right()), lanes, here.along_x(LEFT))
 
@@ -237,11 +237,8 @@
             self.send("b2", j, 0, rows, self.lanes(lax.rem(here.y + LEFT, Y)), here.along_y(RIGHT))
             self.send("b2", j, 1, rows, self.lanes(lax.rem(here.y + RIGHT, Y)), here.along_y(LEFT))
 
-    def start_c(self, j, alone=False):
-        if alone:
-            wait(self.pieces(j, 8), self.got["a2"].at[j])
-        else:
-            wait(self.pieces(j, 6), self.got["b2"].at[j])
+    def start_c(self, j):
+        wait(self.pieces(j, 6), self.got["b2"].at[j])
         for w in range(2):
             for x in range(X):
                 self.send("c", j, w, self.rows(x), ALL, self.here.partner())
@@ -286,23 +283,17 @@
     def if_mine(self, j):
         return pl.when(jnp.logical_and(j >= self.first, j < self.last))
 
-    def end(self, alone):
+    def end(self):
         self.each_core(lambda mine, _: self.wait_parts(len(mine), self.pair_sent))
 
-        def drain(j, alone=False):
-            wait(self.pieces(j, 16 if alone else 4), self.sent["a1"].at[j])
-            wait(self.pieces(j, 8 if alone else 2), self.sent["a2"].at[j])
-            if not alone:
-                wait(self.pieces(j, 12), self.sent["b1"].at[j])
-                wait(self.pieces(j, 6), self.sent["b2"].at[j])
-            wait(self.halves(j, 2), self.sent["d1"].at[j])
-            wait(self.halves(j, 1), self.sent["d2"].at[j])
+        def drain(j):
+            for phase, n in (("a1", 4), ("a2", 2), ("b1", 12), ("b2", 6)):
+                wait(self.pieces(j, n), self.sent[phase].at[j])
+            for phase, n in (("d1", 2), ("d2", 1), ("e", 3)):
+                wait(self.halves(j, n), self.sent[phase].at[j])
             wait(self.w[0].at[j], self.sent["c"].at[j])
-            wait(self.halves(j, 3), self.sent["e"].at[j])
-
-        for j in alone:
-            drain(j, True)
-        loop(self.first + len(alone), self.last, drain)
+
+        loop(self.first, self.last, drain)
 
 
 def normed(wide):
@@ -317,13 +308,14 @@
         out, refs[:] = refs[:n], refs[n:]
         return out
 
-    x_in, *shards = take(4)
+    x_in, dy_in, *shards = take(5)
     h_out, *w_out = take(4)
-    kept_out, next_out = take(3), take(3)
-    a, acc, xs = take(3)
+    kept_out, next_out, turned_out = take(3), take(3), take(2)
+    a, acc, xs, dy_buf = take(4)
+    turned = take(2)
     parts, w, w_next = take(3), take(3), take(3)
     act, by_up, by_gate = parts
-    x_sem, out_sem, next_sem, h_sem, keep_sem = take(5)
+    x_sem, out_sem, next_sem, h_sem, keep_sem, dy_sem, turned_sem = take(7)
     n_sems = len(Fetch.scratch(z))
     here = Here(z)
     fetch = Fetch(z, here, [v.at[0] for v in shards], w, take(n_sems), 0, z.NB)
@@ -341,21 +333,29 @@
             who, phase, j = (later if item[0] == "L" else fetch), item.strip("L")[:-1], int(item[-1])
             if phase == "d1" and j == 0:
                 who.end_pair()
-            do = getattr(who, "start_" + phase)
-            if phase in ("a1", "a2", "c"):
-                do(j, alone=who is later or j == 0)
-            else:
-                do(j)
+            getattr(who, "start_" + phase)(j)
 
     fetches(0)
     load.wait()
 
+    def load_dy(i):
+        return pltpu.make_async_copy(dy_in.at[at(i * z.T3, z.T3), :], dy_buf.at[odd(i)], dy_sem.at[odd(i)])
+
+    load_dy(0).start()
+
     def prepare(i):
-        rows = at(i * z.T3, z.T3)
-        a[rows, :] = normed(xs[rows, :].astype(f32))[0]
+        rows = at(i * z.T3, z.T3, LANES)
+        pl.when(i + 1 < z.T // z.T3)(lambda: load_dy(i + 1).start())
+        value = normed(xs[rows, :].astype(f32))[0]
+        a[rows, :] = value
         acc[rows, :] = jnp.zeros((z.T3, z.D), f32)
+        load_dy(i).wait()
+        for v, part in zip(turned, (value, dy_buf[odd(i)]), strict=True):
+            v[:, rows] = part.T
 
     loop(0, z.T // z.T3, prepare)
+    turn = [pltpu.make_async_copy(v, o, turned_sem.at[k]) for k, (v, o) in enumerate(zip(turned, turned_out, strict=True))]
+    start(turn)
     fetches(1)
     n = z.T // z.TC
 
@@ -418,10 +418,10 @@
         kept(z.NB - 1, n - 2 + i)
     for k, v in enumerate(w):
         wait(v, out_sem.at[k])
-    fetch.end((0,))
-    later.end(early)
+    fetch.end()
+    later.end()
     store.wait()
-    for copy in handed:
+    for copy in (*handed, *turn):
         copy.wait()
 
 
@@ -468,10 +468,18 @@
 
         loop(begin, end, share)
 
-    def start_p(self, u, m=None):
-        here, (i, mm) = self.here, self.which(u, m)
-        for x in range(X):
+    def start_p(self, u, m=None, places=range(X)):
+        here, (i, mm) = self.here, self.which(u, None if isinstance(m, slice) else m)
+        mm = m if isinstance(m, slice) else mm
+        for x in places:
             self.send("p", i, self.stage.at[odd(u), x, 1 - here.c, :, mm], self.got_p.at[lax.rem(u, 3), x, :, mm], here.partner())
+
+    def start_early_p(self, u):
+        self.start_p(u, slice(0, 2), range(2))
+
+    def start_late_p(self, u):
+        self.start_p(u, slice(0, 2), range(2, X))
+        self.start_p(u, slice(2, 3))
 
     def both(self, u, x, y, m):
         return self.stage[odd(u), x, self.here.c, y, m].astype(f32) + self.got_p[lax.rem(u, 3), x, y, m].astype(f32)
@@ -679,20 +687,20 @@
         out, refs[:] = refs[:n], refs[n:]
         return out
 
-    h_in, dh_in, w0, w1, w2 = take(5)
+    h_in, dh_in, dh_t_in, w0, w1, w2 = take(6)
     if first:
         early_in = take(3)
     else:
-        left_in, piece_in, by_up_in, by_gate_in, act_in = take(5)
+        left_in, piece_in, by_up_in, by_gate_in, act_in, a_t_in = take(6)
         take(3)
     dx_out, *outs = take(4)
     spill = take(1)[0]
     if first:
-        left_out, piece_out = take(2)
+        left_out, piece_out, dx_t_out = take(3)
     dx_buf, h_buf, a_t, dh, dh_t, wg, wu, wd, work = take(9)
-    ld_sem, dh_sem, w_sem, sp_sem, s3_sem, o_sem, left_sem = take(7)
-    if first:
-        a = take(1)[0]
+    ld_sem, dh_sem, w_sem, sp_sem, s3_sem, o_sem, left_sem, turned_sem = take(8)
+    if first:
+        a, dx_t_buf, dx_t_sem = take(3)
     else:
         saved, saved_sem, act_sem = take(3)
     if first:
@@ -708,12 +716,17 @@
     def load_h(i):
         return pltpu.make_async_copy(h_in.at[at(i * T3, T3), :], h_buf.at[odd(i)], ld_sem.at[odd(i)])
 
-    load_h(0).start()
+    turn = [pltpu.make_async_copy(dh_t_in, dh_t, turned_sem.at[0])]
+    if first:
+        load_h(0).start()
+        start(turn)
+    else:
+        turn.append(pltpu.make_async_copy(a_t_in, a_t, turned_sem.at[1]))
 
     def loads(j):
         return [pltpu.make_async_copy(src.at[j], dst.at[j], w_sem.at[k, j]) for k, (src, dst) in enumerate(((w0, wg), (w1, wu), (w2, wd)))]
 
-    TS, slots = z.TS, 3
+    TS, slots = z.TS, z.slots
 
     def load_saved(q):
         j, rows, slot = lax.div(q, T // TS), at(lax.rem(q, T // TS) * TS, TS), lax.rem(q, slots)
@@ -732,10 +745,12 @@
     else:
         left = pltpu.make_async_copy(left_in, reduce.stage.at[1], left_sem)
         left.start()
-        for j in range(NB):
+        start(loads(0)[2:])
+        for q in range(slots - 1):
+            start(load_saved(q))
+        start(turn)
+        for j in range(1, NB):
             start(loads(j)[2:])
-        for q in range(2):
-            start(load_saved(q))
         for j in range(NB):
             start(loads(j)[:2])
     whole.wait()
@@ -746,18 +761,21 @@
         pl.when(i + 1 < n3)(lambda: load_h(i + 1).start())
         load_h(i).wait()
         value = normed(h_buf[odd(i)].astype(f32))[0]
-        if first:
-            a[rows, :] = value
+        a[rows, :] = value
         a_t[:, rows] = value.T
-        dh_t[:, rows] = dh[rows, :].T
 
     if not first:
         met()
         left.wait()
         reduce.start_p(1)
         reduce.take_over(0, piece_in)
-    loop(0, n3, prepare)
-    if first:
+    def turned():
+        for copy in turn:
+            copy.wait()
+
+    if first:
+        loop(0, n3, prepare)
+        turned()
         fetch.end_pair()
         fetch.start_a2(z.early)
 
@@ -815,16 +833,22 @@
         def at_2():
             if first:
                 fetch.serve_b(j)
+            else:
+                pl.when(j == 0)(turned)
             step("x1", u)
 
         def at_3():
+            if first:
+                step("early_p", j)
+            else:
+                pl.when(j + 1 < NB)(lambda: reduce.start_early_p(j + base))
             step("y", u - 1)
             step("az", u - 2)
 
         def piece(i):
             halfway(i, T // TS, at_0, at_1)
             q, rows = j * (T // TS) + i, at(i * TS, TS)
-            pl.when(q + 2 < NB * (T // TS))(lambda: start(load_saved(q + 2)))
+            pl.when(q + slots - 1 < NB * (T // TS))(lambda: start(load_saved(q + slots - 1)))
             for copy in load_saved(q):
                 copy.wait()
             by_act = dot(dh[rows, :], wd[j], ((1,), (1,))).astype(bf16).astype(f32)
@@ -870,9 +894,9 @@
 
         loop(0, 2, rows_of)
         if first:
-            step("p", j)
+            step("late_p", j)
         else:
-            pl.when(j + 1 < NB)(lambda: reduce.start_p(j + base))
+            pl.when(j + 1 < NB)(lambda: reduce.start_late_p(j + base))
 
             @pl.when(j + 1 == NB)
             def _():
@@ -895,6 +919,9 @@
 
     def store_3(i):
         return pltpu.make_async_copy(dx_buf.at[odd(i)], dx_out.at[at(i * T3, T3), :], o_sem.at[odd(i)])
+
+    def store_turned(i):
+        return pltpu.make_async_copy(dx_t_buf.at[odd(i)], dx_t_out.at[:, at(i * T3, T3, LANES)], dx_t_sem.at[odd(i)])
 
     start(load_3(0))
     u = NB + base - 1
@@ -964,6 +991,10 @@
         by_square = by_scale * (-0.5 * scale / square) * (2.0 / D)
         dx_buf[slot] = dh[rows, :] + (by_a * scale + by_square * wide).astype(bf16)
         store_3(i).start()
+        if first:
+            pl.when(i > 1)(lambda: store_turned(i - 2).wait())
+            dx_t_buf[slot] = dx_buf[slot].T
+            store_turned(i).start()
 
     loop(0, n3, rows_back)
     assert n3 == 8
@@ -982,10 +1013,12 @@
         reduce.finish(v)
     reduce.end(back, 0 if first else 1)
     if first:
-        fetch.end(())
+        fetch.end()
         left.wait()
     for i in range(max(0, n3 - 2), n3):
         store_3(i).wait()
+        if first:
+            store_turned(i).wait()
 
 
 def call(body, out, n_in, scratch, number, aliases=()):
@@ -1000,37 +1033,38 @@
     )
 
 
-def forward(z, x, shards):
+def forward(z, x, dy, shards):
     S = jax.ShapeDtypeStruct
     wide, tall, tokens, hidden, piece = (z.NB, z.D, z.FB), (z.NB, z.FB, z.D), (z.T, z.D), (z.NB, z.T, z.FB), (2, z.TC, z.FB)
-    scratch = [VMEM(tokens, bf16), VMEM(tokens, f32), VMEM(tokens, bf16), VMEM(piece, bf16), VMEM(piece, f32), VMEM(piece, f32)]
+    scratch = [VMEM(tokens, bf16), VMEM(tokens, f32), VMEM(tokens, bf16), VMEM((2, z.T3, z.D), bf16), VMEM(tokens[::-1], bf16), VMEM(tokens[::-1], bf16)]
+    scratch += [VMEM(piece, bf16), VMEM(piece, f32), VMEM(piece, f32)]
     early = [(z.early, *shape[1:]) for shape in (wide, wide, tall)]
     scratch += [VMEM(shape, bf16) for shape in (wide, wide, tall, *early)]
-    scratch += [DMA, DMA((3,)), DMA((3,)), DMA, DMA((3, 2))] + Fetch.scratch(z) + Fetch.scratch(z)
+    scratch += [DMA, DMA((3,)), DMA((3,)), DMA, DMA((3, 2)), DMA((2,)), DMA((2,))] + Fetch.scratch(z) + Fetch.scratch(z)
     out = [S(tokens, bf16), S(wide, bf16), S(wide, bf16), S(tall, bf16), S(hidden, bf16), S(hidden, f32), S(hidden, f32)]
-    out += [S(shape, bf16) for shape in early]
-    h, *out = call(functools.partial(forward_kernel, z), out, 4, scratch, 0)(x, *shards)
-    return h, out[:3], out[3:6], out[6:]
-
-
-def backward(z, h, dh, w, more, first):
+    out += [S(shape, bf16) for shape in (*early, tokens[::-1], tokens[::-1])]
+    h, *out = call(functools.partial(forward_kernel, z), out, 5, scratch, 0)(x, dy, *shards)
+    return h, out[:3], out[3:6], out[6:9], out[9:]
+
+
+def backward(z, h, dh, dh_t, w, more, first):
     S = jax.ShapeDtypeStruct
     wide, tall, tokens = (z.NB, z.D, z.FB), (z.NB, z.FB, z.D), (z.T, z.D)
     units = z.NB - 1 if first else z.NB + 2
     scratch = [VMEM((2, z.T3, z.D), bf16), VMEM((2, z.T3, z.D), bf16)]
     scratch += [VMEM(tokens[::-1], bf16), VMEM(tokens, bf16), VMEM(tokens[::-1], bf16)]
     scratch += [VMEM(wide, bf16), VMEM(wide, bf16), VMEM(tall, bf16), VMEM((max(3 * z.T, 4 * z.NB * z.T3), z.FB), bf16)]
-    scratch += [DMA((2,)), DMA, DMA((3, z.NB)), DMA((2,)), DMA((2,)), DMA((2,)), DMA]
-    if first:
-        scratch += [VMEM(tokens, bf16)] + Fetch.scratch(z)
+    scratch += [DMA((2,)), DMA, DMA((3, z.NB)), DMA((2,)), DMA((2,)), DMA((2,)), DMA, DMA((2,))]
+    if first:
+        scratch += [VMEM(tokens, bf16), VMEM((2, z.D, z.T3), bf16), DMA((2,))] + Fetch.scratch(z)
     else:
-        scratch += [VMEM((3, 2, z.TS, z.FB), f32), DMA((2, 3)), DMA]
+        scratch += [VMEM((z.slots, 2, z.TS, z.FB), f32), DMA((2, z.slots)), DMA]
     scratch += Reduce.scratch(z, units)
     grads = [S((2, z.h, z.F), bf16), S((2, z.h, z.F), bf16), S((2, z.F // (X * CORES), z.D), bf16)]
     out = [S(tokens, bf16), *grads, S((2, z.NB, z.T, z.FB), bf16)]
     if first:
-        out += [S((X, CORES, *z.unit), bf16), S((3, 16, LANES), bf16)]
-    args = (h, dh, *w, *more)
+        out += [S((X, CORES, *z.unit), bf16), S((3, 16, LANES), bf16), S(tokens[::-1], bf16)]
+    args = (h, dh, dh_t, *w, *more)
     aliases = {} if first else {len(args) - 3 + i: 1 + i for i in range(3)}
     dx, g, u, d, _, *left = call(functools.partial(backward_kernel, z, first), out, len(args), scratch, 1 if first else 2, aliases)(*args)
     return dx, (g, u, d), left
@@ -1039,9 +1073,9 @@
 def solution(mesh):
     def step(x, dy, *weights):
         z = Sizes(mesh, x.shape[1], x.shape[2], weights[0].shape[2])
-        h, w, (act, by_up, by_gate), early = forward(z, x[0], weights)
-        dh, grads, left = backward(z, h, dy[0], weights, early, True)
-        dx, grads, _ = backward(z, x[0], dh, w, (*left, by_up, by_gate, act, *grads), False)
+        h, w, (act, by_up, by_gate), early, (a_t, dy_t) = forward(z, x[0], dy[0], weights)
+        dh, grads, (left, piece, dh_t) = backward(z, h, dy[0], dy_t, weights, early, True)
+        dx, grads, _ = backward(z, x[0], dh, dh_t, w, (left, piece, by_up, by_gate, act, a_t, *grads), False)
         return dx[None], *grads
 
     states, cut = P(("rep", "r", "s"), None, None), P(None, "s", None)

time: 334 us -> 334 us (level)
  no operation moved by 1% of the time
where the time goes in v6:
time: 334 us
  Pallas kernels  326 us (98%)
  local copies, waits for them, and re-layouts  7.34 us (2%)
    pallas_call x2, Pallas kernels, backward(): call(functools.partial(backward_kernel, z, first), out, len(args), scratc...  252 us
    pallas_call x1, Pallas kernels, forward(): call(functools.partial(forward_kernel, z), out, 5, scratch, 0)  73.8 us
    unnamed x10, local copies, waits for them, and re-layouts  7.34 us

profile of v6, /device:TPU:1, one launch (start us, length us, event | category | flops | bytes accessed | tf_op | source)
XLA Modules:
  0.0 334.0 jit_solution(14531029542824461976)
XLA Ops:
  0.6 73.8 %shard_map.84 = (bf16[2048,896]{1,0:T(8,128)(2,1)}, bf16[5,896,512]{2,1,0:T(8,128)(2,1)}, bf16[5,896,512]{2,1,0:T(8,128)(2,1)}, bf16[5,512,896]{2,1,0:T(8,128)(2...) custom-call(bf16[2048,896]{1,0:T(8,128)(2,1)} %bitcast.5, ...), custom_call_target="tpu_custom_call" | custom-call | tf_op jit(solution)/shard_map/pallas_call | solution.py:1046
  74.4 125.8 %shard_map.85 = (bf16[2048,896]{1,0:T(8,128)(2,1)}, bf16[2,112,2560]{2,1,0:T(8,128)(2,1)}, bf16[2,112,2560]{2,1,0:T(8,128)(2,1)}, bf16[2,320,896]{2,1,0:T(8,128)...) custom-call(bf16[2048,896]{1,0:T(8,128)(2,1)} %get-tuple-element.27., ...), custom_call_target="tpu_custom_call" | custom-call | tf_op jit(solution)/shard_map/pallas_call | solution.py:1069
  200.2 126.4 %shard_map.86 = (bf16[2048,896]{1,0:T(8,128)(2,1)}, bf16[2,112,2560]{2,1,0:T(8,128)(2,1)}, bf16[2,112,2560]{2,1,0:T(8,128)(2,1)}, bf16[2,320,896]{2,1,0:T(8,128)(2,1)}, bf16[2,5,2048,512]{3,2,1,0:T(8,128)(2,1)}) custom-call(bf16[2048,896]{1,0:T(8,128)(2,1)} %bitcast.6, ...), custom_call_target="tpu_custom_call", output_to_operand_aliasing={{1}: (12, {}), {2}: (13, {}), {3}: (14, {})} | custom-call | tf_op jit(solution)/shard_map/pallas_call | solution.py:1069
  326.7 0.0 copy-start
  326.7 0.0 copy-start.1
  326.7 4.3 %copy.19 = bf16[1,2048,896]{2,1,0:T(8,128)(2,1)} copy(bf16[1,2048,896]{2,1,0:T(8,128)(2,1)} %bitcast.7) | data formatting | bytes 7340032
  331.0 0.0 copy-done
  331.0 0.0 copy-start.2
  331.0 1.0 copy.20
  332.0 0.0 copy-done.1
  332.0 1.0 copy.21
  333.0 0.0 copy-done.2
  333.0 1.0 copy.22
Async XLA Ops:
  326.7 4.3 %copy-start = (bf16[2,112,2560]{2,1,0:T(8,128)(2,1)S(1)}, bf16[2,112,2560]{2,1,0:T(8,128)(2,1)}, u32[]{:S(2)}) copy-start(bf16[2,112,2560]{2,1,0:T(8,128)(2,1)} %get-tuple-element.55) | copy-start | bytes 3440644
  326.7 5.3 %copy-start.1 = (bf16[2,112,2560]{2,1,0:T(8,128)(2,1)S(1)}, bf16[2,112,2560]{2,1,0:T(8,128)(2,1)}, u32[]{:S(2)}) copy-start(bf16[2,112,2560]{2,1,0:T(8,128)(2,1)} %get-tuple-element.56) | copy-start | bytes 3440644
  331.0 2.0 copy-start.2

commit v7 on v6

--- a/solution.py
+++ b/solution.py
@@ -127,8 +127,8 @@
     def __init__(self, z, here, shards, w, sems, begin, end):
         self.z, self.here, self.shards, self.w, self.first, self.last = z, here, shards, w, begin, end
         self.local, self.local_d, self.pair, self.pair_sent = sems[:4]
-        self.got = dict(zip(self.PHASES, sems[4::2], strict=True))
-        self.sent = dict(zip(self.PHASES, sems[5::2], strict=True))
+        self.got = dict(zip(self.PHASES, sems[4::2]))
+        self.sent = dict(zip(self.PHASES, sems[5::2]))
         self.parts = [[k for k in range(z.NB) if begin <= (c * z.NB + k) // 2 < end] for c in range(CORES)]
 
     @classmethod
@@ -141,7 +141,7 @@
 
     def own(self, j):
         z, here = self.z, self.here
-        for shard, w in zip(self.shards[:2], self.w[:2], strict=True):
+        for shard, w in zip(self.shards[:2], self.w[:2]):
             for l in range(X):
                 slot = w.at[j, self.rows(here.x), pl.ds(l * LANES, LANES)]
                 pltpu.make_async_copy(shard.at[:, at((l * z.NB + j) * LANES, LANES, LANES)], slot, self.local.at[j]).start()
@@ -342,26 +342,31 @@
         return pltpu.make_async_copy(dy_in.at[at(i * z.T3, z.T3), :], dy_buf.at[odd(i)], dy_sem.at[odd(i)])
 
     load_dy(0).start()
+    n3 = z.T // z.T3
 
     def prepare(i):
+        rows = at(i * z.T3, z.T3)
+        a[rows, :] = normed(xs[rows, :].astype(f32))[0]
+        acc[rows, :] = jnp.zeros((z.T3, z.D), f32)
+
+    loop(0, n3, prepare)
+    fetches(1)
+
+    def turn(i):
         rows = at(i * z.T3, z.T3, LANES)
-        pl.when(i + 1 < z.T // z.T3)(lambda: load_dy(i + 1).start())
-        value = normed(xs[rows, :].astype(f32))[0]
-        a[rows, :] = value
-        acc[rows, :] = jnp.zeros((z.T3, z.D), f32)
+        pl.when(i + 1 < n3)(lambda: load_dy(i + 1).start())
         load_dy(i).wait()
-        for v, part in zip(turned, (value, dy_buf[odd(i)]), strict=True):
+        for v, part in zip(turned, (a[rows, :], dy_buf[odd(i)])):
             v[:, rows] = part.T
 
-    loop(0, z.T // z.T3, prepare)
-    turn = [pltpu.make_async_copy(v, o, turned_sem.at[k]) for k, (v, o) in enumerate(zip(turned, turned_out, strict=True))]
-    start(turn)
-    fetches(1)
+    loop(0, n3, turn)
+    sent = [pltpu.make_async_copy(v, o, turned_sem.at[k]) for k, (v, o) in enumerate(zip(turned, turned_out))]
+    start(sent)
     n = z.T // z.TC
 
     def keep(j, i):
         slot = odd(i)
-        return [pltpu.make_async_copy(v.at[slot], o.at[j, at(i * z.TC, z.TC), :], keep_sem.at[k, slot]) for k, (v, o) in enumerate(zip(parts, kept_out, strict=True))]
+        return [pltpu.make_async_copy(v.at[slot], o.at[j, at(i * z.TC, z.TC), :], keep_sem.at[k, slot]) for k, (v, o) in enumerate(zip(parts, kept_out))]
 
     def kept(j, i):
         for copy in keep(j, i):
@@ -374,7 +379,7 @@
     def block(j):
         serve(j, 0)
         fetch.ready(j)
-        start([pltpu.make_async_copy(v.at[j], o.at[j], out_sem.at[k]) for k, (v, o) in enumerate(zip(w, w_out, strict=True))])
+        start([pltpu.make_async_copy(v.at[j], o.at[j], out_sem.at[k]) for k, (v, o) in enumerate(zip(w, w_out))])
 
         def chunk(i):
             @pl.when(i == n // 2)
@@ -412,7 +417,7 @@
     store.start()
     for e in early:
         later.ready(e)
-    handed = [pltpu.make_async_copy(v, o, next_sem.at[k]) for k, (v, o) in enumerate(zip(w_next, next_out, strict=True))]
+    handed = [pltpu.make_async_copy(v, o, next_sem.at[k]) for k, (v, o) in enumerate(zip(w_next, next_out))]
     start(handed)
     for i in range(2):
         kept(z.NB - 1, n - 2 + i)
@@ -421,7 +426,7 @@
     fetch.end()
     later.end()
     store.wait()
-    for copy in (*handed, *turn):
+    for copy in (*handed, *sent):
         copy.wait()
 
 
@@ -432,8 +437,8 @@
         self.z, self.here, self.units, self.base, self.outs = z, here, units, base, outs
         (self.stage, self.got_p, self.got_x1, self.got_x2, self.got_y, self.got_z, self.send_x1, self.send_x2, self.send_y, self.send_z, *refs) = refs
         (self.kept_x, self.kept_y, self.kept_z, self.fin, self.down, self.turned, self.out_sem, self.turned_sem, self.piece_sem, *refs) = refs
-        self.got = dict(zip(self.PHASES, refs[::2], strict=True))
-        self.sent = dict(zip(self.PHASES, refs[1::2], strict=True))
+        self.got = dict(zip(self.PHASES, refs[::2]))
+        self.sent = dict(zip(self.PHASES, refs[1::2]))
 
     @classmethod
     def scratch(cls, z, units):
@@ -719,7 +724,6 @@
     turn = [pltpu.make_async_copy(dh_t_in, dh_t, turned_sem.at[0])]
     if first:
         load_h(0).start()
-        start(turn)
     else:
         turn.append(pltpu.make_async_copy(a_t_in, a_t, turned_sem.at[1]))
 
@@ -736,8 +740,7 @@
         return pltpu.make_async_copy(act_in.at[j], work.at[pl.ds(0, T), :], act_sem)
 
     if first:
-        for j in range(z.early):
-            start(loads(j))
+        start(loads(0))
         fetch.begin_local()
         met()
         fetch.begin_pair()
@@ -748,12 +751,10 @@
         start(loads(0)[2:])
         for q in range(slots - 1):
             start(load_saved(q))
+        load_act(0).start()
         start(turn)
         for j in range(1, NB):
             start(loads(j)[2:])
-        for j in range(NB):
-            start(loads(j)[:2])
-    whole.wait()
     n3 = T // T3
 
     def prepare(i):
@@ -775,7 +776,9 @@
 
     if first:
         loop(0, n3, prepare)
-        turned()
+        for j in range(1, z.early):
+            start(loads(j))
+        start(turn)
         fetch.end_pair()
         fetch.start_a2(z.early)
 
@@ -808,6 +811,8 @@
             pl.when(i == 0)(before)
             pl.when(i == n // 2)(after)
 
+    whole.wait()
+
     def loaded(j):
         for copy in loads(j):
             copy.wait()
@@ -819,7 +824,7 @@
             pl.when(j < z.early)(lambda: loaded(j))
             pl.when(j >= z.early)(lambda: fetch.ready(j))
         else:
-            load_act(j).start()
+            pl.when(j > 0)(lambda: load_act(j).start())
             loads(j)[2].wait()
         pl.when(j > 0)(lambda: spilled(j - 1))
 
@@ -833,8 +838,7 @@
         def at_2():
             if first:
                 fetch.serve_b(j)
-            else:
-                pl.when(j == 0)(turned)
+            pl.when(j == 0)(turned)
             step("x1", u)
 
         def at_3():
@@ -873,6 +877,7 @@
         else:
             loop(0, T // TS, piece)
             load_act(j).wait()
+            start(loads(j)[:2])
         start(spills(j))
         stage, slot, m = reduce.stage, odd(j + base), D // 2
 
@@ -976,6 +981,9 @@
         load_h(i).wait()
         wait(work.at[at(slot * 2 * NB * T3, 2 * NB * T3), :], s3_sem.at[slot])
         pl.when(i > 1)(lambda: store_3(i - 2).wait())
+        if first:
+            pl.when(i > 2)(lambda: store_turned(i - 3).wait())
+            dx_t_buf[1 - slot] = dx_buf[1 - slot].T
         back = []
         for k, w in ((0, wg), (1, wu)):
             total = None
@@ -992,11 +1000,13 @@
         dx_buf[slot] = dh[rows, :] + (by_a * scale + by_square * wide).astype(bf16)
         store_3(i).start()
         if first:
-            pl.when(i > 1)(lambda: store_turned(i - 2).wait())
-            dx_t_buf[slot] = dx_buf[slot].T
-            store_turned(i).start()
+            pl.when(i > 0)(lambda: store_turned(i - 1).start())
 
     loop(0, n3, rows_back)
+    if first:
+        store_turned(n3 - 3).wait()
+        dx_t_buf[odd(n3 - 1)] = dx_buf[odd(n3 - 1)].T
+        store_turned(n3 - 1).start()
     assert n3 == 8
     for text in todo[n3:]:
         steps(text)

time: 334 us -> 328 us (0.982)
  Pallas kernels: 326 us -> 319 us
    pallas_call x2, Pallas kernels: 252 us -> 247 us  [backward(): call(functools.partial(backward_kernel, z, first), out, len(args), scratc...]
where the time goes in v7:
time: 328 us; the launch traced here: 327 us
  Pallas kernels  319 us (97%)
  local copies, waits for them, and re-layouts  7.34 us (2%)
    pallas_call x2, Pallas kernels, backward(): call(functools.partial(backward_kernel, z, first), out, len(args), scratc...  247 us
    pallas_call x1, Pallas kernels, forward(): call(functools.partial(forward_kernel, z), out, 5, scratch, 0)  72.6 us
    unnamed x10, local copies, waits for them, and re-layouts  7.34 us

profile of v7, /device:TPU:1, one launch (start us, length us, event | category | flops | bytes accessed | tf_op | source)
XLA Modules:
  0.0 327.4 jit_solution(12248865441796452656)
XLA Ops:
  0.6 72.6 %shard_map.84 = (bf16[2048,896]{1,0:T(8,128)(2,1)}, bf16[5,896,512]{2,1,0:T(8,128)(2,1)}, bf16[5,896,512]{2,1,0:T(8,128)(2,1)}, bf16[5,512,896]{2,1,0:T(8,128)(2...) custom-call(bf16[2048,896]{1,0:T(8,128)(2,1)} %bitcast.5, ...), custom_call_target="tpu_custom_call" | custom-call | tf_op jit(solution)/shard_map/pallas_call | solution.py:1056
  73.2 124.6 %shard_map.85 = (bf16[2048,896]{1,0:T(8,128)(2,1)}, bf16[2,112,2560]{2,1,0:T(8,128)(2,1)}, bf16[2,112,2560]{2,1,0:T(8,128)(2,1)}, bf16[2,320,896]{2,1,0:T(8,128)...) custom-call(bf16[2048,896]{1,0:T(8,128)(2,1)} %get-tuple-element.27., ...), custom_call_target="tpu_custom_call" | custom-call | tf_op jit(solution)/shard_map/pallas_call | solution.py:1079
  197.8 122.2 %shard_map.86 = (bf16[2048,896]{1,0:T(8,128)(2,1)}, bf16[2,112,2560]{2,1,0:T(8,128)(2,1)}, bf16[2,112,2560]{2,1,0:T(8,128)(2,1)}, bf16[2,320,896]{2,1,0:T(8,128)(2,1)}, bf16[2,5,2048,512]{3,2,1,0:T(8,128)(2,1)}) custom-call(bf16[2048,896]{1,0:T(8,128)(2,1)} %bitcast.6, ...), custom_call_target="tpu_custom_call", output_to_operand_aliasing={{1}: (12, {}), {2}: (13, {}), {3}: (14, {})} | custom-call | tf_op jit(solution)/shard_map/pallas_call | solution.py:1079
  320.0 0.0 copy-start
  320.0 0.0 copy-start.1
  320.0 4.3 %copy.19 = bf16[1,2048,896]{2,1,0:T(8,128)(2,1)} copy(bf16[1,2048,896]{2,1,0:T(8,128)(2,1)} %bitcast.7) | data formatting | bytes 7340032
  324.3 0.0 copy-done
  324.3 0.0 copy-start.2
  324.3 1.0 copy.20
  325.4 0.0 copy-done.1
  325.4 1.0 copy.21
  326.4 0.0 copy-done.2
  326.4 1.0 copy.22
Async XLA Ops:
  320.0 4.3 %copy-start = (bf16[2,112,2560]{2,1,0:T(8,128)(2,1)S(1)}, bf16[2,112,2560]{2,1,0:T(8,128)(2,1)}, u32[]{:S(2)}) copy-start(bf16[2,112,2560]{2,1,0:T(8,128)(2,1)} %get-tuple-element.55) | copy-start | bytes 3440644
  320.0 5.3 %copy-start.1 = (bf16[2,112,2560]{2,1,0:T(8,128)(2,1)S(1)}, bf16[2,112,2560]{2,1,0:T(8,128)(2,1)}, u32[]{:S(2)}) copy-start(bf16[2,112,2560]{2,1,0:T(8,128)(2,1)} %get-tuple-element.56) | copy-start | bytes 3440644
  324.3 2.0 copy-start.2
